TPU v7x, 256 devices: a whole 4x4x8 slice. The times are simulated.
256 devices in a mesh: gx: 8 (over z), gy: 4 (over y), gz: 8 (over x, core).
Axes of the slice: x: 4, y: 4, z: 8, core: 2. Of those that a mesh axis runs over, the one named last changes fastest.
Arguments:
- right_side: float32 [4, 192, 96, 192], P(None, 'gx', 'gy', 'gz'), may hold values from -6 to 6
- iterate: float32 [4, 192, 96, 192], P(None, 'gx', 'gy', 'gz'), may hold values from -6 to 6
- coefficient: float32 [192, 96, 192], P('gx', 'gy', 'gz'), may hold values from 0.1 to 2
- ordering: int32 [8, 4, 8, 216], P('gx', 'gy', 'gz'), may hold values from 0 to 215, as said below
- leaf_inverse: float32 [8, 4, 8, 125, 125], P('gx', 'gy', 'gz'), may hold values from -2 to 3
- leaf_first: float32 [8, 4, 8, 125, 50], P('gx', 'gy', 'gz'), may hold values from -0.5 to 0.5
- leaf_second: float32 [8, 4, 8, 125, 60], P('gx', 'gy', 'gz'), may hold values from -0.5 to 0.5
- leaf_top: float32 [8, 4, 8, 125, 72], P('gx', 'gy', 'gz'), may hold values from -0.5 to 0.5
- first_inverse: float32 [8, 4, 200, 200], P('gx', 'gy', 'gz'), may hold values from -2 to 3
- first_second: float32 [8, 4, 8, 25, 60], P('gx', 'gy', 'gz'), may hold values from -1.25 to 1.25
- first_top: float32 [8, 4, 8, 25, 72], P('gx', 'gy', 'gz'), may hold values from -1.25 to 1.25
- second_inverse: float32 [8, 960, 960], P('gx', ('gy', 'gz')), may hold values from -2 to 3
- second_top: float32 [8, 4, 8, 30, 72], P('gx', 'gy', 'gz'), may hold values from -1 to 1
- top_inverse: float32 [9216, 9216], P(('gx', 'gy', 'gz')), may hold values from -2 to 3
Outputs:
- correction: float32 [4, 192, 96, 192], P(None, 'gx', 'gy', 'gz')
Inputs may be any that keep to these rules, and one draw needn't show every extreme that they name: `ordering`: each device's row names each of its 216 coarse cells once (cell x 6^2 + y * 6 + z): first the 125 cells with x, y and z all below 5, then the 25 cells with z = 5 and x, y below it, then the 30 cells with y = 5 and x below it, then the 36 cells with x = 5, each group in any order.
All inputs are finite; a program needn't handle non-finite values.
Results may differ from a plain program's by a relative error of at most 0.0003.
Values sent between devices are 32-bit elements; how exact they have to be, the bound alone decides.
A program may use at most 64 MiB of HBM per device.

v0:
```python
import jax
import jax.numpy as jnp
from jax import lax
from jax.sharding import Mesh
from jax.sharding import PartitionSpec as P

GZ = ("gz_0", "gz_1")
GX_GY_GZ = ("gx", "gy", "gz_0", "gz_1")
GY_GZ = ("gy", "gz_0", "gz_1")


precise = lax.Precision.HIGHEST


def shifted(shard, axis, by):
    peers = lax.axis_size(axis)
    pairs = [(i, i + by) for i in range(peers) if 0 <= i + by < peers]
    return lax.ppermute(shard, axis, pairs)


def padded_2(shard, sides, width):
    edges = {}
    for axis, dim in sides:
        peers, length = (lax.axis_size(axis), shard.shape[dim])
        up = [(i, (i + 1) % peers) for i in range(peers - 1)]
        last = lax.slice_in_dim(shard, length - width, length, axis=dim)
        leading = lax.slice_in_dim(shard, 0, width, axis=dim)
        edges[dim] = (
            lax.ppermute(last, axis, up),
            lax.ppermute(leading, axis, [(b, a) for a, b in up]),
        )
    done = []
    for _, dim in sides:
        low, high = edges[dim]
        around = [(width, width) if d in done else (0, 0) for d in range(shard.ndim)]
        shard = jnp.concatenate([jnp.pad(low, around), shard, jnp.pad(high, around)], axis=dim)
        done.append(dim)
    return shard


def cut_along(shard, dim, peers):
    before, after = (shard.shape[:dim], shard.shape[dim + 1 :])
    return jnp.moveaxis(shard.reshape(*before, peers, -1, *after), dim, 0)


def summed_on_arrival(shard, axis, dim):
    peers = lax.axis_size(axis)
    pieces = lax.all_to_all(cut_along(shard, dim, peers), axis, 0, 0, tiled=True)
    return jnp.sum(pieces, axis=0)


def sum_by_axis(shard, axes, dim):
    far, near = axes
    own = summed_on_arrival(cut_along(shard, dim, lax.axis_size(far)), near, dim + 1)
    return jnp.sum(lax.all_to_all(own, far, 0, 0, tiled=True), axis=0)


def sent_to_all(shard, axis):
    copies = jnp.broadcast_to(shard, (lax.axis_size(axis), *shard.shape))
    return lax.all_to_all(copies, axis, split_axis=0, concat_axis=0, tiled=True)


def laid_out(pieces, dim):
    pieces = jnp.moveaxis(pieces, 0, dim)
    shape = pieces.shape
    return pieces.reshape(*shape[:dim], shape[dim] * shape[dim + 1], *shape[dim + 2 :])


def gathered_by_axis(shard, axes, dim):
    far, near = axes
    pieces = sent_to_all(sent_to_all(shard, far), near)
    return laid_out(pieces.swapaxes(0, 1).reshape(-1, *shard.shape), dim)


def gather_directly(shard, axis, dim):
    pieces = sent_to_all(shard, axis)
    return laid_out(pieces, dim)


def product(operand, matrix):
    return jnp.dot(operand, matrix, precision=precise, preferred_element_type=jnp.float32)


def product_back(operand, matrix):
    return lax.dot_general(
        operand,
        matrix,
        (((1,), (1,)), ((), ())),
        precision=precise,
        preferred_element_type=jnp.float32,
    )


def weigh(extended, dimension):
    length = extended.shape[dimension] - 1
    previous = lax.slice_in_dim(extended, 0, length, 2, dimension)
    centre = lax.slice_in_dim(extended, 1, length + 1, 2, dimension)
    following = lax.slice_in_dim(extended, 2, length + 1, 2, dimension)
    return 0.25 * previous + 0.5 * centre + 0.25 * following


def spread(extended, dimension):
    length = extended.shape[dimension] - 1
    current = lax.slice_in_dim(extended, 0, length, 1, dimension)
    following = lax.slice_in_dim(extended, 1, length + 1, 1, dimension)
    paired = jnp.stack([current, 0.5 * (current + following)], axis=dimension + 1)
    new_shape = list(current.shape)
    new_shape[dimension] = 2 * length
    return paired.reshape(new_shape)


def lower_rims(values):
    boundary = shifted(values[:, -1:], "gx", 1)
    values = jnp.concatenate([boundary, values], axis=1)
    boundary = shifted(values[:, :, -1:], "gy", 1)
    values = jnp.concatenate([boundary, values], axis=2)
    boundary = shifted(values[:, :, :, -1:], GZ, 1)
    return jnp.concatenate([boundary, values], axis=3)


def upper_rims(values):
    boundary = shifted(values[:, :1], "gx", -1)
    values = jnp.concatenate([values, boundary], axis=1)
    boundary = shifted(values[:, :, :1], "gy", -1)
    values = jnp.concatenate([values, boundary], axis=2)
    boundary = shifted(values[:, :, :, :1], GZ, -1)
    return jnp.concatenate([values, boundary], axis=3)


def restrict(values):
    extended = lower_rims(values)
    for dimension in (1, 2, 3):
        extended = weigh(extended, dimension)
    return extended


def prolong(values):
    extended = upper_rims(values)
    for dimension in (1, 2, 3):
        extended = spread(extended, dimension)
    return extended


def residual_of(right_side, iterate, coefficient):
    padded = padded_2(iterate, (("gx", 1), ("gy", 2), (GZ, 3)), 1)
    beside = padded[:, 2:, 1:-1, 1:-1] + padded[:, :-2, 1:-1, 1:-1]
    beside = beside + padded[:, 1:-1, 2:, 1:-1] + padded[:, 1:-1, :-2, 1:-1]
    beside = beside + padded[:, 1:-1, 1:-1, 2:] + padded[:, 1:-1, 1:-1, :-2]
    return right_side - ((6.0 + coefficient) * iterate - beside)


def per_device(
    right_side,
    iterate,
    coefficient,
    ordering,
    leaf_inverse,
    leaf_first,
    leaf_second,
    leaf_top,
    first_inverse,
    first_second,
    first_top,
    second_inverse,
    second_top,
    top_inverse,
):
    rhs_count = right_side.shape[0]
    leaf_size = leaf_inverse.shape[-1]
    first_size = first_second.shape[3]
    second_size = second_top.shape[3]
    top_size = top_inverse.shape[0]
    first_rows = first_inverse[0, 0]
    second_rows = second_inverse[0]
    coarse = restrict(restrict(residual_of(right_side, iterate, coefficient)))
    coarse_side = coarse.shape[1]
    flattened = coarse.reshape(rhs_count, coarse_side**3)
    order_row = ordering.reshape(-1)
    chosen = jnp.take(flattened, order_row, axis=1)
    first_end = leaf_size + first_size
    second_end = first_end + second_size
    leaf_rhs = chosen[:, :leaf_size]
    first_rhs = chosen[:, leaf_size:first_end]
    second_rhs = chosen[:, first_end:second_end]
    top_rhs = chosen[:, second_end:]
    leaf_block = leaf_inverse[0, 0, 0]
    to_first = leaf_first[0, 0, 0]
    to_second = leaf_second[0, 0, 0]
    to_top = leaf_top[0, 0, 0]
    first_to_second = first_second[0, 0, 0]
    first_to_top = first_top[0, 0, 0]
    second_to_top = second_top[0, 0, 0]
    leaf_solved = product(leaf_rhs, leaf_block)
    toward = product(leaf_solved, to_first)
    arrived = shifted(toward[:, first_size:], GZ, -1)
    first_target = first_rhs - toward[:, :first_size] - arrived
    first_own = summed_on_arrival(product(first_target, first_rows), GZ, 1)
    toward = product(leaf_solved, to_second) + product(first_own, first_to_second)
    arrived = shifted(toward[:, second_size:], "gy", -1)
    second_target = second_rhs - toward[:, :second_size] - arrived
    second_own = summed_on_arrival(product(second_target, second_rows), GY_GZ, 1)
    toward = (
        product(leaf_solved, to_top)
        + product(first_own, first_to_top)
        + product(second_own, second_to_top)
    )
    arrived = shifted(toward[:, top_size:], "gx", -1)
    top_target = top_rhs - toward[:, :top_size] - arrived
    top_own = sum_by_axis(product(top_target, top_inverse), (("gx", "gy"), ("gz_0", "gz_1")), 1)
    top_whole = gathered_by_axis(top_own, (("gx", "gy"), ("gz_0", "gz_1")), 1)
    top_back = product_back(top_whole, top_inverse)
    top_lower = shifted(top_back, "gx", 1)
    top_pair = jnp.concatenate([top_back, top_lower], axis=1)
    second_gap = second_own - product_back(top_pair, second_to_top)
    second_whole = gather_directly(second_gap, GY_GZ, 1)
    second_back = product_back(second_whole, second_rows)
    second_lower = shifted(second_back, "gy", 1)
    second_pair = jnp.concatenate([second_back, second_lower], axis=1)
    first_gap = (
        first_own
        - product_back(second_pair, first_to_second)
        - product_back(top_pair, first_to_top)
    )
    first_whole = gather_directly(first_gap, GZ, 1)
    first_back = product_back(first_whole, first_rows)
    first_lower = shifted(first_back, GZ, 1)
    first_pair = jnp.concatenate([first_back, first_lower], axis=1)
    leaf_gap = (
        leaf_solved - product_back(first_pair, to_first) - product_back(second_pair, to_second)
    )
    leaf_gap = leaf_gap - product_back(top_pair, to_top)
    leaf_back = product_back(leaf_gap, leaf_block)
    ordered = jnp.concatenate([leaf_back, first_back, second_back, top_back], axis=1)
    coarse_cells = jnp.zeros_like(ordered).at[:, order_row].set(ordered)
    coarse_grid = coarse_cells.reshape(rhs_count, coarse_side, coarse_side, coarse_side)
    return prolong(prolong(coarse_grid))


def solution(mesh):
    finer = Mesh(
        mesh.devices.reshape(mesh.shape["gx"], mesh.shape["gy"], 4, 2), ("gx", "gy", "gz_0", "gz_1")
    )
    return jax.shard_map(
        per_device,
        mesh=finer,
        in_specs=(
            P(None, "gx", "gy", GZ),
            P(None, "gx", "gy", GZ),
            P("gx", "gy", GZ),
            P("gx", "gy", GZ, None),
            P("gx", "gy", GZ, None, None),
            P("gx", "gy", GZ, None, None),
            P("gx", "gy", GZ, None, None),
            P("gx", "gy", GZ, None, None),
            P("gx", "gy", GZ, None),
            P("gx", "gy", GZ, None, None),
            P("gx", "gy", GZ, None, None),
            P("gx", GY_GZ, None),
            P("gx", "gy", GZ, None, None),
            P(GX_GY_GZ, None),
        ),
        out_specs=P(None, "gx", "gy", GZ),
        check_vma=False,
    )
```

profile of v0, /device:TPU:1, one launch (start us, length us, event | category | flops | bytes accessed | tf_op | source)
XLA Modules:
  0.0 278.1 jit_solution(7628728062553296326)
XLA Ops:
  0.0 1.6 fusion.84
  1.6 4.3 %collective-permute-start.1 = (f32[4,1,24,24]{3,2,1,0:T(8,128)}, f32[4,1,24,24]{3,2,1,0:T(8,128)S(1)}, u32[]{:S(2)}, u32[]{:S(2)}) collective-permute-start(f32[4,1,24,24]{3,2,1,0:T(8,128)} %get-tuple-element.10), channel_id=1, source_target_pairs={{0,32},{32,64},{64,96},{96,128},{128,160},{160,192},{192,224},{1,3... | collective-permute-start | bytes 27656 | tf_op jit(solution)/shard_map/ppermute | solution.py:29
  5.9 1.3 collective-permute-start
  7.2 3.5 %fusion.82 = (f32[4,24,24,1]{3,2,1,0:T(8,128)}, f32[4,24,24,1]{3,2,1,0:T(8,128)}) fusion(f32[4,24,24,24]{3,2,1,0:T(8,128)} %param.15), kind=kLoop, calls=%fused_computation.161 | loop fusion | bytes 36864 | tf_op jit(solution)/shard_map/slice | solution.py:27
  10.7 2.0 copy.258
  12.7 2.9 %collective-permute-start.4 = (f32[4,24,24,1]{2,1,3,0:T(8,128)S(1)}, f32[4,24,24,1]{2,1,3,0:T(8,128)S(1)}, u32[]{:S(2)}, u32[]{:S(2)}) collective-permute-start(f32[4,24,24,1]{2,1,3,0:T(8,128)S(1)} %copy.258), channel_id=1, source_target_pairs={{1,0},{2,1},{3,2},{4,3},{5,4},{6,5},{7,6},{9,8},{10,9},{11,10},{12... | collective-permute-start | bytes 27656 | tf_op jit(solution)/shard_map/ppermute | solution.py:30
  15.6 1.9 copy.259
  17.5 3.0 %collective-permute-start.5 = (f32[4,24,24,1]{2,1,3,0:T(8,128)S(1)}, f32[4,24,24,1]{2,1,3,0:T(8,128)S(1)}, u32[]{:S(2)}, u32[]{:S(2)}) collective-permute-start(f32[4,24,24,1]{2,1,3,0:T(8,128)S(1)} %copy.259), channel_id=1, source_target_pairs={{0,1},{1,2},{2,3},{3,4},{4,5},{5,6},{6,7},{8,9},{9,10},{10,11},{11... | collective-permute-start | bytes 27656 | tf_op jit(solution)/shard_map/ppermute | solution.py:29
  20.6 1.3 collective-permute-start.2
  21.9 4.0 %collective-permute-start.3 = (f32[4,24,1,24]{3,1,2,0:T(8,128)S(1)}, f32[4,24,1,24]{3,1,2,0:T(8,128)S(1)}, u32[]{:S(2)}, u32[]{:S(2)}) collective-permute-start(f32[4,24,1,24]{3,1,2,0:T(8,128)S(1)} %bitcast.159), channel_id=1, source_target_pairs={{0,8},{8,16},{16,24},{1,9},{9,17},{17,25},{2,10},{10,18},{18,26},{... | collective-permute-start | bytes 27656 | tf_op jit(solution)/shard_map/ppermute | solution.py:29
  27.8 1.7 copy.262
  29.5 1.6 copy.263
  31.7 5.2 %fusion.3 = f32[4,24,24,24]{3,2,1,0:T(8,128)S(1)} fusion(f32[4,24,24,24]{3,2,1,0:T(8,128)} %param.14, f32[4,24,24,1]{3,2,1,0:T(8,128)} %copy.263, f32[4,26,1,24]{3,2,1,0:T(1,128)S(1)} %pad.14.clone, f32[4,26,24,24]{3,2,1,0:T(8,128)} %constant_dynamic-update-slice_fusion, f32[4,26,1,24]{3,2,1,0:T(1,128)S(1)} %pad.15.clone, f32[4,24,24,1]{3,2,1,0:T(8,128)} %copy.262, ...), kind=kLoop, calls=%fused_computation.9 | loop fusion | flops 1327104 | bytes 1015296 | tf_op jit(solution)/shard_map/sub | solution.py:149
  37.0 4.3 %collective-permute-start.6 = (f32[4,1,24,24]{3,2,1,0:T(8,128)S(1)}, f32[4,1,24,24]{3,2,1,0:T(8,128)S(1)}, u32[]{:S(2)}, u32[]{:S(2)}) collective-permute-start(f32[4,1,24,24]{3,2,1,0:T(8,128)S(1)} %slice.264), channel_id=1, source_target_pairs={{0,32},{32,64},{64,96},{96,128},{128,160},{160,192},{192,224},{1,3... | collective-permute-start | bytes 27656 | tf_op jit(solution)/shard_map/ppermute | solution.py:18
  41.3 1.2 collective-permute-done.6
  42.6 3.7 %collective-permute-start.7 = (f32[4,25,1,24]{1,3,2,0:T(8,128)S(1)}, f32[4,25,1,24]{1,3,2,0:T(8,128)S(1)}, u32[]{:S(2)}, u32[]{:S(2)}) collective-permute-start(f32[4,25,1,24]{1,3,2,0:T(8,128)S(1)} %copy.207), channel_id=1, source_target_pairs={{0,8},{8,16},{16,24},{1,9},{9,17},{17,25},{2,10},{10,18},{18,26},{... | collective-permute-start | bytes 28808 | tf_op jit(solution)/shard_map/ppermute | solution.py:18
  46.3 1.2 collective-permute-done.7
  47.5 1.9 pad_maximum_fusion
  50.3 5.4 %collective-permute-start.8 = (f32[4,25,25,1]{2,1,3,0:T(8,128)S(1)}, f32[4,25,25,1]{2,1,3,0:T(8,128)S(1)}, u32[]{:S(2)}, u32[]{:S(2)}) collective-permute-start(f32[4,25,25,1]{2,1,3,0:T(8,128)S(1)} %copy.209), channel_id=1, source_target_pairs={{0,1},{1,2},{2,3},{3,4},{4,5},{5,6},{6,7},{8,9},{9,10},{10,11},{11... | collective-permute-start | bytes 30008 | tf_op jit(solution)/shard_map/ppermute | solution.py:18
  55.6 1.3 collective-permute-done.8
  57.0 2.0 copy.210
  58.9 2.0 maximum_maximum_fusion
  61.9 1.2 slice.219
  63.1 1.3 slice.220
  64.4 1.3 slice.221
  65.8 4.0 %collective-permute-start.9 = (f32[4,1,12,12]{3,2,1,0:T(8,128)S(1)}, f32[4,1,12,12]{3,2,1,0:T(8,128)S(1)}, u32[]{:S(2)}, u32[]{:S(2)}) collective-permute-start(f32[4,1,12,12]{3,2,1,0:T(8,128)S(1)} %slice.265), channel_id=1, source_target_pairs={{0,32},{32,64},{64,96},{96,128},{128,160},{160,192},{192,224},{1,3... | collective-permute-start | bytes 6920 | tf_op jit(solution)/shard_map/ppermute | solution.py:18
  70.9 4.0 %collective-permute-start.10 = (f32[4,13,1,12]{3,2,1,0:T(1,128)S(1)}, f32[4,13,1,12]{3,2,1,0:T(1,128)S(1)}, u32[]{:S(2)}, u32[]{:S(2)}) collective-permute-start(f32[4,13,1,12]{3,2,1,0:T(1,128)S(1)} %pad_maximum_fusion.25), channel_id=1, source_target_pairs={{0,8},{8,16},{16,24},{1,9},{9,17},{17,25},{2,10},{10,18},{18,26},{... | collective-permute-start | bytes 7496 | tf_op jit(solution)/shard_map/ppermute | solution.py:18
  76.0 6.0 %collective-permute-start.11 = (f32[4,13,13,1]{3,2,1,0:T(8,128)S(1)}, f32[4,13,13,1]{3,2,1,0:T(8,128)S(1)}, u32[]{:S(2)}, u32[]{:S(2)}) collective-permute-start(f32[4,13,13,1]{3,2,1,0:T(8,128)S(1)} %pad_maximum_fusion.13), channel_id=1, source_target_pairs={{0,1},{1,2},{2,3},{3,4},{4,5},{5,6},{6,7},{8,9},{9,10},{10,11},{11... | collective-permute-start | bytes 8120 | tf_op jit(solution)/shard_map/ppermute | solution.py:18
  82.0 5.0 %collective-permute-done.11 = f32[4,13,13,1]{3,2,1,0:T(8,128)S(1)} collective-permute-done((f32[4,13,13,1]{3,2,1,0:T(8,128)S(1)}, f32[4,13,13,1]{3,2,1,0:T(8,128)S(1)}, u32[]{:S(2)}, u32[]{:S(2)}) %collective-permute-start.11) | collective-permute-done | bytes 2736 | tf_op jit(solution)/shard_map/ppermute | solution.py:18
  90.8 1.9 collective-permute-start.12
  94.1 2.3 collective-permute-done.12
  97.3 3.7 %all-to-all-start = ((f32[8,4,25]{2,1,0:T(4,128)}), f32[8,4,25]{2,1,0:T(4,128)S(1)}, u32[]{:S(2)}, u32[]{:S(2)}) async-start(f32[8,4,25]{2,1,0:T(4,128)} %convolution_bitcast_fusion.1), calls=%async_computation | async-start | bytes 32768 | tf_op jit(solution)/shard_map/all_to_all | solution.py:48
  101.2 4.5 %all-to-all-done = f32[8,4,25]{2,1,0:T(4,128)S(1)} async-done(((f32[8,4,25]{2,1,0:T(4,128)}), f32[8,4,25]{2,1,0:T(4,128)S(1)}, u32[]{:S(2)}, u32[]{:S(2)}) %all-to-all-start) | async-done | bytes 3232 | tf_op jit(solution)/shard_map/all_to_all | solution.py:48
  105.9 1.3 collective-permute-start.13
  107.4 3.4 %collective-permute-done.13 = f32[4,30]{1,0:T(4,128)S(1)} collective-permute-done((f32[4,30]{1,0:T(4,128)S(1)}, f32[4,30]{1,0:T(4,128)S(1)}, u32[]{:S(2)}, u32[]{:S(2)}) %collective-permute-start.13) | collective-permute-done | bytes 512 | tf_op jit(solution)/shard_map/ppermute | solution.py:18
  110.8 2.0 convolution_bitcast_fusion
  113.6 7.2 %all-to-all-start.1 = ((f32[32,4,30]{2,1,0:T(4,128)}), f32[32,4,30]{2,1,0:T(4,128)S(1)}, u32[]{:S(2)}, u32[]{:S(2)}) async-start(f32[32,4,30]{2,1,0:T(4,128)} %copy.215), calls=%async_computation.1 | async-start | bytes 131072 | tf_op jit(solution)/shard_map/all_to_all | solution.py:48
  121.0 7.2 %all-to-all-done.1 = f32[32,4,30]{2,1,0:T(4,128)S(1)} async-done(((f32[32,4,30]{2,1,0:T(4,128)}), f32[32,4,30]{2,1,0:T(4,128)S(1)}, u32[]{:S(2)}, u32[]{:S(2)}) %all-to-all-start.1) | async-done | bytes 15392 | tf_op jit(solution)/shard_map/all_to_all | solution.py:48
  128.4 1.5 collective-permute-start.14
  129.9 3.7 %collective-permute-done.14 = f32[4,36]{1,0:T(4,128)S(1)} collective-permute-done((f32[4,36]{1,0:T(4,128)S(1)}, f32[4,36]{1,0:T(4,128)S(1)}, u32[]{:S(2)}, u32[]{:S(2)}) %collective-permute-start.14) | collective-permute-done | bytes 608 | tf_op jit(solution)/shard_map/ppermute | solution.py:18
  135.6 9.0 %all_to_all.40 = f32[8,1,4608]{2,1,0:T(1,128)S(1)} all-to-all(f32[8,1,4608]{2,1,0:T(1,128)S(1)} %reshape.122), channel_id=1, replica_groups=mesh['gx'=8,'gy'=4,'gz_0'=4,'gz_1'=2] {'gz_0','gz_1'}, dimensions={0} | all-to-all | bytes 294912 | tf_op jit(solution)/shard_map/all_to_all | solution.py:48
  147.0 21.2 %all_to_all.41 = f32[32,1,144]{2,1,0:T(1,128)S(1)} all-to-all(f32[32,1,144]{2,1,0:T(1,128)S(1)} %reshape.124), channel_id=1, replica_groups=mesh['gx'=8,'gy'=4,'gz_0'=4,'gz_1'=2] {'gx','gy'}, dimensions={0} | all-to-all | bytes 36864 | tf_op jit(solution)/shard_map/all_to_all | solution.py:55
  169.2 11.6 %all_to_all.42 = f32[32,1,144]{2,1,0:T(1,128)S(1)} all-to-all(f32[32,1,144]{2,1,0:T(1,128)S(1)} %reshape.126), channel_id=1, replica_groups=mesh['gx'=8,'gy'=4,'gz_0'=4,'gz_1'=2] {'gx','gy'}, dimensions={0} | all-to-all | bytes 36864 | tf_op jit(solution)/shard_map/all_to_all | solution.py:60
  182.3 11.2 %all_to_all.43 = f32[8,1,4608]{2,1,0:T(1,128)S(1)} all-to-all(f32[8,1,4608]{2,1,0:T(1,128)S(1)} %reshape.128), channel_id=1, replica_groups=mesh['gx'=8,'gy'=4,'gz_0'=4,'gz_1'=2] {'gz_0','gz_1'}, dimensions={0} | all-to-all | bytes 294912 | tf_op jit(solution)/shard_map/all_to_all | solution.py:60
  195.9 1.2 fusion.85
  197.2 2.3 collective-permute-start.15
  200.4 12.1 %all_to_all.44 = f32[32,4,30]{2,1,0:T(4,128)S(1)} all-to-all(f32[32,4,30]{2,1,0:T(4,128)S(1)} %broadcast_in_dim.32), channel_id=1, replica_groups=mesh['gx'=8,'gy'=4,'gz_0'=4,'gz_1'=2] {'gy','gz_0','gz_1'}, dimensions={0} | all-to-all | bytes 30720 | tf_op jit(solution)/shard_map/all_to_all | solution.py:60
  212.9 2.3 collective-permute-start.16
  216.1 8.3 %all_to_all.45 = f32[8,4,25]{2,1,0:T(4,128)S(1)} all-to-all(f32[8,4,25]{2,1,0:T(4,128)S(1)} %broadcast_in_dim.33), channel_id=1, replica_groups=mesh['gx'=8,'gy'=4,'gz_0'=4,'gz_1'=2] {'gz_0','gz_1'}, dimensions={0} | all-to-all | bytes 6400 | tf_op jit(solution)/shard_map/all_to_all | solution.py:60
  224.5 2.8 %collective-permute-start.17 = (f32[4,25]{1,0:T(4,128)S(1)}, f32[4,25]{1,0:T(4,128)S(1)}, u32[]{:S(2)}, u32[]{:S(2)}) collective-permute-start(f32[4,25]{1,0:T(4,128)S(1)} %fusion.39), channel_id=1, source_target_pairs={{0,1},{1,2},{2,3},{3,4},{4,5},{5,6},{6,7},{8,9},{9,10},{10,11},{11... | collective-permute-start | bytes 1208 | tf_op jit(solution)/shard_map/ppermute | solution.py:18
  230.2 1.3 collective-permute-start.18
  231.5 4.0 %collective-permute-done.18 = f32[4,1,6,6]{3,2,1,0:T(8,128)S(1)} collective-permute-done((f32[4,1,6,6]{3,2,1,0:T(8,128)S(1)}, f32[4,1,6,6]{3,2,1,0:T(8,128)S(1)}, u32[]{:S(2)}, u32[]{:S(2)}) %collective-permute-start.18) | collective-permute-done | bytes 608 | tf_op jit(solution)/shard_map/ppermute | solution.py:18
  235.5 1.3 collective-permute-start.19
  236.8 3.7 %collective-permute-done.19 = f32[4,7,1,6]{3,2,1,0:T(1,128)S(1)} collective-permute-done((f32[4,7,1,6]{3,2,1,0:T(1,128)S(1)}, f32[4,7,1,6]{3,2,1,0:T(1,128)S(1)}, u32[]{:S(2)}, u32[]{:S(2)}) %collective-permute-start.19) | collective-permute-done | bytes 704 | tf_op jit(solution)/shard_map/ppermute | solution.py:18
  240.6 3.2 %collective-permute-start.20 = (f32[4,7,7,1]{3,2,1,0:T(8,128)S(1)}, f32[4,7,7,1]{3,2,1,0:T(8,128)S(1)}, u32[]{:S(2)}, u32[]{:S(2)}) collective-permute-start(f32[4,7,7,1]{3,2,1,0:T(8,128)S(1)} %pad_maximum_fusion.20), channel_id=1, source_target_pairs={{1,0},{2,1},{3,2},{4,3},{5,4},{6,5},{7,6},{9,8},{10,9},{11,10},{12... | collective-permute-start | bytes 2360 | tf_op jit(solution)/shard_map/ppermute | solution.py:18
  243.7 5.0 %collective-permute-done.20 = f32[4,7,7,1]{3,2,1,0:T(8,128)S(1)} collective-permute-done((f32[4,7,7,1]{3,2,1,0:T(8,128)S(1)}, f32[4,7,7,1]{3,2,1,0:T(8,128)S(1)}, u32[]{:S(2)}, u32[]{:S(2)}) %collective-permute-start.20) | collective-permute-done | bytes 816 | tf_op jit(solution)/shard_map/ppermute | solution.py:18
  250.1 1.3 collective-permute-start.21
  251.4 3.6 %collective-permute-done.21 = f32[4,1,12,12]{2,0,3,1:T(4,128)S(1)} collective-permute-done((f32[4,1,12,12]{2,0,3,1:T(4,128)S(1)}, f32[4,1,12,12]{2,0,3,1:T(4,128)S(1)}, u32[]{:S(2)}, u32[]{:S(2)}) %collective-permute-start.21) | collective-permute-done | bytes 2336 | tf_op jit(solution)/shard_map/ppermute | solution.py:18
  255.0 1.3 collective-permute-start.22
  256.3 7.5 %collective-permute-done.22 = f32[4,13,1,12]{2,0,3,1:T(4,128)S(1)} collective-permute-done((f32[4,13,1,12]{2,0,3,1:T(4,128)S(1)}, f32[4,13,1,12]{2,0,3,1:T(4,128)S(1)}, u32[]{:S(2)}, u32[]{:S(2)}) %collective-permute-start.22) | collective-permute-done | bytes 2528 | tf_op jit(solution)/shard_map/ppermute | solution.py:18
  263.9 1.9 collective-permute-start.23
  265.9 5.4 %collective-permute-done.23 = f32[4,13,13,1]{2,0,3,1:T(4,128)S(1)} collective-permute-done((f32[4,13,13,1]{2,0,3,1:T(4,128)S(1)}, f32[4,13,13,1]{2,0,3,1:T(4,128)S(1)}, u32[]{:S(2)}, u32[]{:S(2)}) %collective-permute-start.23) | collective-permute-done | bytes 2736 | tf_op jit(solution)/shard_map/ppermute | solution.py:18
  274.0 1.4 copy.240
  275.4 2.7 copy.241
  (172 shorter events, 32.7 us)
Async XLA Ops:
  0.0 133.6 %copy-start = (f32[36,9216]{1,0:T(8,128)S(1)}, f32[36,9216]{1,0:T(8,128)}, u32[]{:S(2)}) copy-start(f32[36,9216]{1,0:T(8,128)} %param.27) | copy-start | bytes 3981316
  1.6 20.4 %collective-permute-start.1 = (f32[4,1,24,24]{3,2,1,0:T(8,128)}, f32[4,1,24,24]{3,2,1,0:T(8,128)S(1)}, u32[]{:S(2)}, u32[]{:S(2)}) collective-permute-start(f32[4,1,24,24]{3,2,1,0:T(8,128)} %get-tuple-element.10), channel_id=1, source_target_pairs={{0,32},{32,64},{64,96},{96,128},{128,160},{160,192},{192,224},{1,3... | collective-permute-start | bytes 27656 | tf_op jit(solution)/shard_map/ppermute | solution.py:29
  5.9 25.2 %collective-permute-start = (f32[4,1,24,24]{3,2,1,0:T(8,128)}, f32[4,1,24,24]{3,2,1,0:T(8,128)S(1)}, u32[]{:S(2)}, u32[]{:S(2)}) collective-permute-start(f32[4,1,24,24]{3,2,1,0:T(8,128)} %get-tuple-element.9), channel_id=1, source_target_pairs={{32,0},{64,32},{96,64},{128,96},{160,128},{192,160},{224,192},{33,... | collective-permute-start | bytes 27656 | tf_op jit(solution)/shard_map/ppermute | solution.py:30
  10.7 9.8 %copy-start.1 = (f32[4,24,24,24]{3,2,1,0:T(8,128)S(1)}, f32[4,24,24,24]{3,2,1,0:T(8,128)}, u32[]{:S(2)}) copy-start(f32[4,24,24,24]{3,2,1,0:T(8,128)} %param.15) | copy-start | bytes 663556
  10.7 11.2 %copy-start.5 = (f32[24,24,24]{2,1,0:T(8,128)S(1)}, f32[24,24,24]{2,1,0:T(8,128)}, u32[]{:S(2)}) copy-start(f32[24,24,24]{2,1,0:T(8,128)} %param.16) | copy-start | bytes 165892
  12.7 15.1 %collective-permute-start.4 = (f32[4,24,24,1]{2,1,3,0:T(8,128)S(1)}, f32[4,24,24,1]{2,1,3,0:T(8,128)S(1)}, u32[]{:S(2)}, u32[]{:S(2)}) collective-permute-start(f32[4,24,24,1]{2,1,3,0:T(8,128)S(1)} %copy.258), channel_id=1, source_target_pairs={{1,0},{2,1},{3,2},{4,3},{5,4},{6,5},{7,6},{9,8},{10,9},{11,10},{12... | collective-permute-start | bytes 27656 | tf_op jit(solution)/shard_map/ppermute | solution.py:30
  17.5 12.0 %collective-permute-start.5 = (f32[4,24,24,1]{2,1,3,0:T(8,128)S(1)}, f32[4,24,24,1]{2,1,3,0:T(8,128)S(1)}, u32[]{:S(2)}, u32[]{:S(2)}) collective-permute-start(f32[4,24,24,1]{2,1,3,0:T(8,128)S(1)} %copy.259), channel_id=1, source_target_pairs={{0,1},{1,2},{2,3},{3,4},{4,5},{5,6},{6,7},{8,9},{9,10},{10,11},{11... | collective-permute-start | bytes 27656 | tf_op jit(solution)/shard_map/ppermute | solution.py:29
  20.6 7.1 %collective-permute-start.2 = (f32[4,24,1,24]{3,1,2,0:T(8,128)S(1)}, f32[4,24,1,24]{3,1,2,0:T(8,128)S(1)}, u32[]{:S(2)}, u32[]{:S(2)}) collective-permute-start(f32[4,24,1,24]{3,1,2,0:T(8,128)S(1)} %bitcast.160), channel_id=1, source_target_pairs={{8,0},{16,8},{24,16},{9,1},{17,9},{25,17},{10,2},{18,10},{26,18},{... | collective-permute-start | bytes 27656 | tf_op jit(solution)/shard_map/ppermute | solution.py:30
  21.9 5.8 %collective-permute-start.3 = (f32[4,24,1,24]{3,1,2,0:T(8,128)S(1)}, f32[4,24,1,24]{3,1,2,0:T(8,128)S(1)}, u32[]{:S(2)}, u32[]{:S(2)}) collective-permute-start(f32[4,24,1,24]{3,1,2,0:T(8,128)S(1)} %bitcast.159), channel_id=1, source_target_pairs={{0,8},{8,16},{16,24},{1,9},{9,17},{17,25},{2,10},{10,18},{18,26},{... | collective-permute-start | bytes 27656 | tf_op jit(solution)/shard_map/ppermute | solution.py:29
  37.0 5.5 %copy-start.2 = (f32[4,24,24,24]{3,2,1,0:T(8,128)}, f32[4,24,24,24]{3,2,1,0:T(8,128)S(1)}, u32[]{:S(2)}) copy-start(f32[4,24,24,24]{3,2,1,0:T(8,128)S(1)} %fusion.3) | copy-start | bytes 663556
  37.0 5.4 %collective-permute-start.6 = (f32[4,1,24,24]{3,2,1,0:T(8,128)S(1)}, f32[4,1,24,24]{3,2,1,0:T(8,128)S(1)}, u32[]{:S(2)}, u32[]{:S(2)}) collective-permute-start(f32[4,1,24,24]{3,2,1,0:T(8,128)S(1)} %slice.264), channel_id=1, source_target_pairs={{0,32},{32,64},{64,96},{96,128},{128,160},{160,192},{192,224},{1,3... | collective-permute-start | bytes 27656 | tf_op jit(solution)/shard_map/ppermute | solution.py:18
  42.6 4.9 %collective-permute-start.7 = (f32[4,25,1,24]{1,3,2,0:T(8,128)S(1)}, f32[4,25,1,24]{1,3,2,0:T(8,128)S(1)}, u32[]{:S(2)}, u32[]{:S(2)}) collective-permute-start(f32[4,25,1,24]{1,3,2,0:T(8,128)S(1)} %copy.207), channel_id=1, source_target_pairs={{0,8},{8,16},{16,24},{1,9},{9,17},{17,25},{2,10},{10,18},{18,26},{... | collective-permute-start | bytes 28808 | tf_op jit(solution)/shard_map/ppermute | solution.py:18
  50.3 8.7 %copy-start.3 = (f32[4,24,24,24]{3,2,1,0:T(8,128)S(1)}, f32[4,24,24,24]{3,2,1,0:T(8,128)}, u32[]{:S(2)}) copy-start(f32[4,24,24,24]{3,2,1,0:T(8,128)} %copy-done.2) | copy-start | bytes 663556
  50.3 6.7 %collective-permute-start.8 = (f32[4,25,25,1]{2,1,3,0:T(8,128)S(1)}, f32[4,25,25,1]{2,1,3,0:T(8,128)S(1)}, u32[]{:S(2)}, u32[]{:S(2)}) collective-permute-start(f32[4,25,25,1]{2,1,3,0:T(8,128)S(1)} %copy.209), channel_id=1, source_target_pairs={{0,1},{1,2},{2,3},{3,4},{4,5},{5,6},{6,7},{8,9},{9,10},{10,11},{11... | collective-permute-start | bytes 30008 | tf_op jit(solution)/shard_map/ppermute | solution.py:18
  64.4 5.4 %copy-start.14 = (s32[1,1,1,216]{3,2,1,0:T(1,128)S(1)}, s32[1,1,1,216]{3,2,1,0:T(1,128)}, u32[]{:S(2)}) copy-start(s32[1,1,1,216]{3,2,1,0:T(1,128)} %param.17) | copy-start | bytes 2596
  65.8 5.0 %collective-permute-start.9 = (f32[4,1,12,12]{3,2,1,0:T(8,128)S(1)}, f32[4,1,12,12]{3,2,1,0:T(8,128)S(1)}, u32[]{:S(2)}, u32[]{:S(2)}) collective-permute-start(f32[4,1,12,12]{3,2,1,0:T(8,128)S(1)} %slice.265), channel_id=1, source_target_pairs={{0,32},{32,64},{64,96},{96,128},{128,160},{160,192},{192,224},{1,3... | collective-permute-start | bytes 6920 | tf_op jit(solution)/shard_map/ppermute | solution.py:18
  70.9 4.9 %collective-permute-start.10 = (f32[4,13,1,12]{3,2,1,0:T(1,128)S(1)}, f32[4,13,1,12]{3,2,1,0:T(1,128)S(1)}, u32[]{:S(2)}, u32[]{:S(2)}) collective-permute-start(f32[4,13,1,12]{3,2,1,0:T(1,128)S(1)} %pad_maximum_fusion.25), channel_id=1, source_target_pairs={{0,8},{8,16},{16,24},{1,9},{9,17},{17,25},{2,10},{10,18},{18,26},{... | collective-permute-start | bytes 7496 | tf_op jit(solution)/shard_map/ppermute | solution.py:18
  76.0 11.0 %collective-permute-start.11 = (f32[4,13,13,1]{3,2,1,0:T(8,128)S(1)}, f32[4,13,13,1]{3,2,1,0:T(8,128)S(1)}, u32[]{:S(2)}, u32[]{:S(2)}) collective-permute-start(f32[4,13,13,1]{3,2,1,0:T(8,128)S(1)} %pad_maximum_fusion.13), channel_id=1, source_target_pairs={{0,1},{1,2},{2,3},{3,4},{4,5},{5,6},{6,7},{8,9},{9,10},{10,11},{11... | collective-permute-start | bytes 8120 | tf_op jit(solution)/shard_map/ppermute | solution.py:18
  87.3 3.1 %copy-start.6 = (f32[1,1,1,125,125]{4,2,3,1,0:T(1,128)S(1)}, f32[1,1,1,125,125]{4,2,3,1,0:T(1,128)}, u32[]{:S(2)}) copy-start(f32[1,1,1,125,125]{4,2,3,1,0:T(1,128)} %param.18) | copy-start | bytes 187504
  87.3 3.2 %copy-start.10 = (f32[1,1,1,125,50]{3,2,4,1,0:T(1,128)S(1)}, f32[1,1,1,125,50]{3,2,4,1,0:T(1,128)}, u32[]{:S(2)}) copy-start(f32[1,1,1,125,50]{3,2,4,1,0:T(1,128)} %param.19) | copy-start | bytes 75004
  87.3 5.4 %copy-start.9 = (f32[1,1,25,200]{3,1,2,0:T(1,128)S(1)}, f32[1,1,25,200]{3,1,2,0:T(1,128)}, u32[]{:S(2)}) copy-start(f32[1,1,25,200]{3,1,2,0:T(1,128)} %param.22) | copy-start | bytes 60004
  87.5 5.4 %copy-start.4 = (f32[1,30,960]{2,0,1:T(1,128)S(1)}, f32[1,30,960]{2,0,1:T(1,128)}, u32[]{:S(2)}) copy-start(f32[1,30,960]{2,0,1:T(1,128)} %param.25) | copy-start | bytes 345604
  90.4 10.7 %copy-start.8 = (f32[1,1,1,125,60]{3,2,4,1,0:T(1,128)S(1)}, f32[1,1,1,125,60]{3,2,4,1,0:T(1,128)}, u32[]{:S(2)}) copy-start(f32[1,1,1,125,60]{3,2,4,1,0:T(1,128)} %param.20) | copy-start | bytes 90004
  90.5 15.2 %copy-start.12 = (f32[1,1,1,25,60]{4,2,3,1,0:T(1,128)S(1)}, f32[1,1,1,25,60]{4,2,3,1,0:T(1,128)}, u32[]{:S(2)}) copy-start(f32[1,1,1,25,60]{4,2,3,1,0:T(1,128)} %param.23) | copy-start | bytes 18004
  90.5 16.7 %copy-start.7 = (f32[1,1,1,125,72]{3,4,2,1,0:T(8,128)S(1)}, f32[1,1,1,125,72]{3,4,2,1,0:T(8,128)}, u32[]{:S(2)}) copy-start(f32[1,1,1,125,72]{3,4,2,1,0:T(8,128)} %param.21) | copy-start | bytes 108004
  90.8 5.7 %collective-permute-start.12 = (f32[4,25]{1,0:T(4,128)S(1)}, f32[4,25]{1,0:T(4,128)S(1)}, u32[]{:S(2)}, u32[]{:S(2)}) collective-permute-start(f32[4,25]{1,0:T(4,128)S(1)} %slice.237), channel_id=1, source_target_pairs={{1,0},{2,1},{3,2},{4,3},{5,4},{6,5},{7,6},{9,8},{10,9},{11,10},{12... | collective-permute-start | bytes 1208 | tf_op jit(solution)/shard_map/ppermute | solution.py:18
  93.5 27.4 %copy-start.11 = (f32[1,1,1,25,72]{4,2,3,1,0:T(1,128)S(1)}, f32[1,1,1,25,72]{4,2,3,1,0:T(1,128)}, u32[]{:S(2)}) copy-start(f32[1,1,1,25,72]{4,2,3,1,0:T(1,128)} %param.24) | copy-start | bytes 21604
  93.5 34.7 %copy-start.13 = (f32[1,1,1,30,72]{4,2,3,1,0:T(1,128)S(1)}, f32[1,1,1,30,72]{4,2,3,1,0:T(1,128)}, u32[]{:S(2)}) copy-start(f32[1,1,1,30,72]{4,2,3,1,0:T(1,128)} %param.26) | copy-start | bytes 25924
  97.3 8.4 %all-to-all-start = ((f32[8,4,25]{2,1,0:T(4,128)}), f32[8,4,25]{2,1,0:T(4,128)S(1)}, u32[]{:S(2)}, u32[]{:S(2)}) async-start(f32[8,4,25]{2,1,0:T(4,128)} %convolution_bitcast_fusion.1), calls=%async_computation | async-start | bytes 32768 | tf_op jit(solution)/shard_map/all_to_all | solution.py:48
  105.9 4.9 %collective-permute-start.13 = (f32[4,30]{1,0:T(4,128)S(1)}, f32[4,30]{1,0:T(4,128)S(1)}, u32[]{:S(2)}, u32[]{:S(2)}) collective-permute-start(f32[4,30]{1,0:T(4,128)S(1)} %slice.240), channel_id=1, source_target_pairs={{8,0},{16,8},{24,16},{9,1},{17,9},{25,17},{10,2},{18,10},{26,18},{... | collective-permute-start | bytes 1448 | tf_op jit(solution)/shard_map/ppermute | solution.py:18
  113.6 14.6 %all-to-all-start.1 = ((f32[32,4,30]{2,1,0:T(4,128)}), f32[32,4,30]{2,1,0:T(4,128)S(1)}, u32[]{:S(2)}, u32[]{:S(2)}) async-start(f32[32,4,30]{2,1,0:T(4,128)} %copy.215), calls=%async_computation.1 | async-start | bytes 131072 | tf_op jit(solution)/shard_map/all_to_all | solution.py:48
  128.4 5.2 %collective-permute-start.14 = (f32[4,36]{1,0:T(4,128)S(1)}, f32[4,36]{1,0:T(4,128)S(1)}, u32[]{:S(2)}, u32[]{:S(2)}) collective-permute-start(f32[4,36]{1,0:T(4,128)S(1)} %slice.243), channel_id=1, source_target_pairs={{32,0},{64,32},{96,64},{128,96},{160,128},{192,160},{224,192},{33,... | collective-permute-start | bytes 1736 | tf_op jit(solution)/shard_map/ppermute | solution.py:18
  197.2 3.0 %collective-permute-start.15 = (f32[4,36]{1,0:T(4,128)S(1)}, f32[4,36]{1,0:T(4,128)S(1)}, u32[]{:S(2)}, u32[]{:S(2)}) collective-permute-start(f32[4,36]{1,0:T(4,128)S(1)} %fusion.85), channel_id=1, source_target_pairs={{0,32},{32,64},{64,96},{96,128},{128,160},{160,192},{192,224},{1,3... | collective-permute-start | bytes 1736 | tf_op jit(solution)/shard_map/ppermute | solution.py:18
  212.9 3.0 %collective-permute-start.16 = (f32[4,30]{1,0:T(4,128)S(1)}, f32[4,30]{1,0:T(4,128)S(1)}, u32[]{:S(2)}, u32[]{:S(2)}) collective-permute-start(f32[4,30]{1,0:T(4,128)S(1)} %fusion.21), channel_id=1, source_target_pairs={{0,8},{8,16},{16,24},{1,9},{9,17},{17,25},{2,10},{10,18},{18,26},{... | collective-permute-start | bytes 1448 | tf_op jit(solution)/shard_map/ppermute | solution.py:18
  224.5 3.5 %collective-permute-start.17 = (f32[4,25]{1,0:T(4,128)S(1)}, f32[4,25]{1,0:T(4,128)S(1)}, u32[]{:S(2)}, u32[]{:S(2)}) collective-permute-start(f32[4,25]{1,0:T(4,128)S(1)} %fusion.39), channel_id=1, source_target_pairs={{0,1},{1,2},{2,3},{3,4},{4,5},{5,6},{6,7},{8,9},{9,10},{10,11},{11... | collective-permute-start | bytes 1208 | tf_op jit(solution)/shard_map/ppermute | solution.py:18
  230.2 5.3 %collective-permute-start.18 = (f32[4,1,6,6]{3,2,1,0:T(8,128)S(1)}, f32[4,1,6,6]{3,2,1,0:T(8,128)S(1)}, u32[]{:S(2)}, u32[]{:S(2)}) collective-permute-start(f32[4,1,6,6]{3,2,1,0:T(8,128)S(1)} %slice.270), channel_id=1, source_target_pairs={{32,0},{64,32},{96,64},{128,96},{160,128},{192,160},{224,192},{33,... | collective-permute-start | bytes 1736 | tf_op jit(solution)/shard_map/ppermute | solution.py:18
  235.5 5.0 %collective-permute-start.19 = (f32[4,7,1,6]{3,2,1,0:T(1,128)S(1)}, f32[4,7,1,6]{3,2,1,0:T(1,128)S(1)}, u32[]{:S(2)}, u32[]{:S(2)}) collective-permute-start(f32[4,7,1,6]{3,2,1,0:T(1,128)S(1)} %slice.271), channel_id=1, source_target_pairs={{8,0},{16,8},{24,16},{9,1},{17,9},{25,17},{10,2},{18,10},{26,18},{... | collective-permute-start | bytes 2024 | tf_op jit(solution)/shard_map/ppermute | solution.py:18
  240.6 8.1 %collective-permute-start.20 = (f32[4,7,7,1]{3,2,1,0:T(8,128)S(1)}, f32[4,7,7,1]{3,2,1,0:T(8,128)S(1)}, u32[]{:S(2)}, u32[]{:S(2)}) collective-permute-start(f32[4,7,7,1]{3,2,1,0:T(8,128)S(1)} %pad_maximum_fusion.20), channel_id=1, source_target_pairs={{1,0},{2,1},{3,2},{4,3},{5,4},{6,5},{7,6},{9,8},{10,9},{11,10},{12... | collective-permute-start | bytes 2360 | tf_op jit(solution)/shard_map/ppermute | solution.py:18
  250.1 4.9 %collective-permute-start.21 = (f32[4,1,12,12]{2,0,3,1:T(4,128)S(1)}, f32[4,1,12,12]{2,0,3,1:T(4,128)S(1)}, u32[]{:S(2)}, u32[]{:S(2)}) collective-permute-start(f32[4,1,12,12]{2,0,3,1:T(4,128)S(1)} %slice.278), channel_id=1, source_target_pairs={{32,0},{64,32},{96,64},{128,96},{160,128},{192,160},{224,192},{33,... | collective-permute-start | bytes 6920 | tf_op jit(solution)/shard_map/ppermute | solution.py:18
  255.0 8.8 %collective-permute-start.22 = (f32[4,13,1,12]{2,0,3,1:T(4,128)S(1)}, f32[4,13,1,12]{2,0,3,1:T(4,128)S(1)}, u32[]{:S(2)}, u32[]{:S(2)}) collective-permute-start(f32[4,13,1,12]{2,0,3,1:T(4,128)S(1)} %pad_maximum_fusion.16), channel_id=1, source_target_pairs={{8,0},{16,8},{24,16},{9,1},{17,9},{25,17},{10,2},{18,10},{26,18},{... | collective-permute-start | bytes 7496 | tf_op jit(solution)/shard_map/ppermute | solution.py:18
  263.9 7.3 %collective-permute-start.23 = (f32[4,13,13,1]{2,0,3,1:T(4,128)S(1)}, f32[4,13,13,1]{2,0,3,1:T(4,128)S(1)}, u32[]{:S(2)}, u32[]{:S(2)}) collective-permute-start(f32[4,13,13,1]{2,0,3,1:T(4,128)S(1)} %pad_maximum_fusion.23), channel_id=1, source_target_pairs={{1,0},{2,1},{3,2},{4,3},{5,4},{6,5},{7,6},{9,8},{10,9},{11,10},{12... | collective-permute-start | bytes 8120 | tf_op jit(solution)/shard_map/ppermute | solution.py:18
where the time goes:
time: 279 us; the launch traced here: 278 us
  starting transfers between devices  77.4 us (28%)
  blocking collectives  73.5 us (26%)
  waiting for transfers between devices  62.6 us (22%)
  local copies, waits for them, and re-layouts  40.7 us (15%)
  other arithmetic  15.3 us (5%)
  matrix products  7.63 us (3%)
    ppermute x18, waiting for transfers between devices, shifted(): return lax.ppermute(shard, axis, pairs)  50.9 us
    ppermute x18, starting transfers between devices, shifted(): return lax.ppermute(shard, axis, pairs)  49.6 us
    all_to_all x4, blocking collectives, sent_to_all(): return lax.all_to_all(copies, axis, split_axis=0, concat_axis=0, tiled=True)  43.2 us
    all_to_all x1, blocking collectives, sum_by_axis(): return jnp.sum(lax.all_to_all(own, far, 0, 0, tiled=True), axis=0)  21.2 us
    unnamed x48, local copies, waits for them, and re-layouts  11.9 us
    all_to_all x2, waiting for transfers between devices, summed_on_arrival(): lax.all_to_all(cut_along(shard, dim, peers), axis, 0, 0, tiled=True)  11.7 us
    ppermute x3, starting transfers between devices, padded_2(): lax.ppermute(last, axis, up)  11.4 us
    all_to_all x2, starting transfers between devices, summed_on_arrival(): lax.all_to_all(cut_along(shard, dim, peers), axis, 0, 0, tiled=True)  11 us
  transfers between devices with their start and end apart: 26, of which 20 were waited for; matrix products, arithmetic and copies ran while one was open for 5% of the time, Pallas kernels for 0%

commit v1 on v0

v1 whole, which is shorter than its diff:
```python
import functools

import jax
import jax.numpy as jnp
from jax import lax
from jax.experimental import pallas as pl
from jax.experimental.pallas import tpu as pltpu
from jax.sharding import PartitionSpec as P

MESH = pl.DeviceIdType.MESH
F32 = jnp.float32
BF16 = jnp.bfloat16
AXES = ("gx", "gy", "gz")

FLAT = ((1, 0), (-1, 0), (0, 1), (0, -1), (1, 1), (1, -1), (-1, 1))
ABOVE = ((0, 0),) + FLAT
BELOW = ((0, 0), (1, 0), (0, 1), (1, 1))
HALO = [(x, y, 0) for x, y in FLAT] + [(x, y, 1) for x, y in ABOVE] + [(x, y, -1) for x, y in BELOW]
RIM = [(1, 0, 0), (0, 1, 0), (1, 1, 0), (0, 0, 1), (1, 0, 1), (0, 1, 1), (1, 1, 1)]


def split(value):
    high = value.astype(BF16)
    return high, (value - high.astype(F32)).astype(BF16)


def dot(left, right, dims=((1,), (0,))):
    return lax.dot_general(left, right, (dims, ((), ())), preferred_element_type=F32)


def times(value, factor, dims=((1,), (0,))):
    high, low = split(value)
    f_high, f_low = factor
    return dot(high, f_high, dims) + dot(low, f_high, dims) + dot(high, f_low, dims)


BACK = ((1,), (1,))


def iota(shape, dim):
    return lax.broadcasted_iota(jnp.int32, shape, dim)


def floats(shape, dim):
    return iota(shape, dim).astype(F32)


def whole_part(value, by):
    return jnp.floor((value + 0.5) * (1.0 / by))


def tent(coarse, fine):
    return jnp.maximum(4.0 - jnp.abs(fine - 4.0 * coarse), 0.0)


def inner(coarse, fine, first):
    below = 1.0 - first * jnp.maximum(1.0 - fine, 0.0)
    return (tent(coarse, fine + 1.0) + tent(coarse, fine - 1.0) * below) * 0.0625


def outer(coarse, fine):
    return tent(coarse, fine) * 0.0625


def kernel(cfg, *refs):
    ngx, ngy, ngz, rhs, fine, side, leaf, n1, n2, n3, ntop = cfg
    plane = ngy * ngz
    cells = side**3
    (rs_h, it_h, cf_h, or_h, li_h, lf_h, ls_h, lt_h, fi_h, fs_h, ft_h, si_h, st_h, ti_h) = refs[:14]
    out_h = refs[14]
    (
        rs, it, cf, od, li, lf, ls, lt, fi, fs, ft, si, st, ti, out_v,
        a21, bmat, e_h, e_l, fsx, fs_hi, fs_lo, stx, st_hi, st_lo,
        w1, w1_h, w1_l, w2, w2_h, w2_l, fi_low, si_low,
        flat, got_flat, got_thin, send1, got1, send2, got2, up_send, up_got,
        part, got5, s6, got6, yall, down_send, down_got, gap2, gap1, corr, got_corr,
        local_sem, out_sem, send_sem, recv_sem,
    ) = refs[15:]

    a, b, c = (lax.axis_index(n) for n in AXES)
    me = b * ngz + c
    used = [0]
    pending = []

    def at(dx, dy, dz):
        return (
            lax.rem(a + (dx + ngx), ngx) if dx else a,
            lax.rem(b + (dy + ngy), ngy) if dy else b,
            lax.rem(c + (dz + ngz), ngz) if dz else c,
        )

    def send(src, dst, device):
        i = used[0]
        used[0] += 1
        copy = pltpu.make_async_remote_copy(
            src_ref=src,
            dst_ref=dst,
            send_sem=send_sem.at[i],
            recv_sem=recv_sem.at[i],
            device_id=device,
            device_id_type=MESH,
        )
        copy.start()
        pending.append(copy)
        return copy

    def arrive(copies):
        for copy in copies:
            copy.wait_recv()

    pairs = [
        (it_h, it), (rs_h, rs), (cf_h, cf), (or_h, od), (li_h, li), (lf_h, lf), (ls_h, ls), (lt_h, lt),
        (fi_h, fi), (si_h, si), (fs_h, fs), (ft_h, ft), (st_h, st), (ti_h, ti),
    ]
    loads = [pltpu.make_async_copy(s, d, local_sem.at[i]) for i, (s, d) in enumerate(pairs)]
    for load in loads:
        load.start()

    partners = set()
    for dy in range(ngy):
        for dz in range(ngz):
            partners.add((0, dy, dz))
    for dx in range(ngx):
        partners.add((dx, 0, 0))
    for d in HALO + RIM:
        for s in (1, -1):
            partners.add((s * d[0] % ngx, s * d[1] % ngy, s * d[2] % ngz))
    partners.discard((0, 0, 0))
    barrier = pltpu.get_barrier_semaphore()
    for d in sorted(partners):
        pl.semaphore_signal(barrier, inc=1, device_id=at(*d), device_id_type=MESH)

    first_x = jnp.where(a == 0, 1.0, 0.0).astype(F32)
    first_y = jnp.where(b == 0, 1.0, 0.0).astype(F32)
    first_z = jnp.where(c == 0, 1.0, 0.0).astype(F32)

    shape = (64, fine * fine)
    row, col = floats(shape, 0), floats(shape, 1)
    cx = whole_part(row, 8)
    cy = row - 8.0 * cx - 1.0
    cx = cx - 1.0
    fx = whole_part(col, fine)
    fy = col - fine * fx
    ox, oy = outer(cx, fx), outer(cy, fy)
    a21[0:64, :] = (inner(cx, fx, first_x) * oy + ox * inner(cy, fy, first_y)).astype(BF16)
    a21[64:128, :] = (ox * oy).astype(BF16)

    zshape = (8 * rhs, 2 * rhs * fine)
    row, col = floats(zshape, 0), floats(zshape, 1)
    cz = whole_part(row, rhs)
    cr = row - rhs * cz
    cz = cz - 1.0
    kind = whole_part(col, rhs * fine)
    rest = col - rhs * fine * kind
    fr = whole_part(rest, fine)
    fz = rest - fine * fr
    same = jnp.maximum(1.0 - jnp.abs(cr - fr), 0.0)
    wvz = ((1.0 - kind) * outer(cz, fz) + kind * inner(cz, fz, first_z)) * same
    wvz = wvz.astype(BF16)

    for load in loads[:3]:
        load.wait()
    g1, g2 = [], []
    own = a21[64:128, :]
    both = a21[...]
    for r in range(rhs):
        now = it[r]
        q = rs[r] - (6.0 + cf[...]) * now
        q_h, q_l = split(q.reshape(fine * fine, fine))
        i_h, i_l = split(now.reshape(fine * fine, fine))
        from_it = dot(both, i_h) + dot(both, i_l)
        g1.append(from_it[0:64] + dot(own, q_h) + dot(own, q_l))
        g2.append(from_it[64:128])
    g_h, g_l = split(jnp.concatenate(g1 + g2, axis=1))
    ct = dot(wvz, g_h, BACK) + dot(wvz, g_l, BACK)
    for j in range(4):
        lo = ct[2 * rhs * j : 2 * rhs * j + rhs]
        hi = ct[2 * rhs * j + rhs : 2 * rhs * j + 2 * rhs]
        flat[j] = jnp.concatenate([lo, hi], axis=1)

    pl.semaphore_wait(barrier, len(partners))

    halo_copies = []
    for i, (dx, dy, dz) in enumerate(HALO):
        if dz == 0:
            src, dst = flat, got_flat.at[i]
        else:
            src, dst = flat.at[3 if dz == 1 else 0], got_thin.at[i - len(FLAT)]
        halo_copies.append(send(src, dst, at(dx, dy, dz)))
    for load in loads[3:]:
        load.wait()
    fi_copy = send(fi, fi_low, at(0, 0, 1))
    si_copy = send(si, si_low, at(0, 1, 0))

    shape = (cells, 512)
    m, k = iota(shape, 0), iota(shape, 1)
    e1, e2 = leaf + n1, leaf + n1 + n2
    want = jnp.where(m < e1, m + (128 - leaf), jnp.where(m < e2, m + (256 - e1), m + (384 - e2)))
    bmat[...] = jnp.where((m >= leaf) & (k == want), 1.0, 0.0).astype(F32)
    li_v = li[...]
    li_pair = split(li_v)
    bmat[0:leaf, 0:leaf] = li_v
    bmat[0:leaf, 128 : 128 + 2 * n1] = -times(li_v, split(lf[...]))
    bmat[0:leaf, 256 : 256 + 2 * n2] = -times(li_v, split(ls[...]))
    bmat[0:leaf, 384 : 384 + 2 * n3] = -times(li_v, split(lt[...]))
    bh, bl = split(bmat[...])
    shape = (512, cells)
    k = iota(shape, 0)
    z, x, y = k >> 6, (k >> 3) & 7, k & 7
    inside = (z >= 1) & (z <= side) & (x >= 1) & (x <= side) & (y >= 1) & (y <= side)
    cell = jnp.where(inside, ((x - 1) * side + (y - 1)) * side + (z - 1), -1)
    chosen = jnp.where(cell == od[...], 1.0, 0.0).astype(BF16)
    e_h[...] = dot(chosen, bh).astype(BF16)
    e_l[...] = dot(chosen, bl).astype(BF16)

    fsx[...] = jnp.zeros(fsx.shape, F32)
    fsx[0:n1, 0 : 2 * n2] = -fs[...]
    fsx[0:n1, 128 : 128 + 2 * n3] = -ft[...]
    stx[...] = jnp.zeros(stx.shape, F32)
    stx[0:n2, 0 : 2 * n3] = -st[...]
    place1 = n1 * lax.rem(c, 4)
    place2 = n2 * lax.rem(me, 4)
    shift = (128, 32)
    put1 = jnp.where(iota(shift, 0) == iota(shift, 1) + place1, 1.0, 0.0).astype(BF16)
    put2 = jnp.where(iota(shift, 0) == iota(shift, 1) + place2, 1.0, 0.0).astype(BF16)
    hi, lo = split(fsx[...])
    fs_hi[...] = dot(put1, hi).astype(BF16)
    fs_lo[...] = dot(put1, lo).astype(BF16)
    hi, lo = split(stx[...])
    st_hi[...] = dot(put2, hi).astype(BF16)
    st_lo[...] = dot(put2, lo).astype(BF16)

    groups1 = (ngz + 3) // 4
    groups2 = (plane + 3) // 4

    def grouped(w, high, low, mine, lower, size, groups, members, keep):
        w[...] = jnp.zeros(w.shape, F32)
        mine_v = mine[...]
        lower_v = jnp.where(keep, lower[...], 0.0)
        for g in range(groups):
            wide = min(4, members - 4 * g) * size
            s = slice(4 * g * size, 4 * g * size + wide)
            w[0:size, 128 * g : 128 * g + wide] = mine_v[:, s]
            w[size : 2 * size, 128 * g : 128 * g + wide] = lower_v[:, s]
        hi, lo = split(w[...])
        high[...] = hi
        low[...] = lo

    fi_copy.wait_recv()
    grouped(w1, w1_h, w1_l, fi, fi_low, n1, groups1, ngz, c > 0)

    arrive(halo_copies)
    lane = iota((rhs, 128), 1)
    at_z, at_x, at_y = lane >> 6, (lane >> 3) & 7, lane & 7

    def along(at_, d):
        if d == 0:
            return (at_ >= 1) & (at_ <= side)
        return at_ == (1 if d == 1 else side)

    def exists(i, d, n):
        return (i - d >= 0) & (i - d < n) if d else True

    total = [flat[j] for j in range(4)]
    for i, (dx, dy, dz) in enumerate(HALO):
        turn = (-(side * 8) * dx - side * dy) % 128
        keep = along(at_x, dx) & along(at_y, dy)
        there = exists(a, dx, ngx) & exists(b, dy, ngy) & exists(c, dz, ngz)
        keep = keep & there
        if dz == 0:
            for j in range(4):
                v = got_flat[i, j]
                v = pltpu.roll(v, turn, 1) if turn else v
                total[j] += jnp.where(keep, v, 0.0)
        else:
            v = got_thin[i - len(FLAT)]
            v = pltpu.roll(v, turn, 1) if turn else v
            keep = keep & (at_z == (1 if dz == 1 else 0))
            j = 0 if dz == 1 else 3
            total[j] += jnp.where(keep, v, 0.0)

    e_pair = (e_h[...], e_l[...])
    s = times(jnp.concatenate(total, axis=1), e_pair)
    s_leaf, s1, s23 = s[:, 0:128], s[:, 128:256], s[:, 256:512]

    w1_pair = (w1_h[...], w1_l[...])
    partial = times(s1, w1_pair)
    for g in range(groups1):
        send1[g] = partial[:, 128 * g : 128 * g + 128]
    copies = []
    for k in range(1, ngz):
        there = at(0, 0, k)
        copies.append(send(send1.at[there[2] // 4], got1.at[k], there))
    own1 = send1[c // 4]

    si_copy.wait_recv()
    grouped(w2, w2_h, w2_l, si, si_low, n2, groups2, plane, b > 0)

    arrive(copies)
    for k in range(1, ngz):
        own1 += got1[k]
    own1 = jnp.where((lane >= place1) & (lane < place1 + n1), own1, 0.0)
    fs_pair = (fs_hi[...], fs_lo[...])
    s23 = s23 + times(own1, fs_pair)
    s2, s3 = s23[:, 0:128], s23[:, 128:256]

    w2_pair = (w2_h[...], w2_l[...])
    partial = times(s2, w2_pair)
    for g in range(groups2):
        send2[g] = partial[:, 128 * g : 128 * g + 128]
    others = []
    for k in range(1, plane):
        d = lax.rem(me + k, plane)
        others.append((d, (a, lax.div(d, ngz), lax.rem(d, ngz))))
    copies = [send(send2.at[d // 4], got2.at[k], there) for k, (d, there) in enumerate(others, 1)]
    own2 = send2[me // 4]
    arrive(copies)
    for k in range(1, plane):
        own2 += got2[k]
    own2 = jnp.where((lane >= place2) & (lane < place2 + n2), own2, 0.0)
    st_pair = (st_hi[...], st_lo[...])
    s3 = s3 + times(own2, st_pair)

    up_send[...] = s3
    copies = [send(up_send, up_got, at(-1, 0, 0))]
    arrive(copies)
    target = s3 + jnp.where(a < ngx - 1, pltpu.roll(up_got[...], 128 - n3, 1), 0.0)
    columns = jnp.transpose(jnp.concatenate([target, jnp.zeros((8 - rhs, 128), F32)], axis=0))
    spread = [jnp.broadcast_to(columns[0:n3, r : r + 1], (n3, 128)) for r in range(rhs)]

    width = ntop // ngz
    step = 128 if width % 128 == 0 else width
    copies = []
    for j in list(range(1, ngz)) + [0]:
        group = at(0, 0, j)[2]
        for p in range(0, width, step):
            start = group * width + p
            if step == 128:
                start = pl.multiple_of(start, 128)
            block = ti[:, pl.ds(start, step)]
            for r in range(rhs):
                scale = spread[r] if step == 128 else jnp.broadcast_to(spread[r][:, 0:1], (n3, step))
                part[r, group, :, p : p + step] = jnp.sum(scale * block, axis=0, keepdims=True)
        for i in list(range(1, ngy)) + [0]:
            if i or j:
                there = at(0, i, j)
                copies.append(send(part.at[there[1], there[2]], got5.at[i * ngz + j], there))
    term = part[b, c]
    arrive(copies)
    for k in range(1, plane):
        term += got5[k]
    s6[...] = term
    copies = [send(s6, got6.at[k], at(k, 0, 0)) for k in range(1, ngx)]
    arrive(copies)
    for k in range(1, ngx):
        term += got6[k]
    yall[b, c] = term
    copies = [send(yall.at[b, c], yall.at[b, c], there) for _, there in others]
    arrive(copies)

    total = [jnp.zeros((n3, step), F32) for _ in range(rhs)]
    for g in range(ngz):
        for p in range(0, width, step):
            block = ti[:, g * width + p : g * width + p + step]
            for r in range(rhs):
                total[r] += block * yall[r, g, :, p : p + step]
    ones = jnp.ones((8, step), BF16)
    back = jnp.zeros((rhs, n3), F32)
    which = iota((rhs, n3), 0)
    for r in range(rhs):
        hi, lo = split(total[r])
        both_sums = dot(ones, hi, BACK) + dot(ones, lo, BACK)
        back += jnp.where(which == r, both_sums[0:rhs], 0.0)
    down_send[...] = jnp.zeros((rhs, 128), F32)
    down_send[:, 0:n3] = back
    copies = [send(down_send, down_got, at(1, 0, 0))]
    arrive(copies)
    z3 = down_send[...] + jnp.where(a > 0, pltpu.roll(down_got[...], n3, 1), 0.0)

    gap2[me] = own2 + times(z3, st_pair, BACK)
    copies = [send(gap2.at[me], gap2.at[me], there) for _, there in others]
    gap_first = own1 + times(z3, (fs_pair[0][:, 128:256], fs_pair[1][:, 128:256]), BACK)
    arrive(copies)

    def gathered(ref, members):
        blocks = []
        for g in range((members + 3) // 4):
            block = ref[4 * g]
            for i in range(4 * g + 1, min(4 * g + 4, members)):
                block += ref[i]
            blocks.append(block)
        return jnp.concatenate(blocks, axis=1)

    z2 = times(gathered(gap2, plane), w2_pair, BACK)

    gap1[c] = gap_first + times(z2, (fs_pair[0][:, 0:128], fs_pair[1][:, 0:128]), BACK)
    copies = [send(gap1.at[c], gap1.at[c], at(0, 0, k)) for k in range(1, ngz)]
    arrive(copies)
    z1 = times(gathered(gap1, ngz), w1_pair, BACK)

    result = times(jnp.concatenate([s_leaf, z1, z2, z3], axis=1), e_pair, BACK)
    for j in range(4):
        corr[j] = result[:, 128 * j : 128 * j + 128]
    copies = []
    for i, (dx, dy, dz) in enumerate(RIM):
        there = at(-dx, -dy, -dz)
        if dz == 0:
            copies.append(send(corr, got_corr.at[i], there))
        else:
            copies.append(send(corr.at[0], got_corr.at[i, 0], there))

    shape = (fine * fine, 128)
    row, col = floats(shape, 0), floats(shape, 1)
    fx = whole_part(row, fine)
    fy = row - fine * fx
    half = whole_part(col, 64)
    rest = col - 64.0 * half
    cx = whole_part(rest, 8)
    cy = rest - 8.0 * cx - 1.0
    spread_xy = (tent(cx - 1.0, fx) * tent(cy, fy) * 0.0625).astype(BF16)
    shape = (rhs * fine, 8 * rhs)
    row, col = floats(shape, 0), floats(shape, 1)
    fr = whole_part(row, fine)
    fz = row - fine * fr
    cz = whole_part(col, rhs)
    cr = col - rhs * cz
    same = jnp.maximum(1.0 - jnp.abs(cr - fr), 0.0)
    spread_z = (tent(cz - 1.0, fz) * same * 0.25).astype(BF16)

    arrive(copies)
    total = [corr[j] for j in range(4)]
    for i, (dx, dy, dz) in enumerate(RIM):
        turn = side * 8 * dx + side * dy
        keep = (at_x == side + 1) if dx else (at_x <= side)
        keep = keep & ((at_y == side + 1) if dy else (at_y <= side))
        if dx:
            keep = keep & (a < ngx - 1)
        if dy:
            keep = keep & (b < ngy - 1)
        if dz:
            keep = keep & (c < ngz - 1) & (at_z == 1)
        for j in range(4) if dz == 0 else (0,):
            v = got_corr[i, j]
            v = pltpu.roll(v, turn, 1) if turn else v
            total[j if dz == 0 else 3] += jnp.where(keep, v, 0.0)
    rows = []
    for j in range(4):
        rows += [total[j][:, 0:64], total[j][:, 64:128]]
    ct_h, ct_l = split(jnp.concatenate(rows, axis=0))
    ht = dot(spread_z, ct_h) + dot(spread_z, ct_l)
    ht_h = ht.astype(BF16).astype(F32)
    ht = jnp.concatenate([ht_h, ht - ht_h], axis=1)
    stores = []
    for r in range(rhs):
        part_r = ht[r * fine : (r + 1) * fine].astype(BF16)
        out_v[r] = dot(spread_xy, part_r, BACK).reshape(fine, fine, fine)
        store = pltpu.make_async_copy(out_v.at[r], out_h.at[r], out_sem.at[r])
        store.start()
        stores.append(store)
    for copy in pending:
        copy.wait_send()
    for store in stores:
        store.wait()


def per_device(mesh_sizes, *args):
    (rs, it, cf, od, li, lf, ls, lt, fi, fs, ft, si, st, ti) = args
    ngx, ngy, ngz = mesh_sizes
    od = od.reshape(1, -1)
    li, lf, ls, lt, fs, ft, st = (v[0, 0, 0] for v in (li, lf, ls, lt, fs, ft, st))
    fi, si = fi[0, 0], si[0]
    rhs, fine = rs.shape[0], rs.shape[1]
    side = fine // 4
    leaf, n1, n2, n3, ntop = li.shape[0], fs.shape[0], st.shape[0], ti.shape[0], ti.shape[1]
    cfg = (ngx, ngy, ngz, rhs, fine, side, leaf, n1, n2, n3, ntop)
    plane = ngy * ngz
    groups1, groups2 = (ngz + 3) // 4, (plane + 3) // 4
    cells = side**3
    inputs = [rs, it, cf, od, li, lf, ls, lt, fi, fs, ft, si, st, ti]
    v = pltpu.VMEM
    width = ntop // ngz
    copies = len(HALO) + 2 + 3 * (ngz - 1) + 4 * (plane - 1) + 2 + (ngx - 1) + len(RIM)
    scratch = [v(x.shape, x.dtype) for x in inputs]
    scratch += [
        v(rs.shape, F32),
        v((128, fine * fine), BF16),
        v((cells, 512), F32), v((512, 512), BF16), v((512, 512), BF16),
        v((32, 256), F32), v((128, 256), BF16), v((128, 256), BF16),
        v((32, 128), F32), v((128, 128), BF16), v((128, 128), BF16),
        v((128, 128 * groups1), F32), v((128, 128 * groups1), BF16), v((128, 128 * groups1), BF16),
        v((128, 128 * groups2), F32), v((128, 128 * groups2), BF16), v((128, 128 * groups2), BF16),
        v(fi.shape, F32), v(si.shape, F32),
        v((4, rhs, 128), F32), v((len(FLAT), 4, rhs, 128), F32), v((len(HALO) - len(FLAT), rhs, 128), F32),
        v((groups1, rhs, 128), F32), v((ngz, rhs, 128), F32),
        v((groups2, rhs, 128), F32), v((plane, rhs, 128), F32),
        v((rhs, 128), F32), v((rhs, 128), F32),
        v((rhs, ngz, 1, width), F32), v((plane, 1, width), F32),
        v((1, width), F32), v((ngx, 1, width), F32),
        v((rhs, ngz, 1, width), F32),
        v((rhs, 128), F32), v((rhs, 128), F32),
        v((plane, rhs, 128), F32), v((ngz, rhs, 128), F32),
        v((4, rhs, 128), F32), v((len(RIM), 4, rhs, 128), F32),
        pltpu.SemaphoreType.DMA((len(inputs),)), pltpu.SemaphoreType.DMA((rhs,)),
        pltpu.SemaphoreType.DMA((copies,)), pltpu.SemaphoreType.DMA((copies,)),
    ]
    return pl.pallas_call(
        functools.partial(kernel, cfg),
        out_shape=jax.ShapeDtypeStruct(rs.shape, F32),
        in_specs=[pl.BlockSpec(memory_space=pl.ANY)] * len(inputs),
        out_specs=pl.BlockSpec(memory_space=pl.ANY),
        scratch_shapes=scratch,
        compiler_params=pltpu.CompilerParams(
            collective_id=0, has_side_effects=True, vmem_limit_bytes=48 * 1024 * 1024
        ),
        name="coarse_correction",
    )(*inputs)


def solution(mesh):
    sizes = tuple(mesh.shape[n] for n in AXES)
    cells = P("gx", "gy", "gz")
    lines = P("gx", "gy", "gz", None)
    blocks = P("gx", "gy", "gz", None, None)
    field = P(None, "gx", "gy", "gz")
    return jax.shard_map(
        functools.partial(per_device, sizes),
        mesh=mesh,
        in_specs=(
            field, field, cells, lines, blocks, blocks, blocks, blocks, lines, blocks, blocks,
            P("gx", ("gy", "gz"), None), blocks, P(("gx", "gy", "gz"), None),
        ),
        out_specs=field,
        check_vma=False,
    )
```

time: 279 us -> 79.5 us (0.28)
  starting transfers between devices: 77.4 us -> 0 us
  blocking collectives: 73.5 us -> 0 us
  Pallas kernels: 0 us -> 65 us
  waiting for transfers between devices: 62.6 us -> 0 us
  local copies, waits for them, and re-layouts: 40.7 us -> 13.8 us
  other arithmetic: 15.3 us -> 0 us
  matrix products: 7.63 us -> 0 us
    all_to_all x6 -> x0, blocking collectives: 73.5 us -> none  [the longest x4 43.2 us: sent_to_all(): return lax.all_to_all(copies, axis, split_axis=0, concat_axis=0, tiled=True)]
    ppermute x24 -> x0, starting transfers between devices: 66.4 us -> none  [the longest x18 49.6 us: shifted(): return lax.ppermute(shard, axis, pairs)]
    pallas_call x0 -> x1, Pallas kernels: none -> 65 us  [per_device(): pl.pallas_call(functools.partial(kernel, cfg), out_shape=jax.ShapeDtypeSt...]
    ppermute x24 -> x0, waiting for transfers between devices: 50.9 us -> none  [the longest x18 50.9 us: shifted(): return lax.ppermute(shard, axis, pairs)]
    slice x25 -> x0, local copies, waits for them, and re-layouts: 12.6 us -> none  [the longest x2 5.04 us: padded_2(): leading = lax.slice_in_dim(shard, 0, width, axis=dim)]
    all_to_all x2 -> x0, waiting for transfers between devices: 11.7 us -> none  [summed_on_arrival(): lax.all_to_all(cut_along(shard, dim, peers), axis, 0, 0, tiled=True)]
    all_to_all x2 -> x0, starting transfers between devices: 11 us -> none  [summed_on_arrival(): lax.all_to_all(cut_along(shard, dim, peers), axis, 0, 0, tiled=True)]
    dot_general x20 -> x0, matrix products: 7.63 us -> none  [the longest x10 4.69 us: product(): jnp.dot(operand, matrix, precision=precise, preferred_element_type=jnp.fl...]
  transfers between devices with their start and end apart: 26 -> 0, of which waited for: 20 -> 0; matrix products, arithmetic and copies ran while one was open for 5% -> 0% of each run, Pallas kernels for 0% -> 0%
where the time goes in v1:
time: 79.5 us; the launch traced here: 78.8 us
  Pallas kernels  65 us (82%)
  local copies, waits for them, and re-layouts  13.8 us (17%)
    pallas_call x1, Pallas kernels, per_device(): pl.pallas_call(functools.partial(kernel, cfg), out_shape=jax.ShapeDtypeSt...  65 us
    unnamed x20, local copies, waits for them, and re-layouts  13.8 us

profile of v1, /device:TPU:1, one launch (start us, length us, event | category | flops | bytes accessed | tf_op | source)
XLA Modules:
  0.0 78.8 jit_solution(1373595016370250726)
XLA Ops:
  0.0 0.7 copy.35
  0.7 0.7 copy.34
  1.4 0.7 copy.33
  2.1 0.7 copy.32
  2.9 0.8 %copy.31 = f32[1,1,1,125,125]{4,3,2,1,0:T(8,128)S(1)} copy(f32[1,1,1,125,125]{4,2,3,1,0:T(1,128)} %param.18) | data formatting | bytes 125000
  3.7 0.8 %copy.15 = f32[1,1,1,125,50]{4,3,2,1,0:T(8,128)S(1)} copy(f32[1,1,1,125,50]{3,2,4,1,0:T(1,128)} %param.19) | data formatting | bytes 50000 | tf_op args[5]
  4.6 0.9 %copy.16 = f32[1,1,1,125,60]{4,3,2,1,0:T(8,128)S(1)} copy(f32[1,1,1,125,60]{3,2,4,1,0:T(1,128)} %param.20) | data formatting | bytes 60000 | tf_op args[6]
  5.4 0.9 %copy.17 = f32[1,1,1,125,72]{4,3,2,1,0:T(8,128)S(1)} copy(f32[1,1,1,125,72]{3,4,2,1,0:T(8,128)} %param.21) | data formatting | bytes 72000 | tf_op args[7]
  6.3 0.9 %copy.30 = f32[1,30,960]{2,1,0:T(8,128)S(1)} copy(f32[1,30,960]{2,0,1:T(1,128)} %param.25) | data formatting | bytes 230400
  7.2 0.0 copy-start
  7.3 1.4 %copy-done = f32[36,9216]{1,0:T(8,128)S(1)} copy-done((f32[36,9216]{1,0:T(8,128)S(1)}, f32[36,9216]{1,0:T(8,128)}, u32[]{:S(2)}) %copy-start) | copy-done | bytes 1327128
  8.6 0.0 copy-start.1
  8.6 1.3 %copy-done.1 = f32[4,24,24,24]{3,2,1,0:T(8,128)S(1)} copy-done((f32[4,24,24,24]{3,2,1,0:T(8,128)S(1)}, f32[4,24,24,24]{3,2,1,0:T(8,128)}, u32[]{:S(2)}) %copy-start.1) | copy-done | bytes 221208
  9.9 0.0 copy-start.2
  9.9 1.3 %copy-done.2 = f32[4,24,24,24]{3,2,1,0:T(8,128)S(1)} copy-done((f32[4,24,24,24]{3,2,1,0:T(8,128)S(1)}, f32[4,24,24,24]{3,2,1,0:T(8,128)}, u32[]{:S(2)}) %copy-start.2) | copy-done | bytes 221208
  11.2 0.0 copy-start.3
  11.2 1.0 %copy-done.3 = f32[24,24,24]{2,1,0:T(8,128)S(1)} copy-done((f32[24,24,24]{2,1,0:T(8,128)S(1)}, f32[24,24,24]{2,1,0:T(8,128)}, u32[]{:S(2)}) %copy-start.3) | copy-done | bytes 55320
  12.1 0.0 copy-start.4
  12.1 0.7 copy-done.4
  12.8 65.0 %coarse_correction.1 = f32[4,24,24,24]{3,2,1,0:T(8,128)S(1)} custom-call(f32[4,24,24,24]{3,2,1,0:T(8,128)S(1)} %copy-done.1, f32[4,24,24,24]{3,2,1,0:T(8,128)S(1)} %copy-done.2, f32[24,24,24]{2,1,0:T(8,128)S(1)} %copy-done.3, s32[1,216]{1,0:T(1,128)S(1)} %bitcast.31, f32[125,125]{1,0:T(8,128)S(1)} %bitcast.23, f32[125,50]{1,0:T(8,128)S(1)} %bitcast.24, ...), custom_call_target="tpu_custom_call" | custom-call | tf_op jit(solution)/shard_map/coarse_correction/pallas_call | solution.py:506
  77.8 1.0 %copy.37 = f32[4,24,24,24]{3,2,1,0:T(8,128)} copy(f32[4,24,24,24]{3,2,1,0:T(8,128)S(1)} %coarse_correction.1) | data formatting | bytes 442368
Async XLA Ops:
  7.2 1.4 %copy-start = (f32[36,9216]{1,0:T(8,128)S(1)}, f32[36,9216]{1,0:T(8,128)}, u32[]{:S(2)}) copy-start(f32[36,9216]{1,0:T(8,128)} %refs_13_.1) | copy-start | bytes 3981316
  8.6 1.3 %copy-start.1 = (f32[4,24,24,24]{3,2,1,0:T(8,128)S(1)}, f32[4,24,24,24]{3,2,1,0:T(8,128)}, u32[]{:S(2)}) copy-start(f32[4,24,24,24]{3,2,1,0:T(8,128)} %refs_0_.1) | copy-start | bytes 663556
  9.9 1.3 %copy-start.2 = (f32[4,24,24,24]{3,2,1,0:T(8,128)S(1)}, f32[4,24,24,24]{3,2,1,0:T(8,128)}, u32[]{:S(2)}) copy-start(f32[4,24,24,24]{3,2,1,0:T(8,128)} %refs_1_.1) | copy-start | bytes 663556
  11.2 1.0 %copy-start.3 = (f32[24,24,24]{2,1,0:T(8,128)S(1)}, f32[24,24,24]{2,1,0:T(8,128)}, u32[]{:S(2)}) copy-start(f32[24,24,24]{2,1,0:T(8,128)} %refs_2_.1) | copy-start | bytes 165892
  12.1 0.7 copy-start.4

commit v2 on v1

--- a/solution.py
+++ b/solution.py
@@ -1,3 +1,4 @@
+import contextlib
 import functools
 
 import jax
@@ -69,18 +70,24 @@
     (rs_h, it_h, cf_h, or_h, li_h, lf_h, ls_h, lt_h, fi_h, fs_h, ft_h, si_h, st_h, ti_h) = refs[:14]
     out_h = refs[14]
     (
-        rs, it, cf, od, li, lf, ls, lt, fi, fs, ft, si, st, ti, out_v,
+        rs, it, cf, od, li, lf, ls, lt, fi, fs, ft, si, st, ti,
         a21, bmat, e_h, e_l, fsx, fs_hi, fs_lo, stx, st_hi, st_lo,
-        w1, w1_h, w1_l, w2, w2_h, w2_l, fi_low, si_low,
+        w1, w1_h, w1_l, w2, w2_h, w2_l, fi_low, si_low, rall, total_ref,
         flat, got_flat, got_thin, send1, got1, send2, got2, up_send, up_got,
         part, got5, s6, got6, yall, down_send, down_got, gap2, gap1, corr, got_corr,
-        local_sem, out_sem, send_sem, recv_sem,
+        local_sem, send_sem, recv_sem,
     ) = refs[15:]
 
     a, b, c = (lax.axis_index(n) for n in AXES)
     me = b * ngz + c
     used = [0]
     pending = []
+    stack = contextlib.ExitStack()
+
+    def phase(name):
+        stack.close()
+        stack.enter_context(jax.named_scope(name))
+
 
     def at(dx, dy, dz):
         return (
@@ -108,14 +115,17 @@
         for copy in copies:
             copy.wait_recv()
 
+    phase("p00_loads")
     pairs = [
         (it_h, it), (rs_h, rs), (cf_h, cf), (or_h, od), (li_h, li), (lf_h, lf), (ls_h, ls), (lt_h, lt),
         (fi_h, fi), (si_h, si), (fs_h, fs), (ft_h, ft), (st_h, st), (ti_h, ti),
     ]
+    pairs = [(s.at[:, 0, :] if len(s.shape) > len(d.shape) else s, d) for s, d in pairs]
     loads = [pltpu.make_async_copy(s, d, local_sem.at[i]) for i, (s, d) in enumerate(pairs)]
     for load in loads:
         load.start()
 
+    phase("p01_signal")
     partners = set()
     for dy in range(ngy):
         for dz in range(ngz):
@@ -134,6 +144,7 @@
     first_y = jnp.where(b == 0, 1.0, 0.0).astype(F32)
     first_z = jnp.where(c == 0, 1.0, 0.0).astype(F32)
 
+    phase("p02_weights")
     shape = (64, fine * fine)
     row, col = floats(shape, 0), floats(shape, 1)
     cx = whole_part(row, 8)
@@ -158,6 +169,7 @@
     wvz = ((1.0 - kind) * outer(cz, fz) + kind * inner(cz, fz, first_z)) * same
     wvz = wvz.astype(BF16)
 
+    phase("p03_wait_residual")
     for load in loads[:3]:
         load.wait()
     g1, g2 = [], []
@@ -178,6 +190,7 @@
         hi = ct[2 * rhs * j + rhs : 2 * rhs * j + 2 * rhs]
         flat[j] = jnp.concatenate([lo, hi], axis=1)
 
+    phase("p05_barrier")
     pl.semaphore_wait(barrier, len(partners))
 
     halo_copies = []
@@ -192,17 +205,18 @@
     fi_copy = send(fi, fi_low, at(0, 0, 1))
     si_copy = send(si, si_low, at(0, 1, 0))
 
-    shape = (cells, 512)
+    phase("p07_factor")
+    shape = (cells, 384)
     m, k = iota(shape, 0), iota(shape, 1)
     e1, e2 = leaf + n1, leaf + n1 + n2
-    want = jnp.where(m < e1, m + (128 - leaf), jnp.where(m < e2, m + (256 - e1), m + (384 - e2)))
+    want = jnp.where(m < e1, m + (192 - leaf), jnp.where(m < e2, m + (128 - e1), m + (256 - e2)))
     bmat[...] = jnp.where((m >= leaf) & (k == want), 1.0, 0.0).astype(F32)
     li_v = li[...]
     li_pair = split(li_v)
     bmat[0:leaf, 0:leaf] = li_v
-    bmat[0:leaf, 128 : 128 + 2 * n1] = -times(li_v, split(lf[...]))
-    bmat[0:leaf, 256 : 256 + 2 * n2] = -times(li_v, split(ls[...]))
-    bmat[0:leaf, 384 : 384 + 2 * n3] = -times(li_v, split(lt[...]))
+    bmat[0:leaf, 192 : 192 + 2 * n1] = -times(li_v, split(lf[...]), BACK)
+    bmat[0:leaf, 128 : 128 + 2 * n2] = -times(li_v, split(ls[...]), BACK)
+    bmat[0:leaf, 256 : 256 + 2 * n3] = -times(li_v, split(lt[...]), BACK)
     bh, bl = split(bmat[...])
     shape = (512, cells)
     k = iota(shape, 0)
@@ -213,12 +227,13 @@
     e_h[...] = dot(chosen, bh).astype(BF16)
     e_l[...] = dot(chosen, bl).astype(BF16)
 
+    phase("p08_place")
     fsx[...] = jnp.zeros(fsx.shape, F32)
     fsx[0:n1, 0 : 2 * n2] = -fs[...]
     fsx[0:n1, 128 : 128 + 2 * n3] = -ft[...]
     stx[...] = jnp.zeros(stx.shape, F32)
     stx[0:n2, 0 : 2 * n3] = -st[...]
-    place1 = n1 * lax.rem(c, 4)
+    place1 = 32 * lax.rem(c, 4)
     place2 = n2 * lax.rem(me, 4)
     shift = (128, 32)
     put1 = jnp.where(iota(shift, 0) == iota(shift, 1) + place1, 1.0, 0.0).astype(BF16)
@@ -233,23 +248,21 @@
     groups1 = (ngz + 3) // 4
     groups2 = (plane + 3) // 4
 
-    def grouped(w, high, low, mine, lower, size, groups, members, keep):
-        w[...] = jnp.zeros(w.shape, F32)
-        mine_v = mine[...]
-        lower_v = jnp.where(keep, lower[...], 0.0)
-        for g in range(groups):
-            wide = min(4, members - 4 * g) * size
-            s = slice(4 * g * size, 4 * g * size + wide)
-            w[0:size, 128 * g : 128 * g + wide] = mine_v[:, s]
-            w[size : 2 * size, 128 * g : 128 * g + wide] = lower_v[:, s]
-        hi, lo = split(w[...])
-        high[...] = hi
-        low[...] = lo
-
+    phase("p09_w1")
     fi_copy.wait_recv()
-    grouped(w1, w1_h, w1_l, fi, fi_low, n1, groups1, ngz, c > 0)
-
+    w1[...] = jnp.zeros(w1.shape, F32)
+    mine = fi[:, 0, :]
+    lower = jnp.where(c > 0, fi_low[:, 0, :], 0.0)
+    for m in range(ngz):
+        w1[64 : 64 + n1, 32 * m : 32 * m + n1] = mine[:, n1 * m : n1 * m + n1]
+        w1[64 + n1 : 64 + 2 * n1, 32 * m : 32 * m + n1] = lower[:, n1 * m : n1 * m + n1]
+    hi, lo = split(w1[...])
+    w1_h[...] = hi
+    w1_l[...] = lo
+
+    phase("p10_wait_halo")
     arrive(halo_copies)
+    phase("p11_add_halo")
     lane = iota((rhs, 128), 1)
     at_z, at_x, at_y = lane >> 6, (lane >> 3) & 7, lane & 7
 
@@ -279,12 +292,14 @@
             j = 0 if dz == 1 else 3
             total[j] += jnp.where(keep, v, 0.0)
 
+    phase("p12_leaf")
     e_pair = (e_h[...], e_l[...])
     s = times(jnp.concatenate(total, axis=1), e_pair)
-    s_leaf, s1, s23 = s[:, 0:128], s[:, 128:256], s[:, 256:512]
-
+    s_leaf, s12, s3 = s[:, 0:128], s[:, 128:256], s[:, 256:384]
+
+    phase("p13_first_product")
     w1_pair = (w1_h[...], w1_l[...])
-    partial = times(s1, w1_pair)
+    partial = times(s12, w1_pair)
     for g in range(groups1):
         send1[g] = partial[:, 128 * g : 128 * g + 128]
     copies = []
@@ -293,19 +308,33 @@
         copies.append(send(send1.at[there[2] // 4], got1.at[k], there))
     own1 = send1[c // 4]
 
+    phase("p15_w2")
     si_copy.wait_recv()
-    grouped(w2, w2_h, w2_l, si, si_low, n2, groups2, plane, b > 0)
-
-    arrive(copies)
-    for k in range(1, ngz):
+    w2[...] = jnp.zeros(w2.shape, F32)
+    mine = si[:, 0, :]
+    lower = jnp.where(b > 0, si_low[:, 0, :], 0.0)
+    for g in range(groups2):
+        wide = min(4, plane - 4 * g) * n2
+        cut = slice(4 * g * n2, 4 * g * n2 + wide)
+        w2[0:n2, 128 * g : 128 * g + wide] = mine[:, cut]
+        w2[n2 : 2 * n2, 128 * g : 128 * g + wide] = lower[:, cut]
+    hi, lo = split(w2[...])
+    w2_h[0:64, :] = hi
+    w2_l[0:64, :] = lo
+    back_rows = times(fsx[:, 0:64], (hi, lo))
+    rall[c] = back_rows
+
+    phase("p16_wait_first")
+    for k, copy in enumerate(copies, 1):
+        copy.wait_recv()
         own1 += got1[k]
+    phase("p17_second_product")
     own1 = jnp.where((lane >= place1) & (lane < place1 + n1), own1, 0.0)
     fs_pair = (fs_hi[...], fs_lo[...])
-    s23 = s23 + times(own1, fs_pair)
-    s2, s3 = s23[:, 0:128], s23[:, 128:256]
-
-    w2_pair = (w2_h[...], w2_l[...])
-    partial = times(s2, w2_pair)
+    more = times(own1, fs_pair)
+    s2, s3 = s12[:, 0:64] + more[:, 0:64], s3 + more[:, 128:256]
+
+    partial = times(s2, (w2_h[0:64, :], w2_l[0:64, :]))
     for g in range(groups2):
         send2[g] = partial[:, 128 * g : 128 * g + 128]
     others = []
@@ -313,24 +342,36 @@
         d = lax.rem(me + k, plane)
         others.append((d, (a, lax.div(d, ngz), lax.rem(d, ngz))))
     copies = [send(send2.at[d // 4], got2.at[k], there) for k, (d, there) in enumerate(others, 1)]
+    phase("p18_wait_second")
     own2 = send2[me // 4]
-    arrive(copies)
-    for k in range(1, plane):
+    chips = ngz // 2
+    other = (a, b, c + 1 - 2 * lax.rem(c, 2))
+    beside = [send(rall.at[c], rall.at[c], other)]
+    if chips > 1:
+        after, before = at(0, 0, 2), at(0, 0, -2)
+        beside.append(send(rall.at[c], rall.at[c], after))
+        beside.append(send(rall.at[c], rall.at[c], before))
+    for k, copy in enumerate(copies, 1):
+        copy.wait_recv()
         own2 += got2[k]
+    phase("p19_second_done")
     own2 = jnp.where((lane >= place2) & (lane < place2 + n2), own2, 0.0)
     st_pair = (st_hi[...], st_lo[...])
     s3 = s3 + times(own2, st_pair)
 
+    phase("p20_up")
     up_send[...] = s3
     copies = [send(up_send, up_got, at(-1, 0, 0))]
     arrive(copies)
+    phase("p21_target")
     target = s3 + jnp.where(a < ngx - 1, pltpu.roll(up_got[...], 128 - n3, 1), 0.0)
     columns = jnp.transpose(jnp.concatenate([target, jnp.zeros((8 - rhs, 128), F32)], axis=0))
     spread = [jnp.broadcast_to(columns[0:n3, r : r + 1], (n3, 128)) for r in range(rhs)]
 
+    phase("p22_top_product")
     width = ntop // ngz
     step = 128 if width % 128 == 0 else width
-    copies = []
+    copies, slots = [], []
     for j in list(range(1, ngz)) + [0]:
         group = at(0, 0, j)[2]
         for p in range(0, width, step):
@@ -344,26 +385,49 @@
         for i in list(range(1, ngy)) + [0]:
             if i or j:
                 there = at(0, i, j)
+                slots.append(i * ngz + j)
                 copies.append(send(part.at[there[1], there[2]], got5.at[i * ngz + j], there))
+    phase("p23_wait_top1")
     term = part[b, c]
-    arrive(copies)
-    for k in range(1, plane):
-        term += got5[k]
+    for copy, slot in zip(copies, slots):
+        copy.wait_recv()
+        term += got5[slot]
+    phase("p24_top2")
     s6[...] = term
     copies = [send(s6, got6.at[k], at(k, 0, 0)) for k in range(1, ngx)]
-    arrive(copies)
-    for k in range(1, ngx):
+    arrive(beside)
+    if chips > 1:
+        across = [
+            send(rall.at[before[2], 0:16], rall.at[before[2], 0:16], after),
+            send(rall.at[after[2], 16:32], rall.at[after[2], 16:32], before),
+        ]
+        beside = [send(rall.at[d[2]], rall.at[d[2]], other) for d in (after, before)]
+    for k, copy in enumerate(copies, 1):
+        copy.wait_recv()
         term += got6[k]
+    phase("p25_top3")
     yall[b, c] = term
     copies = [send(yall.at[b, c], yall.at[b, c], there) for _, there in others]
-    arrive(copies)
-
-    total = [jnp.zeros((n3, step), F32) for _ in range(rhs)]
-    for g in range(ngz):
+    if chips > 1:
+        far = lax.rem(c + 4, ngz)
+        arrive(across)
+        beside.append(send(rall.at[far], rall.at[far], other))
+
+    phase("p26_top_back")
+    total_ref[...] = jnp.zeros(total_ref.shape, F32)
+    for k in range(plane):
+        d = lax.rem(me + (plane - k), plane) if k else me
+        r, group = lax.div(d, ngz), lax.rem(d, ngz)
+        if k:
+            copies[k - 1].wait_recv()
+        add = total_ref[r]
         for p in range(0, width, step):
-            block = ti[:, g * width + p : g * width + p + step]
-            for r in range(rhs):
-                total[r] += block * yall[r, g, :, p : p + step]
+            start = group * width + p
+            if step == 128:
+                start = pl.multiple_of(start, 128)
+            add += ti[:, pl.ds(start, step)] * yall[r, group, :, p : p + step]
+        total_ref[r] = add
+    total = [total_ref[r] for r in range(rhs)]
     ones = jnp.ones((8, step), BF16)
     back = jnp.zeros((rhs, n3), F32)
     which = iota((rhs, n3), 0)
@@ -371,16 +435,26 @@
         hi, lo = split(total[r])
         both_sums = dot(ones, hi, BACK) + dot(ones, lo, BACK)
         back += jnp.where(which == r, both_sums[0:rhs], 0.0)
+    phase("p27_down")
     down_send[...] = jnp.zeros((rhs, 128), F32)
     down_send[:, 0:n3] = back
     copies = [send(down_send, down_got, at(1, 0, 0))]
     arrive(copies)
+    phase("p28_gap2")
     z3 = down_send[...] + jnp.where(a > 0, pltpu.roll(down_got[...], n3, 1), 0.0)
 
     gap2[me] = own2 + times(z3, st_pair, BACK)
     copies = [send(gap2.at[me], gap2.at[me], there) for _, there in others]
-    gap_first = own1 + times(z3, (fs_pair[0][:, 128:256], fs_pair[1][:, 128:256]), BACK)
-    arrive(copies)
+    gap1[c] = own1 + times(z3, (fs_pair[0][:, 128:256], fs_pair[1][:, 128:256]), BACK)
+    line = [send(gap1.at[c], gap1.at[c], at(0, 0, k)) for k in range(1, ngz)]
+
+    phase("p29_rows")
+    arrive(beside[1:] if chips == 1 else beside)
+    hi, lo = split(rall[...].reshape(32 * ngz, 128 * groups2))
+    rows = dot(w1_h[64:128, 0 : 32 * ngz], hi) + dot(w1_l[64:128, 0 : 32 * ngz], hi) + dot(w1_h[64:128, 0 : 32 * ngz], lo)
+    hi, lo = split(rows)
+    w2_h[64:128, :] = hi
+    w2_l[64:128, :] = lo
 
     def gathered(ref, members):
         blocks = []
@@ -391,16 +465,17 @@
             blocks.append(block)
         return jnp.concatenate(blocks, axis=1)
 
-    z2 = times(gathered(gap2, plane), w2_pair, BACK)
-
-    gap1[c] = gap_first + times(z2, (fs_pair[0][:, 0:128], fs_pair[1][:, 0:128]), BACK)
-    copies = [send(gap1.at[c], gap1.at[c], at(0, 0, k)) for k in range(1, ngz)]
+    phase("p30_wait_gap")
+    arrive(line)
+    z12 = times(gathered(gap1, ngz), w1_pair, BACK)
     arrive(copies)
-    z1 = times(gathered(gap1, ngz), w1_pair, BACK)
-
-    result = times(jnp.concatenate([s_leaf, z1, z2, z3], axis=1), e_pair, BACK)
+    phase("p31_z_leaf")
+    z12 = z12 + times(gathered(gap2, plane), (w2_h[...], w2_l[...]), BACK)
+
+    result = times(jnp.concatenate([s_leaf, z12, z3], axis=1), e_pair, BACK)
     for j in range(4):
         corr[j] = result[:, 128 * j : 128 * j + 128]
+    phase("p32_rim")
     copies = []
     for i, (dx, dy, dz) in enumerate(RIM):
         there = at(-dx, -dy, -dz)
@@ -409,25 +484,8 @@
         else:
             copies.append(send(corr.at[0], got_corr.at[i, 0], there))
 
-    shape = (fine * fine, 128)
-    row, col = floats(shape, 0), floats(shape, 1)
-    fx = whole_part(row, fine)
-    fy = row - fine * fx
-    half = whole_part(col, 64)
-    rest = col - 64.0 * half
-    cx = whole_part(rest, 8)
-    cy = rest - 8.0 * cx - 1.0
-    spread_xy = (tent(cx - 1.0, fx) * tent(cy, fy) * 0.0625).astype(BF16)
-    shape = (rhs * fine, 8 * rhs)
-    row, col = floats(shape, 0), floats(shape, 1)
-    fr = whole_part(row, fine)
-    fz = row - fine * fr
-    cz = whole_part(col, rhs)
-    cr = col - rhs * cz
-    same = jnp.maximum(1.0 - jnp.abs(cr - fr), 0.0)
-    spread_z = (tent(cz - 1.0, fz) * same * 0.25).astype(BF16)
-
     arrive(copies)
+    phase("p33_prolong")
     total = [corr[j] for j in range(4)]
     for i, (dx, dy, dz) in enumerate(RIM):
         turn = side * 8 * dx + side * dy
@@ -446,7 +504,34 @@
     rows = []
     for j in range(4):
         rows += [total[j][:, 0:64], total[j][:, 64:128]]
-    ct_h, ct_l = split(jnp.concatenate(rows, axis=0))
+    out_h[...] = jnp.concatenate(rows, axis=0)
+    phase("p34_finish")
+    for copy in pending:
+        copy.wait_send()
+    stack.close()
+
+
+def prolong(cfg, ct, out_h, out_v, out_sem):
+    rhs, fine = cfg[3], cfg[4]
+    shape = (fine * fine, 128)
+    row, col = floats(shape, 0), floats(shape, 1)
+    fx = whole_part(row, fine)
+    fy = row - fine * fx
+    half = whole_part(col, 64)
+    rest = col - 64.0 * half
+    cx = whole_part(rest, 8)
+    cy = rest - 8.0 * cx - 1.0
+    spread_xy = (tent(cx - 1.0, fx) * tent(cy, fy) * 0.0625).astype(BF16)
+    shape = (rhs * fine, 8 * rhs)
+    row, col = floats(shape, 0), floats(shape, 1)
+    fr = whole_part(row, fine)
+    fz = row - fine * fr
+    cz = whole_part(col, rhs)
+    cr = col - rhs * cz
+    same = jnp.maximum(1.0 - jnp.abs(cr - fr), 0.0)
+    spread_z = (tent(cz - 1.0, fz) * same * 0.25).astype(BF16)
+
+    ct_h, ct_l = split(ct[...])
     ht = dot(spread_z, ct_h) + dot(spread_z, ct_l)
     ht_h = ht.astype(BF16).astype(F32)
     ht = jnp.concatenate([ht_h, ht - ht_h], axis=1)
@@ -457,8 +542,6 @@
         store = pltpu.make_async_copy(out_v.at[r], out_h.at[r], out_sem.at[r])
         store.start()
         stores.append(store)
-    for copy in pending:
-        copy.wait_send()
     for store in stores:
         store.wait()
 
@@ -467,11 +550,13 @@
     (rs, it, cf, od, li, lf, ls, lt, fi, fs, ft, si, st, ti) = args
     ngx, ngy, ngz = mesh_sizes
     od = od.reshape(1, -1)
-    li, lf, ls, lt, fs, ft, st = (v[0, 0, 0] for v in (li, lf, ls, lt, fs, ft, st))
-    fi, si = fi[0, 0], si[0]
     rhs, fine = rs.shape[0], rs.shape[1]
     side = fine // 4
-    leaf, n1, n2, n3, ntop = li.shape[0], fs.shape[0], st.shape[0], ti.shape[0], ti.shape[1]
+    leaf, n1, n2, n3, ntop = li.shape[3], fs.shape[3], st.shape[3], ti.shape[0], ti.shape[1]
+    li, fs, ft, st = (jnp.transpose(v, (0, 1, 3, 2, 4))[0, 0] for v in (li, fs, ft, st))
+    fi, si = jnp.transpose(fi, (0, 2, 1, 3))[0], jnp.transpose(si, (1, 0, 2))
+    lf, ls = (jnp.transpose(v, (0, 1, 4, 2, 3))[0, 0] for v in (lf, ls))
+    lt = jnp.transpose(lt, (0, 1, 2, 4, 3))[0, 0, 0]
     cfg = (ngx, ngy, ngz, rhs, fine, side, leaf, n1, n2, n3, ntop)
     plane = ngy * ngz
     groups1, groups2 = (ngz + 3) // 4, (plane + 3) // 4
@@ -479,17 +564,18 @@
     inputs = [rs, it, cf, od, li, lf, ls, lt, fi, fs, ft, si, st, ti]
     v = pltpu.VMEM
     width = ntop // ngz
-    copies = len(HALO) + 2 + 3 * (ngz - 1) + 4 * (plane - 1) + 2 + (ngx - 1) + len(RIM)
-    scratch = [v(x.shape, x.dtype) for x in inputs]
+    step = 128 if width % 128 == 0 else width
+    copies = len(HALO) + 2 + 8 + 2 * (ngz - 1) + 4 * (plane - 1) + 2 + (ngx - 1) + len(RIM)
+    narrow = [x.reshape(x.shape[0], -1) if any(x is y for y in (li, lf, ls, fs, ft, st)) else x for x in inputs]
+    scratch = [v(x.shape, x.dtype) for x in narrow]
     scratch += [
-        v(rs.shape, F32),
         v((128, fine * fine), BF16),
-        v((cells, 512), F32), v((512, 512), BF16), v((512, 512), BF16),
+        v((cells, 384), F32), v((512, 384), BF16), v((512, 384), BF16),
         v((32, 256), F32), v((128, 256), BF16), v((128, 256), BF16),
         v((32, 128), F32), v((128, 128), BF16), v((128, 128), BF16),
         v((128, 128 * groups1), F32), v((128, 128 * groups1), BF16), v((128, 128 * groups1), BF16),
-        v((128, 128 * groups2), F32), v((128, 128 * groups2), BF16), v((128, 128 * groups2), BF16),
-        v(fi.shape, F32), v(si.shape, F32),
+        v((64, 128 * groups2), F32), v((128, 128 * groups2), BF16), v((128, 128 * groups2), BF16),
+        v(fi.shape, F32), v(si.shape, F32), v((ngz, 32, 128 * groups2), F32), v((rhs, n3, step), F32),
         v((4, rhs, 128), F32), v((len(FLAT), 4, rhs, 128), F32), v((len(HALO) - len(FLAT), rhs, 128), F32),
         v((groups1, rhs, 128), F32), v((ngz, rhs, 128), F32),
         v((groups2, rhs, 128), F32), v((plane, rhs, 128), F32),
@@ -500,20 +586,29 @@
         v((rhs, 128), F32), v((rhs, 128), F32),
         v((plane, rhs, 128), F32), v((ngz, rhs, 128), F32),
         v((4, rhs, 128), F32), v((len(RIM), 4, rhs, 128), F32),
-        pltpu.SemaphoreType.DMA((len(inputs),)), pltpu.SemaphoreType.DMA((rhs,)),
+        pltpu.SemaphoreType.DMA((len(inputs),)),
         pltpu.SemaphoreType.DMA((copies,)), pltpu.SemaphoreType.DMA((copies,)),
     ]
-    return pl.pallas_call(
+    coarse = pl.pallas_call(
         functools.partial(kernel, cfg),
-        out_shape=jax.ShapeDtypeStruct(rs.shape, F32),
+        out_shape=jax.ShapeDtypeStruct((8 * rhs, 64), F32),
         in_specs=[pl.BlockSpec(memory_space=pl.ANY)] * len(inputs),
-        out_specs=pl.BlockSpec(memory_space=pl.ANY),
+        out_specs=pl.BlockSpec(memory_space=pltpu.VMEM),
         scratch_shapes=scratch,
         compiler_params=pltpu.CompilerParams(
-            collective_id=0, has_side_effects=True, vmem_limit_bytes=48 * 1024 * 1024
+            collective_id=0, has_side_effects=True, vmem_limit_bytes=67043328
         ),
         name="coarse_correction",
     )(*inputs)
+    return pl.pallas_call(
+        functools.partial(prolong, cfg),
+        out_shape=jax.ShapeDtypeStruct(rs.shape, F32),
+        in_specs=[pl.BlockSpec(memory_space=pltpu.VMEM)],
+        out_specs=pl.BlockSpec(memory_space=pl.ANY),
+        scratch_shapes=[v(rs.shape, F32), pltpu.SemaphoreType.DMA((rhs,))],
+        compiler_params=pltpu.CompilerParams(vmem_limit_bytes=67043328),
+        name="prolong",
+    )(coarse)
 
 
 def solution(mesh):

time: 79.5 us -> 61.8 us (0.78)
  local copies, waits for them, and re-layouts: 13.8 us -> 0 us
  Pallas kernels: 65 us -> 61.7 us
    unnamed x20 -> x0, local copies, waits for them, and re-layouts: 13.8 us -> none
    pallas_call x1, Pallas kernels: 65 us -> 59.4 us  [per_device(): pl.pallas_call(functools.partial(kernel, cfg), out_shape=jax.ShapeDtypeSt...]
    pallas_call x0 -> x1, Pallas kernels: none -> 2.21 us  [per_device(): pl.pallas_call(functools.partial(prolong, cfg), out_shape=jax.ShapeDtypeS...]
where the time goes in v2:
time: 61.8 us; the launch traced here: 61.7 us
  Pallas kernels  61.7 us (100%)
    pallas_call x1, Pallas kernels, per_device(): pl.pallas_call(functools.partial(kernel, cfg), out_shape=jax.ShapeDtypeSt...  59.4 us
    pallas_call x1, Pallas kernels, per_device(): pl.pallas_call(functools.partial(prolong, cfg), out_shape=jax.ShapeDtypeS...  2.21 us

profile of v2, /device:TPU:1, one launch (start us, length us, event | category | flops | bytes accessed | tf_op | source)
XLA Modules:
  0.0 61.7 jit_solution(13411399968527051272)
XLA Ops:
  0.0 59.4 %coarse_correction.1.ct = f32[32,64]{1,0:T(8,128)} custom-call(f32[4,24,24,24]{3,2,1,0:T(8,128)} %refs_0_.1, f32[4,24,24,24]{3,2,1,0:T(8,128)} %refs_1_.1, f32[24,24,24]{2,1,0:T(8,128)} %refs_2_.1, s32[1,216]{1,0:T(1,128)} %bitcast.25, f32[125,1,125]{2,1,0:T(1,128)} %bitcast.17, f32[50,1,125]{2,1,0:T(1,128)} %bitcast.20, f32[60,1,125]{2,1,0:T(1,128)} %bitcast.19, ...), custom_call_target="tpu_custom_call" | custom-call | tf_op jit(solution)/shard_map/coarse_correction/pallas_call | solution.py:592
  59.5 2.2 %prolong.1 = f32[4,24,24,24]{3,2,1,0:T(8,128)} custom-call(f32[32,64]{1,0:T(8,128)} %coarse_correction.1.ct), custom_call_target="tpu_custom_call" | custom-call | tf_op jit(solution)/shard_map/prolong/pallas_call | solution.py:603

commit v3 on v2

--- a/solution.py
+++ b/solution.py
@@ -30,9 +30,15 @@
 
 
 def times(value, factor, dims=((1,), (0,))):
-    high, low = split(value)
     f_high, f_low = factor
-    return dot(high, f_high, dims) + dot(low, f_high, dims) + dot(high, f_low, dims)
+    n = value.shape[0]
+    if n > 4:
+        high, low = split(value)
+        return dot(high, f_high, dims) + dot(low, f_high, dims) + dot(high, f_low, dims)
+    high = value.astype(BF16).astype(F32)
+    both = jnp.concatenate([high, value - high], axis=0).astype(BF16)
+    out = dot(both, f_high, dims) + dot(both, f_low, dims)
+    return out[0:n] + out[n : 2 * n]
 
 
 BACK = ((1,), (1,))
@@ -67,15 +73,16 @@
     ngx, ngy, ngz, rhs, fine, side, leaf, n1, n2, n3, ntop = cfg
     plane = ngy * ngz
     cells = side**3
-    (rs_h, it_h, cf_h, or_h, li_h, lf_h, ls_h, lt_h, fi_h, fs_h, ft_h, si_h, st_h, ti_h) = refs[:14]
+    (rs_h, it_h, cf_h, od_h, li_h, lf_h, ls_h, lt_h, fi_h, fs_h, ft_h, si_h, st_h, ti_h) = refs[:14]
     out_h = refs[14]
     (
         rs, it, cf, od, li, lf, ls, lt, fi, fs, ft, si, st, ti,
         a21, bmat, e_h, e_l, fsx, fs_hi, fs_lo, stx, st_hi, st_lo,
-        w1, w1_h, w1_l, w2, w2_h, w2_l, fi_low, si_low, rall, total_ref,
+        stu, ftu, back_hi, back_lo, st_high, ft_high,
+        w1, w1_h, w1_l, w2, w2_h, w2_l, fi_low, si_low, rall, total_ref, r_hi, r_lo,
         flat, got_flat, got_thin, send1, got1, send2, got2, up_send, up_got,
-        part, got5, s6, got6, yall, down_send, down_got, gap2, gap1, corr, got_corr,
-        local_sem, send_sem, recv_sem,
+        part, got5, s6, got6, yall, down_send, down_got, gap2, gap1, low2, low1, corr, got_corr,
+        local_sem, word1, word2, word3, send_sem, recv_sem,
     ) = refs[15:]
 
     a, b, c = (lax.axis_index(n) for n in AXES)
@@ -95,6 +102,9 @@
             lax.rem(b + (dy + ngy), ngy) if dy else b,
             lax.rem(c + (dz + ngz), ngz) if dz else c,
         )
+
+    def far_first(d):
+        return -sum(min(i % n, -i % n) * w for i, n, w in zip(d, (ngx, ngy, ngz), (2, 2, 1))), d
 
     def send(src, dst, device):
         i = used[0]
@@ -116,28 +126,26 @@
             copy.wait_recv()
 
     phase("p00_loads")
+    first = [(cf_h, cf)]
+    for r in range(rhs):
+        first += [(it_h.at[r], it.at[r]), (rs_h.at[r], rs.at[r])]
     pairs = [
-        (it_h, it), (rs_h, rs), (cf_h, cf), (or_h, od), (li_h, li), (lf_h, lf), (ls_h, ls), (lt_h, lt),
-        (fi_h, fi), (si_h, si), (fs_h, fs), (ft_h, ft), (st_h, st), (ti_h, ti),
+        (od_h, od), (li_h, li), (lf_h, lf), (ls_h, ls), (lt_h, lt),
+        (fi_h, fi), (si_h, si), (fs_h, fs), (ft_h, ft), (st_h, st),
     ]
-    pairs = [(s.at[:, 0, :] if len(s.shape) > len(d.shape) else s, d) for s, d in pairs]
+    pairs = first + [(s.at[:, 0, :] if len(s.shape) > len(d.shape) else s, d) for s, d in pairs] + [(ti_h, ti)]
     loads = [pltpu.make_async_copy(s, d, local_sem.at[i]) for i, (s, d) in enumerate(pairs)]
-    for load in loads:
+    for load in loads[:-1]:
         load.start()
 
     phase("p01_signal")
-    partners = set()
-    for dy in range(ngy):
-        for dz in range(ngz):
-            partners.add((0, dy, dz))
-    for dx in range(ngx):
-        partners.add((dx, 0, 0))
+    partners = {(0, 0, dz) for dz in range(ngz)}
     for d in HALO + RIM:
         for s in (1, -1):
             partners.add((s * d[0] % ngx, s * d[1] % ngy, s * d[2] % ngz))
     partners.discard((0, 0, 0))
     barrier = pltpu.get_barrier_semaphore()
-    for d in sorted(partners):
+    for d in sorted(partners, key=far_first):
         pl.semaphore_signal(barrier, inc=1, device_id=at(*d), device_id_type=MESH)
 
     first_x = jnp.where(a == 0, 1.0, 0.0).astype(F32)
@@ -170,20 +178,22 @@
     wvz = wvz.astype(BF16)
 
     phase("p03_wait_residual")
-    for load in loads[:3]:
-        load.wait()
-    g1, g2 = [], []
+    loads[0].wait()
+    diagonal = 6.0 + cf[...]
+    its, qs = [], []
+    for r in range(rhs):
+        loads[2 * r + 1].wait()
+        loads[2 * r + 2].wait()
+        now = it[r]
+        its.append(now.reshape(fine * fine, fine))
+        qs.append((rs[r] - diagonal * now).reshape(fine * fine, fine))
+    i_h, i_l = split(jnp.concatenate(its, axis=1))
+    q_h, q_l = split(jnp.concatenate(qs, axis=1))
     own = a21[64:128, :]
     both = a21[...]
-    for r in range(rhs):
-        now = it[r]
-        q = rs[r] - (6.0 + cf[...]) * now
-        q_h, q_l = split(q.reshape(fine * fine, fine))
-        i_h, i_l = split(now.reshape(fine * fine, fine))
-        from_it = dot(both, i_h) + dot(both, i_l)
-        g1.append(from_it[0:64] + dot(own, q_h) + dot(own, q_l))
-        g2.append(from_it[64:128])
-    g_h, g_l = split(jnp.concatenate(g1 + g2, axis=1))
+    from_it = dot(both, i_h) + dot(both, i_l)
+    g1 = from_it[0:64] + dot(own, q_h) + dot(own, q_l)
+    g_h, g_l = split(jnp.concatenate([g1, from_it[64:128]], axis=1))
     ct = dot(wvz, g_h, BACK) + dot(wvz, g_l, BACK)
     for j in range(4):
         lo = ct[2 * rhs * j : 2 * rhs * j + rhs]
@@ -200,10 +210,18 @@
         else:
             src, dst = flat.at[3 if dz == 1 else 0], got_thin.at[i - len(FLAT)]
         halo_copies.append(send(src, dst, at(dx, dy, dz)))
-    for load in loads[3:]:
+    def tell(sem):
+        for dx in (1, -1):
+            pl.semaphore_signal(sem, inc=1, device_id=at(dx, 0, 0), device_id_type=MESH)
+
+    tell(word1)
+    loads[-1].start()
+    for load in loads[1 + 2 * rhs : -1]:
         load.wait()
     fi_copy = send(fi, fi_low, at(0, 0, 1))
     si_copy = send(si, si_low, at(0, 1, 0))
+    st_copy = send(st, st_high, at(-1, 0, 0))
+    ft_copy = send(ft, ft_high, at(-1, 0, 0))
 
     phase("p07_factor")
     shape = (cells, 384)
@@ -242,8 +260,8 @@
     fs_hi[...] = dot(put1, hi).astype(BF16)
     fs_lo[...] = dot(put1, lo).astype(BF16)
     hi, lo = split(stx[...])
-    st_hi[...] = dot(put2, hi).astype(BF16)
-    st_lo[...] = dot(put2, lo).astype(BF16)
+    st_hi[0:128, :] = dot(put2, hi).astype(BF16)
+    st_lo[0:128, :] = dot(put2, lo).astype(BF16)
 
     groups1 = (ngz + 3) // 4
     groups2 = (plane + 3) // 4
@@ -298,12 +316,17 @@
     s_leaf, s12, s3 = s[:, 0:128], s[:, 128:256], s[:, 256:384]
 
     phase("p13_first_product")
+    word = pl.semaphore_wait
+    word(word1, 2)
+    tell(word2)
+
     w1_pair = (w1_h[...], w1_l[...])
     partial = times(s12, w1_pair)
     for g in range(groups1):
         send1[g] = partial[:, 128 * g : 128 * g + 128]
+    steps = sorted(range(1, ngz), key=lambda k: -min(k, ngz - k))
     copies = []
-    for k in range(1, ngz):
+    for k in steps:
         there = at(0, 0, k)
         copies.append(send(send1.at[there[2] // 4], got1.at[k], there))
     own1 = send1[c // 4]
@@ -323,27 +346,60 @@
     w2_l[0:64, :] = lo
     back_rows = times(fsx[:, 0:64], (hi, lo))
     rall[c] = back_rows
+    rows_h, rows_l = split(back_rows)
+    r_hi[...] = dot(put1, rows_h).astype(BF16)
+    r_lo[...] = dot(put1, rows_l).astype(BF16)
+    partial = times(s12[:, 0:64], (hi, lo))
 
     phase("p16_wait_first")
-    for k, copy in enumerate(copies, 1):
+    for k, copy in reversed(list(zip(steps, copies))):
         copy.wait_recv()
         own1 += got1[k]
     phase("p17_second_product")
     own1 = jnp.where((lane >= place1) & (lane < place1 + n1), own1, 0.0)
-    fs_pair = (fs_hi[...], fs_lo[...])
-    more = times(own1, fs_pair)
-    s2, s3 = s12[:, 0:64] + more[:, 0:64], s3 + more[:, 128:256]
-
-    partial = times(s2, (w2_h[0:64, :], w2_l[0:64, :]))
+    partial = partial + times(own1, (r_hi[...], r_lo[...]))
     for g in range(groups2):
         send2[g] = partial[:, 128 * g : 128 * g + 128]
-    others = []
-    for k in range(1, plane):
-        d = lax.rem(me + k, plane)
-        others.append((d, (a, lax.div(d, ngz), lax.rem(d, ngz))))
-    copies = [send(send2.at[d // 4], got2.at[k], there) for k, (d, there) in enumerate(others, 1)]
+    offsets = [(dy, dz) for dy in range(ngy) for dz in range(ngz) if dy or dz]
+    offsets = sorted(offsets, key=lambda d: far_first((0,) + d))
+    copies, copies_up = [], []
+
+    def group_of(there):
+        return (there[1] * ngz + there[2]) // 4
+
+    for dy, dz in offsets:
+        there = at(-1, dy, dz)
+        copies_up.append(send(send2.at[group_of(there)], got2.at[1, dy * ngz + dz], there))
+    for dy, dz in offsets:
+        there = at(0, dy, dz)
+        copies.append(send(send2.at[group_of(there)], got2.at[0, dy * ngz + dz], there))
+    copies_up.append(send(send2.at[me // 4], got2.at[1, 0], at(-1, 0, 0)))
+    word(word2, 2)
+    tell(word3)
+    own2 = send2[me // 4]
+
+    fs_top = (fs_hi[:, 128:256], fs_lo[:, 128:256])
+    s3 = s3 + times(own1, fs_top)
+    up_send[...] = s3
+    up_copy = send(up_send, up_got, at(-1, 0, 0))
+
     phase("p18_wait_second")
-    own2 = send2[me // 4]
+    stu[...] = jnp.zeros(stu.shape, F32)
+    ftu[...] = jnp.zeros(ftu.shape, F32)
+    st_copy.wait_recv()
+    ft_copy.wait_recv()
+    stu[0:n2, 0:n3] = -st_high[:, n3 : 2 * n3]
+    ftu[0:n1, 0:n3] = -ft_high[:, n3 : 2 * n3]
+    for ref, put, row in ((stu, put2, 128), (ftu, put1, 384)):
+        hi, lo = split(jnp.where(a < ngx - 1, ref[...], 0.0))
+        back_hi[row : row + 128, :] = dot(put, hi).astype(BF16)
+        back_lo[row : row + 128, :] = dot(put, lo).astype(BF16)
+    column = iota((128, 128), 1)
+    for got, src in ((back_hi, (st_hi[0:128, :], fs_top[0])), (back_lo, (st_lo[0:128, :], fs_top[1]))):
+        for row, rows in zip((0, 256), src):
+            got[row : row + 128, :] = jnp.where(column < n3, rows.astype(F32), 0.0).astype(BF16)
+    st_hi[128:256, :] = back_hi[128:256, :]
+    st_lo[128:256, :] = back_lo[128:256, :]
     chips = ngz // 2
     other = (a, b, c + 1 - 2 * lax.rem(c, 2))
     beside = [send(rall.at[c], rall.at[c], other)]
@@ -351,28 +407,29 @@
         after, before = at(0, 0, 2), at(0, 0, -2)
         beside.append(send(rall.at[c], rall.at[c], after))
         beside.append(send(rall.at[c], rall.at[c], before))
-    for k, copy in enumerate(copies, 1):
+    up_copy.wait_recv()
+    copies_up[-1].wait_recv()
+    above = got2[1, 0]
+    target = s3 + jnp.where(a < ngx - 1, pltpu.roll(up_got[...], 128 - n3, 1), 0.0)
+    for (dy, dz), copy, copy_up in reversed(list(zip(offsets, copies, copies_up))):
         copy.wait_recv()
-        own2 += got2[k]
-    phase("p19_second_done")
-    own2 = jnp.where((lane >= place2) & (lane < place2 + n2), own2, 0.0)
-    st_pair = (st_hi[...], st_lo[...])
-    s3 = s3 + times(own2, st_pair)
-
-    phase("p20_up")
-    up_send[...] = s3
-    copies = [send(up_send, up_got, at(-1, 0, 0))]
-    arrive(copies)
+        own2 += got2[0, dy * ngz + dz]
+        copy_up.wait_recv()
+        above += got2[1, dy * ngz + dz]
     phase("p21_target")
-    target = s3 + jnp.where(a < ngx - 1, pltpu.roll(up_got[...], 128 - n3, 1), 0.0)
+    mine = (lane >= place2) & (lane < place2 + n2)
+    own2 = jnp.where(mine, own2, 0.0)
+    above = jnp.where(mine, above, 0.0)
+    target = target + times(jnp.concatenate([own2, above], axis=1), (st_hi[...], st_lo[...]))
     columns = jnp.transpose(jnp.concatenate([target, jnp.zeros((8 - rhs, 128), F32)], axis=0))
     spread = [jnp.broadcast_to(columns[0:n3, r : r + 1], (n3, 128)) for r in range(rhs)]
 
     phase("p22_top_product")
     width = ntop // ngz
     step = 128 if width % 128 == 0 else width
+    loads[-1].wait()
     copies, slots = [], []
-    for j in list(range(1, ngz)) + [0]:
+    for j in steps + [0]:
         group = at(0, 0, j)[2]
         for p in range(0, width, step):
             start = group * width + p
@@ -382,19 +439,22 @@
             for r in range(rhs):
                 scale = spread[r] if step == 128 else jnp.broadcast_to(spread[r][:, 0:1], (n3, step))
                 part[r, group, :, p : p + step] = jnp.sum(scale * block, axis=0, keepdims=True)
-        for i in list(range(1, ngy)) + [0]:
+        for i in sorted(range(ngy), key=lambda i: -min(i, ngy - i)):
             if i or j:
                 there = at(0, i, j)
                 slots.append(i * ngz + j)
                 copies.append(send(part.at[there[1], there[2]], got5.at[i * ngz + j], there))
     phase("p23_wait_top1")
     term = part[b, c]
-    for copy, slot in zip(copies, slots):
+    near = sorted(zip(slots, copies), key=lambda e: far_first((0, e[0] // ngz, e[0] % ngz)), reverse=True)
+    for slot, copy in near:
         copy.wait_recv()
         term += got5[slot]
+    word(word3, 2)
     phase("p24_top2")
     s6[...] = term
-    copies = [send(s6, got6.at[k], at(k, 0, 0)) for k in range(1, ngx)]
+    along_x = sorted(range(1, ngx), key=lambda k: -min(k, ngx - k))
+    copies = [send(s6, got6.at[k], at(k, 0, 0)) for k in along_x]
     arrive(beside)
     if chips > 1:
         across = [
@@ -402,12 +462,12 @@
             send(rall.at[after[2], 16:32], rall.at[after[2], 16:32], before),
         ]
         beside = [send(rall.at[d[2]], rall.at[d[2]], other) for d in (after, before)]
-    for k, copy in enumerate(copies, 1):
+    for k, copy in reversed(list(zip(along_x, copies))):
         copy.wait_recv()
         term += got6[k]
     phase("p25_top3")
     yall[b, c] = term
-    copies = [send(yall.at[b, c], yall.at[b, c], there) for _, there in others]
+    copies = [send(yall.at[b, c], yall.at[b, c], at(0, dy, dz)) for dy, dz in offsets]
     if chips > 1:
         far = lax.rem(c + 4, ngz)
         arrive(across)
@@ -415,11 +475,10 @@
 
     phase("p26_top_back")
     total_ref[...] = jnp.zeros(total_ref.shape, F32)
-    for k in range(plane):
-        d = lax.rem(me + (plane - k), plane) if k else me
-        r, group = lax.div(d, ngz), lax.rem(d, ngz)
-        if k:
-            copies[k - 1].wait_recv()
+    for (dy, dz), copy in [((0, 0), None)] + list(reversed(list(zip(offsets, copies)))):
+        _, r, group = at(0, -dy, -dz)
+        if copy is not None:
+            copy.wait_recv()
         add = total_ref[r]
         for p in range(0, width, step):
             start = group * width + p
@@ -438,15 +497,17 @@
     phase("p27_down")
     down_send[...] = jnp.zeros((rhs, 128), F32)
     down_send[:, 0:n3] = back
-    copies = [send(down_send, down_got, at(1, 0, 0))]
-    arrive(copies)
-    phase("p28_gap2")
-    z3 = down_send[...] + jnp.where(a > 0, pltpu.roll(down_got[...], n3, 1), 0.0)
-
-    gap2[me] = own2 + times(z3, st_pair, BACK)
-    copies = [send(gap2.at[me], gap2.at[me], there) for _, there in others]
-    gap1[c] = own1 + times(z3, (fs_pair[0][:, 128:256], fs_pair[1][:, 128:256]), BACK)
-    line = [send(gap1.at[c], gap1.at[c], at(0, 0, k)) for k in range(1, ngz)]
+    right_sides = times(down_send[...], (back_hi[...], back_lo[...]), BACK)
+    gap2[0, me] = own2 + right_sides[:, 0:128]
+    low2[...] = right_sides[:, 128:256]
+    gap1[0, c] = own1 + right_sides[:, 256:384]
+    low1[...] = right_sides[:, 384:512]
+    copies = [send(low2, gap2.at[1, me], at(1, dy, dz)) for dy, dz in offsets]
+    copies += [send(gap2.at[0, me], gap2.at[0, me], at(0, dy, dz)) for dy, dz in offsets]
+    copies.append(send(low2, gap2.at[1, me], at(1, 0, 0)))
+    line = [send(low1, gap1.at[1, c], at(1, 0, k)) for k in steps + [0]]
+    line += [send(gap1.at[0, c], gap1.at[0, c], at(0, 0, k)) for k in steps]
+    down_copy = send(down_send, down_got, at(1, 0, 0))
 
     phase("p29_rows")
     arrive(beside[1:] if chips == 1 else beside)
@@ -459,20 +520,24 @@
     def gathered(ref, members):
         blocks = []
         for g in range((members + 3) // 4):
-            block = ref[4 * g]
+            own_part, lower_part = ref[0, 4 * g], ref[1, 4 * g]
             for i in range(4 * g + 1, min(4 * g + 4, members)):
-                block += ref[i]
-            blocks.append(block)
+                own_part += ref[0, i]
+                lower_part += ref[1, i]
+            blocks.append(own_part + jnp.where(a > 0, lower_part, 0.0))
         return jnp.concatenate(blocks, axis=1)
 
     phase("p30_wait_gap")
+    arrive([down_copy])
+    z3 = down_send[...] + jnp.where(a > 0, pltpu.roll(down_got[...], n3, 1), 0.0)
+    corr_part = times(jnp.concatenate([s_leaf, z3], axis=1), tuple(jnp.concatenate([e[:, 0:128], e[:, 256:384]], axis=1) for e in e_pair), BACK)
     arrive(line)
     z12 = times(gathered(gap1, ngz), w1_pair, BACK)
     arrive(copies)
     phase("p31_z_leaf")
     z12 = z12 + times(gathered(gap2, plane), (w2_h[...], w2_l[...]), BACK)
 
-    result = times(jnp.concatenate([s_leaf, z12, z3], axis=1), e_pair, BACK)
+    result = corr_part + times(z12, (e_h[:, 128:256], e_l[:, 128:256]), BACK)
     for j in range(4):
         corr[j] = result[:, 128 * j : 128 * j + 128]
     phase("p32_rim")
@@ -565,28 +630,31 @@
     v = pltpu.VMEM
     width = ntop // ngz
     step = 128 if width % 128 == 0 else width
-    copies = len(HALO) + 2 + 8 + 2 * (ngz - 1) + 4 * (plane - 1) + 2 + (ngx - 1) + len(RIM)
+    copies = len(HALO) + 4 + 8 + 3 * ngz - 2 + 6 * plane - 4 + 2 + (ngx - 1) + len(RIM)
     narrow = [x.reshape(x.shape[0], -1) if any(x is y for y in (li, lf, ls, fs, ft, st)) else x for x in inputs]
     scratch = [v(x.shape, x.dtype) for x in narrow]
     scratch += [
         v((128, fine * fine), BF16),
         v((cells, 384), F32), v((512, 384), BF16), v((512, 384), BF16),
         v((32, 256), F32), v((128, 256), BF16), v((128, 256), BF16),
-        v((32, 128), F32), v((128, 128), BF16), v((128, 128), BF16),
+        v((32, 128), F32), v((256, 128), BF16), v((256, 128), BF16),
+        v((32, 128), F32), v((32, 128), F32), v((512, 128), BF16), v((512, 128), BF16), v(st.shape[::2], F32), v(ft.shape[::2], F32),
         v((128, 128 * groups1), F32), v((128, 128 * groups1), BF16), v((128, 128 * groups1), BF16),
         v((64, 128 * groups2), F32), v((128, 128 * groups2), BF16), v((128, 128 * groups2), BF16),
         v(fi.shape, F32), v(si.shape, F32), v((ngz, 32, 128 * groups2), F32), v((rhs, n3, step), F32),
+        v((128, 128 * groups2), BF16), v((128, 128 * groups2), BF16),
         v((4, rhs, 128), F32), v((len(FLAT), 4, rhs, 128), F32), v((len(HALO) - len(FLAT), rhs, 128), F32),
         v((groups1, rhs, 128), F32), v((ngz, rhs, 128), F32),
-        v((groups2, rhs, 128), F32), v((plane, rhs, 128), F32),
+        v((groups2, rhs, 128), F32), v((2, plane, rhs, 128), F32),
         v((rhs, 128), F32), v((rhs, 128), F32),
         v((rhs, ngz, 1, width), F32), v((plane, 1, width), F32),
         v((1, width), F32), v((ngx, 1, width), F32),
         v((rhs, ngz, 1, width), F32),
         v((rhs, 128), F32), v((rhs, 128), F32),
-        v((plane, rhs, 128), F32), v((ngz, rhs, 128), F32),
+        v((2, plane, rhs, 128), F32), v((2, ngz, rhs, 128), F32), v((rhs, 128), F32), v((rhs, 128), F32),
         v((4, rhs, 128), F32), v((len(RIM), 4, rhs, 128), F32),
-        pltpu.SemaphoreType.DMA((len(inputs),)),
+        pltpu.SemaphoreType.DMA((len(inputs) + 2 * rhs - 2,)),
+        *[pltpu.SemaphoreType.REGULAR] * 3,
         pltpu.SemaphoreType.DMA((copies,)), pltpu.SemaphoreType.DMA((copies,)),
     ]
     coarse = pl.pallas_call(

time: 61.8 us -> 58 us (0.939)
  Pallas kernels: 61.7 us -> 57.8 us
    pallas_call x1, Pallas kernels: 59.4 us -> 55.6 us  [per_device(): pl.pallas_call(functools.partial(kernel, cfg), out_shape=jax.ShapeDtypeSt...]
where the time goes in v3:
time: 58 us; the launch traced here: 57.8 us
  Pallas kernels  57.8 us (100%)
    pallas_call x1, Pallas kernels, per_device(): pl.pallas_call(functools.partial(kernel, cfg), out_shape=jax.ShapeDtypeSt...  55.6 us
    pallas_call x1, Pallas kernels, per_device(): pl.pallas_call(functools.partial(prolong, cfg), out_shape=jax.ShapeDtypeS...  2.21 us

profile of v3, /device:TPU:1, one launch (start us, length us, event | category | flops | bytes accessed | tf_op | source)
XLA Modules:
  0.0 57.8 jit_solution(13543505333849745272)
XLA Ops:
  0.0 55.6 %coarse_correction.1.ct = f32[32,64]{1,0:T(8,128)} custom-call(f32[4,24,24,24]{3,2,1,0:T(8,128)} %refs_0_.1, f32[4,24,24,24]{3,2,1,0:T(8,128)} %refs_1_.1, f32[24,24,24]{2,1,0:T(8,128)} %refs_2_.1, s32[1,216]{1,0:T(1,128)} %bitcast.25, f32[125,1,125]{2,1,0:T(1,128)} %bitcast.17, f32[50,1,125]{2,1,0:T(1,128)} %bitcast.20, f32[60,1,125]{2,1,0:T(1,128)} %bitcast.19, ...), custom_call_target="tpu_custom_call" | custom-call | tf_op jit(solution)/shard_map/coarse_correction/pallas_call | solution.py:660
  55.6 2.2 %prolong.1 = f32[4,24,24,24]{3,2,1,0:T(8,128)} custom-call(f32[32,64]{1,0:T(8,128)} %coarse_correction.1.ct), custom_call_target="tpu_custom_call" | custom-call | tf_op jit(solution)/shard_map/prolong/pallas_call | solution.py:671

commit v4 on v3

--- a/solution.py
+++ b/solution.py
@@ -77,9 +77,9 @@
     out_h = refs[14]
     (
         rs, it, cf, od, li, lf, ls, lt, fi, fs, ft, si, st, ti,
-        a21, bmat, e_h, e_l, fsx, fs_hi, fs_lo, stx, st_hi, st_lo,
+        pack_it, pack_q, a21, bmat, e_h, e_l, fsx, fs_hi, fs_lo, stx, st_hi, st_lo,
         stu, ftu, back_hi, back_lo, st_high, ft_high,
-        w1, w1_h, w1_l, w2, w2_h, w2_l, fi_low, si_low, rall, total_ref, r_hi, r_lo,
+        w1, w1_h, w1_l, w2, w2_h, w2_l, fi_low, si_low, rall, r_hi, r_lo,
         flat, got_flat, got_thin, send1, got1, send2, got2, up_send, up_got,
         part, got5, s6, got6, yall, down_send, down_got, gap2, gap1, low2, low1, corr, got_corr,
         local_sem, word1, word2, word3, send_sem, recv_sem,
@@ -96,12 +96,21 @@
         stack.enter_context(jax.named_scope(name))
 
 
+    known = {}
+
+    def step_along(name, here, by, n):
+        by %= n
+        if (name, by) not in known:
+            known[name, by] = lax.rem(here + by, n) if by else here
+        return known[name, by]
+
     def at(dx, dy, dz):
-        return (
-            lax.rem(a + (dx + ngx), ngx) if dx else a,
-            lax.rem(b + (dy + ngy), ngy) if dy else b,
-            lax.rem(c + (dz + ngz), ngz) if dz else c,
-        )
+        return step_along("x", a, dx, ngx), step_along("y", b, dy, ngy), step_along("z", c, dz, ngz)
+
+    def quarter(dz):
+        if ("q", dz % ngz) not in known:
+            known["q", dz % ngz] = lax.div(step_along("z", c, dz, ngz), 4)
+        return known["q", dz % ngz]
 
     def far_first(d):
         return -sum(min(i % n, -i % n) * w for i, n, w in zip(d, (ngx, ngy, ngz), (2, 2, 1))), d
@@ -121,14 +130,21 @@
         pending.append(copy)
         return copy
 
+    def drain():
+        for copy in pending:
+            copy.wait_send()
+        pending.clear()
+
     def arrive(copies):
         for copy in copies:
             copy.wait_recv()
 
     phase("p00_loads")
     first = [(cf_h, cf)]
+    half = fine // 2
     for r in range(rhs):
-        first += [(it_h.at[r], it.at[r]), (rs_h.at[r], rs.at[r])]
+        for h in (0, half):
+            first += [(x.at[r, h : h + half], y.at[r, h : h + half]) for x, y in ((it_h, it), (rs_h, rs))]
     pairs = [
         (od_h, od), (li_h, li), (lf_h, lf), (ls_h, ls), (lt_h, lt),
         (fi_h, fi), (si_h, si), (fs_h, fs), (ft_h, ft), (st_h, st),
@@ -180,15 +196,15 @@
     phase("p03_wait_residual")
     loads[0].wait()
     diagonal = 6.0 + cf[...]
-    its, qs = [], []
     for r in range(rhs):
-        loads[2 * r + 1].wait()
-        loads[2 * r + 2].wait()
+        for load in loads[4 * r + 1 : 4 * r + 5]:
+            load.wait()
         now = it[r]
-        its.append(now.reshape(fine * fine, fine))
-        qs.append((rs[r] - diagonal * now).reshape(fine * fine, fine))
-    i_h, i_l = split(jnp.concatenate(its, axis=1))
-    q_h, q_l = split(jnp.concatenate(qs, axis=1))
+        at_r = slice(fine * r, fine * r + fine)
+        pack_it[:, at_r] = now.reshape(fine * fine, fine)
+        pack_q[:, at_r] = (rs[r] - diagonal * now).reshape(fine * fine, fine)
+    i_h, i_l = split(pack_it[...])
+    q_h, q_l = split(pack_q[...])
     own = a21[64:128, :]
     both = a21[...]
     from_it = dot(both, i_h) + dot(both, i_l)
@@ -204,7 +220,8 @@
     pl.semaphore_wait(barrier, len(partners))
 
     halo_copies = []
-    for i, (dx, dy, dz) in enumerate(HALO):
+    halo = sorted(enumerate(HALO), key=lambda e: far_first(e[1]))
+    for i, (dx, dy, dz) in halo:
         if dz == 0:
             src, dst = flat, got_flat.at[i]
         else:
@@ -216,7 +233,7 @@
 
     tell(word1)
     loads[-1].start()
-    for load in loads[1 + 2 * rhs : -1]:
+    for load in loads[1 + 4 * rhs : -1]:
         load.wait()
     fi_copy = send(fi, fi_low, at(0, 0, 1))
     si_copy = send(si, si_low, at(0, 1, 0))
@@ -277,9 +294,11 @@
     hi, lo = split(w1[...])
     w1_h[...] = hi
     w1_l[...] = lo
+    e_mid = (e_h[:, 128:256], e_l[:, 128:256])
+    lead = dot(e_mid[0], hi) + dot(e_mid[1], hi) + dot(e_mid[0], lo)
+    lead_pair = split(lead)
 
     phase("p10_wait_halo")
-    arrive(halo_copies)
     phase("p11_add_halo")
     lane = iota((rhs, 128), 1)
     at_z, at_x, at_y = lane >> 6, (lane >> 3) & 7, lane & 7
@@ -293,7 +312,8 @@
         return (i - d >= 0) & (i - d < n) if d else True
 
     total = [flat[j] for j in range(4)]
-    for i, (dx, dy, dz) in enumerate(HALO):
+    for (i, (dx, dy, dz)), copy in reversed(list(zip(halo, halo_copies))):
+        copy.wait_recv()
         turn = (-(side * 8) * dx - side * dy) % 128
         keep = along(at_x, dx) & along(at_y, dy)
         there = exists(a, dx, ngx) & exists(b, dy, ngy) & exists(c, dz, ngz)
@@ -311,25 +331,23 @@
             total[j] += jnp.where(keep, v, 0.0)
 
     phase("p12_leaf")
-    e_pair = (e_h[...], e_l[...])
-    s = times(jnp.concatenate(total, axis=1), e_pair)
-    s_leaf, s12, s3 = s[:, 0:128], s[:, 128:256], s[:, 256:384]
-
-    phase("p13_first_product")
-    word = pl.semaphore_wait
-    word(word1, 2)
-    tell(word2)
-
-    w1_pair = (w1_h[...], w1_l[...])
-    partial = times(s12, w1_pair)
+    gathered_cells = jnp.concatenate(total, axis=1)
+    partial = times(gathered_cells, lead_pair)
     for g in range(groups1):
         send1[g] = partial[:, 128 * g : 128 * g + 128]
     steps = sorted(range(1, ngz), key=lambda k: -min(k, ngz - k))
     copies = []
     for k in steps:
         there = at(0, 0, k)
-        copies.append(send(send1.at[there[2] // 4], got1.at[k], there))
-    own1 = send1[c // 4]
+        copies.append(send(send1.at[quarter(k)], got1.at[k], there))
+    own1 = send1[quarter(0)]
+    word = pl.semaphore_wait
+    word(word1, 2)
+    tell(word2)
+    e_pair = (e_h[...], e_l[...])
+    s = times(gathered_cells, e_pair)
+    s_leaf, s12, s3 = s[:, 0:128], s[:, 128:256], s[:, 256:384]
+    w1_pair = (w1_h[...], w1_l[...])
 
     phase("p15_w2")
     si_copy.wait_recv()
@@ -364,15 +382,17 @@
     offsets = sorted(offsets, key=lambda d: far_first((0,) + d))
     copies, copies_up = [], []
 
-    def group_of(there):
-        return (there[1] * ngz + there[2]) // 4
+    def group_of(dy, dz):
+        if ngz % 4:
+            return lax.div(step_along("y", b, dy, ngy) * ngz + step_along("z", c, dz, ngz), 4)
+        return step_along("y", b, dy, ngy) * (ngz // 4) + quarter(dz)
 
     for dy, dz in offsets:
         there = at(-1, dy, dz)
-        copies_up.append(send(send2.at[group_of(there)], got2.at[1, dy * ngz + dz], there))
+        copies_up.append(send(send2.at[group_of(dy, dz)], got2.at[1, dy * ngz + dz], there))
     for dy, dz in offsets:
         there = at(0, dy, dz)
-        copies.append(send(send2.at[group_of(there)], got2.at[0, dy * ngz + dz], there))
+        copies.append(send(send2.at[group_of(dy, dz)], got2.at[0, dy * ngz + dz], there))
     copies_up.append(send(send2.at[me // 4], got2.at[1, 0], at(-1, 0, 0)))
     word(word2, 2)
     tell(word3)
@@ -474,19 +494,20 @@
         beside.append(send(rall.at[far], rall.at[far], other))
 
     phase("p26_top_back")
-    total_ref[...] = jnp.zeros(total_ref.shape, F32)
-    for (dy, dz), copy in [((0, 0), None)] + list(reversed(list(zip(offsets, copies)))):
-        _, r, group = at(0, -dy, -dz)
-        if copy is not None:
-            copy.wait_recv()
-        add = total_ref[r]
+    arrivals = dict(zip(offsets, copies))
+    total = [jnp.zeros((n3, step), F32) for _ in range(rhs)]
+    for dz in [0] + list(reversed(steps)):
+        group = step_along("z", c, -dz, ngz)
+        for dy in sorted(range(ngy), key=lambda i: min(i, ngy - i)):
+            if dy or dz:
+                arrivals[dy, dz].wait_recv()
         for p in range(0, width, step):
             start = group * width + p
             if step == 128:
                 start = pl.multiple_of(start, 128)
-            add += ti[:, pl.ds(start, step)] * yall[r, group, :, p : p + step]
-        total_ref[r] = add
-    total = [total_ref[r] for r in range(rhs)]
+            block = ti[:, pl.ds(start, step)]
+            for r in range(rhs):
+                total[r] += block * yall[r, group, :, p : p + step]
     ones = jnp.ones((8, step), BF16)
     back = jnp.zeros((rhs, n3), F32)
     which = iota((rhs, n3), 0)
@@ -527,6 +548,7 @@
             blocks.append(own_part + jnp.where(a > 0, lower_part, 0.0))
         return jnp.concatenate(blocks, axis=1)
 
+    drain()
     phase("p30_wait_gap")
     arrive([down_copy])
     z3 = down_send[...] + jnp.where(a > 0, pltpu.roll(down_got[...], n3, 1), 0.0)
@@ -542,17 +564,17 @@
         corr[j] = result[:, 128 * j : 128 * j + 128]
     phase("p32_rim")
     copies = []
-    for i, (dx, dy, dz) in enumerate(RIM):
+    rim = sorted(enumerate(RIM), key=lambda e: far_first(e[1]))
+    for i, (dx, dy, dz) in rim:
         there = at(-dx, -dy, -dz)
         if dz == 0:
             copies.append(send(corr, got_corr.at[i], there))
         else:
             copies.append(send(corr.at[0], got_corr.at[i, 0], there))
 
-    arrive(copies)
-    phase("p33_prolong")
     total = [corr[j] for j in range(4)]
-    for i, (dx, dy, dz) in enumerate(RIM):
+    for (i, (dx, dy, dz)), copy in reversed(list(zip(rim, copies))):
+        copy.wait_recv()
         turn = side * 8 * dx + side * dy
         keep = (at_x == side + 1) if dx else (at_x <= side)
         keep = keep & ((at_y == side + 1) if dy else (at_y <= side))
@@ -571,22 +593,23 @@
         rows += [total[j][:, 0:64], total[j][:, 64:128]]
     out_h[...] = jnp.concatenate(rows, axis=0)
     phase("p34_finish")
-    for copy in pending:
-        copy.wait_send()
+    drain()
     stack.close()
 
 
-def prolong(cfg, ct, out_h, out_v, out_sem):
+def prolong(cfg, ct_h, out_h, ct, out_v, in_sem, out_sem):
     rhs, fine = cfg[3], cfg[4]
-    shape = (fine * fine, 128)
-    row, col = floats(shape, 0), floats(shape, 1)
-    fx = whole_part(row, fine)
-    fy = row - fine * fx
-    half = whole_part(col, 64)
-    rest = col - 64.0 * half
+    load = pltpu.make_async_copy(ct_h, ct, in_sem)
+    load.start()
+    stack = contextlib.ExitStack()
+    stack.enter_context(jax.named_scope("q0"))
+    shape = (fine, 128)
+    fx, col = floats(shape, 0), floats(shape, 1)
+    rest = col - 64.0 * whole_part(col, 64)
     cx = whole_part(rest, 8)
-    cy = rest - 8.0 * cx - 1.0
-    spread_xy = (tent(cx - 1.0, fx) * tent(cy, fy) * 0.0625).astype(BF16)
+    along_x = tent(cx - 1.0, fx) * 0.25
+    along_y = tent(rest - 8.0 * cx - 1.0, fx) * 0.25
+    spread_xy = (along_x[:, None, :] * along_y[None, :, :]).reshape(fine * fine, 128).astype(BF16)
     shape = (rhs * fine, 8 * rhs)
     row, col = floats(shape, 0), floats(shape, 1)
     fr = whole_part(row, fine)
@@ -596,10 +619,17 @@
     same = jnp.maximum(1.0 - jnp.abs(cr - fr), 0.0)
     spread_z = (tent(cz - 1.0, fz) * same * 0.25).astype(BF16)
 
+    stack.close()
+    stack.enter_context(jax.named_scope("q1"))
+    load.wait()
+    stack.close()
+    stack.enter_context(jax.named_scope("q2"))
     ct_h, ct_l = split(ct[...])
     ht = dot(spread_z, ct_h) + dot(spread_z, ct_l)
     ht_h = ht.astype(BF16).astype(F32)
     ht = jnp.concatenate([ht_h, ht - ht_h], axis=1)
+    stack.close()
+    stack.enter_context(jax.named_scope("q3"))
     stores = []
     for r in range(rhs):
         part_r = ht[r * fine : (r + 1) * fine].astype(BF16)
@@ -607,8 +637,11 @@
         store = pltpu.make_async_copy(out_v.at[r], out_h.at[r], out_sem.at[r])
         store.start()
         stores.append(store)
+    stack.close()
+    stack.enter_context(jax.named_scope("q4"))
     for store in stores:
         store.wait()
+    stack.close()
 
 
 def per_device(mesh_sizes, *args):
@@ -634,14 +667,14 @@
     narrow = [x.reshape(x.shape[0], -1) if any(x is y for y in (li, lf, ls, fs, ft, st)) else x for x in inputs]
     scratch = [v(x.shape, x.dtype) for x in narrow]
     scratch += [
-        v((128, fine * fine), BF16),
+        v((fine * fine, rhs * fine), F32), v((fine * fine, rhs * fine), F32), v((128, fine * fine), BF16),
         v((cells, 384), F32), v((512, 384), BF16), v((512, 384), BF16),
         v((32, 256), F32), v((128, 256), BF16), v((128, 256), BF16),
         v((32, 128), F32), v((256, 128), BF16), v((256, 128), BF16),
         v((32, 128), F32), v((32, 128), F32), v((512, 128), BF16), v((512, 128), BF16), v(st.shape[::2], F32), v(ft.shape[::2], F32),
         v((128, 128 * groups1), F32), v((128, 128 * groups1), BF16), v((128, 128 * groups1), BF16),
         v((64, 128 * groups2), F32), v((128, 128 * groups2), BF16), v((128, 128 * groups2), BF16),
-        v(fi.shape, F32), v(si.shape, F32), v((ngz, 32, 128 * groups2), F32), v((rhs, n3, step), F32),
+        v(fi.shape, F32), v(si.shape, F32), v((ngz, 32, 128 * groups2), F32),
         v((128, 128 * groups2), BF16), v((128, 128 * groups2), BF16),
         v((4, rhs, 128), F32), v((len(FLAT), 4, rhs, 128), F32), v((len(HALO) - len(FLAT), rhs, 128), F32),
         v((groups1, rhs, 128), F32), v((ngz, rhs, 128), F32),
@@ -653,7 +686,7 @@
         v((rhs, 128), F32), v((rhs, 128), F32),
         v((2, plane, rhs, 128), F32), v((2, ngz, rhs, 128), F32), v((rhs, 128), F32), v((rhs, 128), F32),
         v((4, rhs, 128), F32), v((len(RIM), 4, rhs, 128), F32),
-        pltpu.SemaphoreType.DMA((len(inputs) + 2 * rhs - 2,)),
+        pltpu.SemaphoreType.DMA((len(inputs) + 4 * rhs - 2,)),
         *[pltpu.SemaphoreType.REGULAR] * 3,
         pltpu.SemaphoreType.DMA((copies,)), pltpu.SemaphoreType.DMA((copies,)),
     ]
@@ -671,9 +704,9 @@
     return pl.pallas_call(
         functools.partial(prolong, cfg),
         out_shape=jax.ShapeDtypeStruct(rs.shape, F32),
-        in_specs=[pl.BlockSpec(memory_space=pltpu.VMEM)],
+        in_specs=[pl.BlockSpec(memory_space=pl.ANY)],
         out_specs=pl.BlockSpec(memory_space=pl.ANY),
-        scratch_shapes=[v(rs.shape, F32), pltpu.SemaphoreType.DMA((rhs,))],
+        scratch_shapes=[v((8 * rhs, 64), F32), v(rs.shape, F32), pltpu.SemaphoreType.DMA, pltpu.SemaphoreType.DMA((rhs,))],
         compiler_params=pltpu.CompilerParams(vmem_limit_bytes=67043328),
         name="prolong",
     )(coarse)

time: 58 us -> 57.5 us (level)
  no operation moved by 1% of the time
where the time goes in v4:
time: 57.5 us; the launch traced here: 57.3 us
  Pallas kernels  57.3 us (100%)
    pallas_call x1, Pallas kernels, per_device(): pl.pallas_call(functools.partial(kernel, cfg), out_shape=jax.ShapeDtypeSt...  55.2 us
    pallas_call x1, Pallas kernels, per_device(): pl.pallas_call(functools.partial(prolong, cfg), out_shape=jax.ShapeDtypeS...  2.17 us

profile of v4, /device:TPU:1, one launch (start us, length us, event | category | flops | bytes accessed | tf_op | source)
XLA Modules:
  0.0 57.3 jit_solution(888532183121128630)
XLA Ops:
  0.0 55.2 %coarse_correction.1.ct_h = f32[32,64]{1,0:T(8,128)} custom-call(f32[4,24,24,24]{3,2,1,0:T(8,128)} %refs_0_.1, f32[4,24,24,24]{3,2,1,0:T(8,128)} %refs_1_.1, f32[24,24,24]{2,1,0:T(8,128)} %refs_2_.1, s32[1,216]{1,0:T(1,128)} %bitcast.25, f32[125,1,125]{2,1,0:T(1,128)} %bitcast.17, f32[50,1,125]{2,1,0:T(1,128)} %bitcast.20, f32[60,1,125]{2,1,0:T(1,128)} %bitcast.19, ...), custom_call_target="tpu_custom_call" | custom-call | tf_op jit(solution)/shard_map/coarse_correction/pallas_call | solution.py:693
  55.2 2.2 %prolong.1 = f32[4,24,24,24]{3,2,1,0:T(8,128)} custom-call(f32[32,64]{1,0:T(8,128)} %coarse_correction.1.ct_h), custom_call_target="tpu_custom_call" | custom-call | tf_op jit(solution)/shard_map/prolong/pallas_call | solution.py:704

commit v5 on v4

--- a/solution.py
+++ b/solution.py
@@ -18,6 +18,11 @@
 BELOW = ((0, 0), (1, 0), (0, 1), (1, 1))
 HALO = [(x, y, 0) for x, y in FLAT] + [(x, y, 1) for x, y in ABOVE] + [(x, y, -1) for x, y in BELOW]
 RIM = [(1, 0, 0), (0, 1, 0), (1, 1, 0), (0, 0, 1), (1, 0, 1), (0, 1, 1), (1, 1, 1)]
+
+(
+    HALO_G, FI_G, SI_G, ST_G, FT_G, FIRST_G, SECOND_G, UP_G, ROWS_G, ACROSS_G, CORE_G,
+    TERM_G, LINE_G, GAP_G, FIRST_GAP_G, DOWN_G, RIM_G, SPREAD_G,
+) = range(18)
 
 
 def split(value):
@@ -80,15 +85,13 @@
         pack_it, pack_q, a21, bmat, e_h, e_l, fsx, fs_hi, fs_lo, stx, st_hi, st_lo,
         stu, ftu, back_hi, back_lo, st_high, ft_high,
         w1, w1_h, w1_l, w2, w2_h, w2_l, fi_low, si_low, rall, r_hi, r_lo,
-        flat, got_flat, got_thin, send1, got1, send2, got2, up_send, up_got,
+        flat, got_halo, send1, got1, send2, got2, up_send, up_got,
         part, got5, s6, got6, yall, down_send, down_got, gap2, gap1, low2, low1, corr, got_corr,
-        local_sem, word1, word2, word3, send_sem, recv_sem,
+        local_sem, word1, word2, word3, go, send_sem, recv_sem,
     ) = refs[15:]
 
     a, b, c = (lax.axis_index(n) for n in AXES)
     me = b * ngz + c
-    used = [0]
-    pending = []
     stack = contextlib.ExitStack()
 
     def phase(name):
@@ -112,45 +115,50 @@
             known["q", dz % ngz] = lax.div(step_along("z", c, dz, ngz), 4)
         return known["q", dz % ngz]
 
+    for n, here, size in (("x", a, ngx), ("y", b, ngy), ("z", c, ngz)):
+        for by in range(size):
+            step_along(n, here, by, size)
+    for dz in range(ngz):
+        quarter(dz)
+    chips = ngz // 2
+    chip, core = lax.div(c, 2), lax.rem(c, 2)
+    chip_at = [lax.rem(chip + j, chips) if j else chip for j in range(chips)]
+    keeper = core == 1
+    other = (a, b, c + 1 - 2 * core)
+
     def far_first(d):
         return -sum(min(i % n, -i % n) * w for i, n, w in zip(d, (ngx, ngy, ngz), (2, 2, 1))), d
 
-    def send(src, dst, device):
-        i = used[0]
-        used[0] += 1
-        copy = pltpu.make_async_remote_copy(
+    def copy_of(src, dst, device, group, into=None):
+        return pltpu.make_async_remote_copy(
             src_ref=src,
             dst_ref=dst,
-            send_sem=send_sem.at[i],
-            recv_sem=recv_sem.at[i],
+            send_sem=send_sem.at[group],
+            recv_sem=recv_sem.at[group if into is None else into],
             device_id=device,
             device_id_type=MESH,
         )
-        copy.start()
-        pending.append(copy)
-        return copy
-
-    def drain():
-        for copy in pending:
-            copy.wait_send()
-        pending.clear()
-
-    def arrive(copies):
-        for copy in copies:
-            copy.wait_recv()
+
+    def send(src, dst, device, group, into=None):
+        copy_of(src, dst, device, group, into).start()
+
+    def arrived(group, ref):
+        copy_of(ref, ref, other, group).wait_recv()
+
+    def sent(group, ref):
+        copy_of(ref, ref, other, group).wait_send()
 
     phase("p00_loads")
     first = [(cf_h, cf)]
-    half = fine // 2
     for r in range(rhs):
-        for h in (0, half):
-            first += [(x.at[r, h : h + half], y.at[r, h : h + half]) for x, y in ((it_h, it), (rs_h, rs))]
+        first += [(it_h.at[r], it.at[r]), (rs_h.at[r], rs.at[r])]
     pairs = [
         (od_h, od), (li_h, li), (lf_h, lf), (ls_h, ls), (lt_h, lt),
         (fi_h, fi), (si_h, si), (fs_h, fs), (ft_h, ft), (st_h, st),
     ]
     pairs = first + [(s.at[:, 0, :] if len(s.shape) > len(d.shape) else s, d) for s, d in pairs] + [(ti_h, ti)]
-    loads = [pltpu.make_async_copy(s, d, local_sem.at[i]) for i, (s, d) in enumerate(pairs)]
+    spots = [0] + [1 + i // 2 for i in range(2 * rhs)] + list(range(1 + rhs, len(pairs) - rhs))
+    loads = [pltpu.make_async_copy(s, d, local_sem.at[i]) for i, (s, d) in zip(spots, pairs)]
     for load in loads[:-1]:
         load.start()
 
@@ -197,8 +205,7 @@
     loads[0].wait()
     diagonal = 6.0 + cf[...]
     for r in range(rhs):
-        for load in loads[4 * r + 1 : 4 * r + 5]:
-            load.wait()
+        pltpu.make_async_copy(it_h.at[0:2], it.at[0:2], local_sem.at[1 + r]).wait()
         now = it[r]
         at_r = slice(fine * r, fine * r + fine)
         pack_it[:, at_r] = now.reshape(fine * fine, fine)
@@ -219,26 +226,27 @@
     phase("p05_barrier")
     pl.semaphore_wait(barrier, len(partners))
 
-    halo_copies = []
     halo = sorted(enumerate(HALO), key=lambda e: far_first(e[1]))
+    thin = 4 * len(FLAT)
     for i, (dx, dy, dz) in halo:
         if dz == 0:
-            src, dst = flat, got_flat.at[i]
+            send(flat, got_halo.at[4 * i : 4 * i + 4], at(dx, dy, dz), HALO_G)
         else:
-            src, dst = flat.at[3 if dz == 1 else 0], got_thin.at[i - len(FLAT)]
-        halo_copies.append(send(src, dst, at(dx, dy, dz)))
+            src = flat.at[3 if dz == 1 else 0]
+            send(src, got_halo.at[thin + i - len(FLAT)], at(dx, dy, dz), HALO_G)
+
     def tell(sem):
         for dx in (1, -1):
             pl.semaphore_signal(sem, inc=1, device_id=at(dx, 0, 0), device_id_type=MESH)
 
     tell(word1)
     loads[-1].start()
-    for load in loads[1 + 4 * rhs : -1]:
+    for load in loads[1 + 2 * rhs : -1]:
         load.wait()
-    fi_copy = send(fi, fi_low, at(0, 0, 1))
-    si_copy = send(si, si_low, at(0, 1, 0))
-    st_copy = send(st, st_high, at(-1, 0, 0))
-    ft_copy = send(ft, ft_high, at(-1, 0, 0))
+    send(fi, fi_low, at(0, 0, 1), FI_G)
+    send(si, si_low, at(0, 1, 0), SI_G)
+    send(st, st_high, at(-1, 0, 0), ST_G)
+    send(ft, ft_high, at(-1, 0, 0), FT_G)
 
     phase("p07_factor")
     shape = (cells, 384)
@@ -284,7 +292,7 @@
     groups2 = (plane + 3) // 4
 
     phase("p09_w1")
-    fi_copy.wait_recv()
+    arrived(FI_G, fi_low)
     w1[...] = jnp.zeros(w1.shape, F32)
     mine = fi[:, 0, :]
     lower = jnp.where(c > 0, fi_low[:, 0, :], 0.0)
@@ -312,19 +320,19 @@
         return (i - d >= 0) & (i - d < n) if d else True
 
     total = [flat[j] for j in range(4)]
-    for (i, (dx, dy, dz)), copy in reversed(list(zip(halo, halo_copies))):
-        copy.wait_recv()
+    arrived(HALO_G, got_halo)
+    for i, (dx, dy, dz) in halo:
         turn = (-(side * 8) * dx - side * dy) % 128
         keep = along(at_x, dx) & along(at_y, dy)
         there = exists(a, dx, ngx) & exists(b, dy, ngy) & exists(c, dz, ngz)
         keep = keep & there
         if dz == 0:
             for j in range(4):
-                v = got_flat[i, j]
+                v = got_halo[4 * i + j]
                 v = pltpu.roll(v, turn, 1) if turn else v
                 total[j] += jnp.where(keep, v, 0.0)
         else:
-            v = got_thin[i - len(FLAT)]
+            v = got_halo[thin + i - len(FLAT)]
             v = pltpu.roll(v, turn, 1) if turn else v
             keep = keep & (at_z == (1 if dz == 1 else 0))
             j = 0 if dz == 1 else 3
@@ -336,10 +344,8 @@
     for g in range(groups1):
         send1[g] = partial[:, 128 * g : 128 * g + 128]
     steps = sorted(range(1, ngz), key=lambda k: -min(k, ngz - k))
-    copies = []
     for k in steps:
-        there = at(0, 0, k)
-        copies.append(send(send1.at[quarter(k)], got1.at[k], there))
+        send(send1.at[quarter(k)], got1.at[k], at(0, 0, k), FIRST_G)
     own1 = send1[quarter(0)]
     word = pl.semaphore_wait
     word(word1, 2)
@@ -350,7 +356,7 @@
     w1_pair = (w1_h[...], w1_l[...])
 
     phase("p15_w2")
-    si_copy.wait_recv()
+    arrived(SI_G, si_low)
     w2[...] = jnp.zeros(w2.shape, F32)
     mine = si[:, 0, :]
     lower = jnp.where(b > 0, si_low[:, 0, :], 0.0)
@@ -370,8 +376,8 @@
     partial = times(s12[:, 0:64], (hi, lo))
 
     phase("p16_wait_first")
-    for k, copy in reversed(list(zip(steps, copies))):
-        copy.wait_recv()
+    arrived(FIRST_G, got1.at[1:ngz])
+    for k in steps:
         own1 += got1[k]
     phase("p17_second_product")
     own1 = jnp.where((lane >= place1) & (lane < place1 + n1), own1, 0.0)
@@ -380,7 +386,6 @@
         send2[g] = partial[:, 128 * g : 128 * g + 128]
     offsets = [(dy, dz) for dy in range(ngy) for dz in range(ngz) if dy or dz]
     offsets = sorted(offsets, key=lambda d: far_first((0,) + d))
-    copies, copies_up = [], []
 
     def group_of(dy, dz):
         if ngz % 4:
@@ -389,11 +394,11 @@
 
     for dy, dz in offsets:
         there = at(-1, dy, dz)
-        copies_up.append(send(send2.at[group_of(dy, dz)], got2.at[1, dy * ngz + dz], there))
+        send(send2.at[group_of(dy, dz)], got2.at[plane + dy * ngz + dz], there, SECOND_G)
     for dy, dz in offsets:
         there = at(0, dy, dz)
-        copies.append(send(send2.at[group_of(dy, dz)], got2.at[0, dy * ngz + dz], there))
-    copies_up.append(send(send2.at[me // 4], got2.at[1, 0], at(-1, 0, 0)))
+        send(send2.at[group_of(dy, dz)], got2.at[dy * ngz + dz], there, SECOND_G)
+    send(send2.at[me // 4], got2.at[plane], at(-1, 0, 0), SECOND_G)
     word(word2, 2)
     tell(word3)
     own2 = send2[me // 4]
@@ -401,13 +406,13 @@
     fs_top = (fs_hi[:, 128:256], fs_lo[:, 128:256])
     s3 = s3 + times(own1, fs_top)
     up_send[...] = s3
-    up_copy = send(up_send, up_got, at(-1, 0, 0))
+    send(up_send, up_got, at(-1, 0, 0), UP_G)
 
     phase("p18_wait_second")
     stu[...] = jnp.zeros(stu.shape, F32)
     ftu[...] = jnp.zeros(ftu.shape, F32)
-    st_copy.wait_recv()
-    ft_copy.wait_recv()
+    arrived(ST_G, st_high)
+    arrived(FT_G, ft_high)
     stu[0:n2, 0:n3] = -st_high[:, n3 : 2 * n3]
     ftu[0:n1, 0:n3] = -ft_high[:, n3 : 2 * n3]
     for ref, put, row in ((stu, put2, 128), (ftu, put1, 384)):
@@ -420,22 +425,18 @@
             got[row : row + 128, :] = jnp.where(column < n3, rows.astype(F32), 0.0).astype(BF16)
     st_hi[128:256, :] = back_hi[128:256, :]
     st_lo[128:256, :] = back_lo[128:256, :]
-    chips = ngz // 2
-    other = (a, b, c + 1 - 2 * lax.rem(c, 2))
-    beside = [send(rall.at[c], rall.at[c], other)]
+    send(rall.at[c], rall.at[c], other, ROWS_G)
     if chips > 1:
         after, before = at(0, 0, 2), at(0, 0, -2)
-        beside.append(send(rall.at[c], rall.at[c], after))
-        beside.append(send(rall.at[c], rall.at[c], before))
-    up_copy.wait_recv()
-    copies_up[-1].wait_recv()
-    above = got2[1, 0]
+        send(rall.at[c], rall.at[c], after, ROWS_G)
+        send(rall.at[c], rall.at[c], before, ROWS_G)
+    arrived(UP_G, up_got)
     target = s3 + jnp.where(a < ngx - 1, pltpu.roll(up_got[...], 128 - n3, 1), 0.0)
-    for (dy, dz), copy, copy_up in reversed(list(zip(offsets, copies, copies_up))):
-        copy.wait_recv()
-        own2 += got2[0, dy * ngz + dz]
-        copy_up.wait_recv()
-        above += got2[1, dy * ngz + dz]
+    arrived(SECOND_G, got2.at[1 : 2 * plane])
+    above = got2[plane]
+    for dy, dz in offsets:
+        own2 += got2[dy * ngz + dz]
+        above += got2[plane + dy * ngz + dz]
     phase("p21_target")
     mine = (lane >= place2) & (lane < place2 + n2)
     own2 = jnp.where(mine, own2, 0.0)
@@ -445,62 +446,93 @@
     spread = [jnp.broadcast_to(columns[0:n3, r : r + 1], (n3, 128)) for r in range(rhs)]
 
     phase("p22_top_product")
-    width = ntop // ngz
+    width = 2 * (ntop // ngz)
     step = 128 if width % 128 == 0 else width
+    chip_steps = sorted(range(chips), key=lambda j: -min(j, chips - j))
+    rows = sorted(range(ngy), key=lambda i: -min(i, ngy - i))
+
+    def term_to(i, j):
+        there = step_along("y", b, i, ngy)
+        spot = 2 * (i * chips + j) + core
+        send(part.at[there, chip_at[j]], got5.at[spot], (a, there, 2 * chip_at[j] + 1), TERM_G)
+
     loads[-1].wait()
-    copies, slots = [], []
-    for j in steps + [0]:
-        group = at(0, 0, j)[2]
+    for j in chip_steps:
         for p in range(0, width, step):
-            start = group * width + p
+            start = chip_at[j] * width + p
             if step == 128:
                 start = pl.multiple_of(start, 128)
             block = ti[:, pl.ds(start, step)]
             for r in range(rhs):
                 scale = spread[r] if step == 128 else jnp.broadcast_to(spread[r][:, 0:1], (n3, step))
-                part[r, group, :, p : p + step] = jnp.sum(scale * block, axis=0, keepdims=True)
-        for i in sorted(range(ngy), key=lambda i: -min(i, ngy - i)):
+                part[r, chip_at[j], :, p : p + step] = jnp.sum(scale * block, axis=0, keepdims=True)
+        for i in rows:
             if i or j:
-                there = at(0, i, j)
-                slots.append(i * ngz + j)
-                copies.append(send(part.at[there[1], there[2]], got5.at[i * ngz + j], there))
+                term_to(i, j)
+
+    @pl.when(jnp.logical_not(keeper))
+    def _():
+        term_to(0, 0)
+
     phase("p23_wait_top1")
-    term = part[b, c]
-    near = sorted(zip(slots, copies), key=lambda e: far_first((0, e[0] // ngz, e[0] % ngz)), reverse=True)
-    for slot, copy in near:
-        copy.wait_recv()
-        term += got5[slot]
-    word(word3, 2)
+    along_x = sorted(range(1, ngx), key=lambda k: -min(k, ngx - k))
+
+    @pl.when(keeper)
+    def _():
+        term = part[b, chip]
+        arrived(TERM_G, got5.at[1:plane])
+        for k in range(plane):
+            if k != 1:
+                term += got5[k]
+        s6[...] = term
+        pl.semaphore_signal(go, inc=1, device_id=other, device_id_type=MESH)
+        pl.semaphore_wait(word3, 2)
+        for k in along_x:
+            send(s6, got6.at[k], at(k, 0, 0), LINE_G)
+
+    @pl.when(jnp.logical_not(keeper))
+    def _():
+        pl.semaphore_wait(word3, 2)
+        pl.semaphore_wait(go, 1)
+
     phase("p24_top2")
-    s6[...] = term
-    along_x = sorted(range(1, ngx), key=lambda k: -min(k, ngx - k))
-    copies = [send(s6, got6.at[k], at(k, 0, 0)) for k in along_x]
-    arrive(beside)
+    arrived(ROWS_G, rall.at[0 : 3 if chips > 1 else 1])
     if chips > 1:
-        across = [
-            send(rall.at[before[2], 0:16], rall.at[before[2], 0:16], after),
-            send(rall.at[after[2], 16:32], rall.at[after[2], 16:32], before),
-        ]
-        beside = [send(rall.at[d[2]], rall.at[d[2]], other) for d in (after, before)]
-    for k, copy in reversed(list(zip(along_x, copies))):
-        copy.wait_recv()
-        term += got6[k]
+        send(rall.at[before[2], 0:16], rall.at[before[2], 0:16], after, ACROSS_G)
+        send(rall.at[after[2], 16:32], rall.at[after[2], 16:32], before, ACROSS_G)
+        for d in (after, before):
+            send(rall.at[d[2]], rall.at[d[2]], other, CORE_G)
+
+    @pl.when(keeper)
+    def _():
+        term = s6[...]
+        arrived(LINE_G, got6.at[1:ngx])
+        for k in along_x:
+            term += got6[k]
+        yall[b, chip] = term
+        for dy, dz in offsets:
+            send(yall.at[b, chip], yall.at[b, chip], at(0, dy, dz), SPREAD_G, SPREAD_G + (1 + dz) // 2 % chips)
+
     phase("p25_top3")
-    yall[b, c] = term
-    copies = [send(yall.at[b, c], yall.at[b, c], at(0, dy, dz)) for dy, dz in offsets]
     if chips > 1:
-        far = lax.rem(c + 4, ngz)
-        arrive(across)
-        beside.append(send(rall.at[far], rall.at[far], other))
+        far = at(0, 0, 4)[2]
+        arrived(ACROSS_G, rall.at[0])
+        send(rall.at[far], rall.at[far], other, CORE_G)
+
+    @pl.when(keeper)
+    def _():
+        arrived(SPREAD_G, got5.at[1:ngy])
+
+    @pl.when(jnp.logical_not(keeper))
+    def _():
+        arrived(SPREAD_G, got5.at[0:ngy])
 
     phase("p26_top_back")
-    arrivals = dict(zip(offsets, copies))
     total = [jnp.zeros((n3, step), F32) for _ in range(rhs)]
-    for dz in [0] + list(reversed(steps)):
-        group = step_along("z", c, -dz, ngz)
-        for dy in sorted(range(ngy), key=lambda i: min(i, ngy - i)):
-            if dy or dz:
-                arrivals[dy, dz].wait_recv()
+    for j in reversed(chip_steps):
+        group = chip_at[(-j) % chips]
+        if j:
+            arrived(SPREAD_G + j, got5.at[0:ngy])
         for p in range(0, width, step):
             start = group * width + p
             if step == 128:
@@ -508,6 +540,7 @@
             block = ti[:, pl.ds(start, step)]
             for r in range(rhs):
                 total[r] += block * yall[r, group, :, p : p + step]
+    phase("p27_down")
     ones = jnp.ones((8, step), BF16)
     back = jnp.zeros((rhs, n3), F32)
     which = iota((rhs, n3), 0)
@@ -515,23 +548,27 @@
         hi, lo = split(total[r])
         both_sums = dot(ones, hi, BACK) + dot(ones, lo, BACK)
         back += jnp.where(which == r, both_sums[0:rhs], 0.0)
-    phase("p27_down")
     down_send[...] = jnp.zeros((rhs, 128), F32)
     down_send[:, 0:n3] = back
     right_sides = times(down_send[...], (back_hi[...], back_lo[...]), BACK)
-    gap2[0, me] = own2 + right_sides[:, 0:128]
+    gap2[me] = own2 + right_sides[:, 0:128]
     low2[...] = right_sides[:, 128:256]
-    gap1[0, c] = own1 + right_sides[:, 256:384]
+    gap1[c] = own1 + right_sides[:, 256:384]
     low1[...] = right_sides[:, 384:512]
-    copies = [send(low2, gap2.at[1, me], at(1, dy, dz)) for dy, dz in offsets]
-    copies += [send(gap2.at[0, me], gap2.at[0, me], at(0, dy, dz)) for dy, dz in offsets]
-    copies.append(send(low2, gap2.at[1, me], at(1, 0, 0)))
-    line = [send(low1, gap1.at[1, c], at(1, 0, k)) for k in steps + [0]]
-    line += [send(gap1.at[0, c], gap1.at[0, c], at(0, 0, k)) for k in steps]
-    down_copy = send(down_send, down_got, at(1, 0, 0))
+    for dy, dz in offsets:
+        send(low2, gap2.at[plane + me], at(1, dy, dz), GAP_G)
+    for dy, dz in offsets:
+        send(gap2.at[me], gap2.at[me], at(0, dy, dz), GAP_G)
+    send(low2, gap2.at[plane + me], at(1, 0, 0), GAP_G)
+    for k in steps + [0]:
+        send(low1, gap1.at[ngz + c], at(1, 0, k), FIRST_GAP_G)
+    for k in steps:
+        send(gap1.at[c], gap1.at[c], at(0, 0, k), FIRST_GAP_G)
+    send(down_send, down_got, at(1, 0, 0), DOWN_G)
 
     phase("p29_rows")
-    arrive(beside[1:] if chips == 1 else beside)
+    if chips > 1:
+        arrived(CORE_G, rall.at[0:3])
     hi, lo = split(rall[...].reshape(32 * ngz, 128 * groups2))
     rows = dot(w1_h[64:128, 0 : 32 * ngz], hi) + dot(w1_l[64:128, 0 : 32 * ngz], hi) + dot(w1_h[64:128, 0 : 32 * ngz], lo)
     hi, lo = split(rows)
@@ -541,21 +578,39 @@
     def gathered(ref, members):
         blocks = []
         for g in range((members + 3) // 4):
-            own_part, lower_part = ref[0, 4 * g], ref[1, 4 * g]
+            own_part, lower_part = ref[4 * g], ref[members + 4 * g]
             for i in range(4 * g + 1, min(4 * g + 4, members)):
-                own_part += ref[0, i]
-                lower_part += ref[1, i]
+                own_part += ref[i]
+                lower_part += ref[members + i]
             blocks.append(own_part + jnp.where(a > 0, lower_part, 0.0))
         return jnp.concatenate(blocks, axis=1)
 
-    drain()
+    for group, ref in ((HALO_G, got_halo), (FI_G, fi), (SI_G, si), (ST_G, st), (FT_G, ft), (FIRST_G, got1.at[1:ngz])):
+        sent(group, ref)
+    sent(SECOND_G, got2.at[1 : 2 * plane])
+    sent(UP_G, up_send)
+    sent(ROWS_G, rall.at[0 : 3 if chips > 1 else 1])
+    if chips > 1:
+        sent(ACROSS_G, rall.at[0])
+        sent(CORE_G, rall.at[0:3])
+
+    @pl.when(keeper)
+    def _():
+        sent(TERM_G, got5.at[1 : plane // 2])
+        sent(LINE_G, got6.at[1:ngx])
+        sent(SPREAD_G, got5.at[1:plane])
+
+    @pl.when(jnp.logical_not(keeper))
+    def _():
+        sent(TERM_G, got5.at[0 : plane // 2])
+
     phase("p30_wait_gap")
-    arrive([down_copy])
+    arrived(DOWN_G, down_got)
     z3 = down_send[...] + jnp.where(a > 0, pltpu.roll(down_got[...], n3, 1), 0.0)
     corr_part = times(jnp.concatenate([s_leaf, z3], axis=1), tuple(jnp.concatenate([e[:, 0:128], e[:, 256:384]], axis=1) for e in e_pair), BACK)
-    arrive(line)
+    arrived(FIRST_GAP_G, gap1.at[1 : 2 * ngz])
     z12 = times(gathered(gap1, ngz), w1_pair, BACK)
-    arrive(copies)
+    arrived(GAP_G, gap2.at[1 : 2 * plane])
     phase("p31_z_leaf")
     z12 = z12 + times(gathered(gap2, plane), (w2_h[...], w2_l[...]), BACK)
 
@@ -563,18 +618,18 @@
     for j in range(4):
         corr[j] = result[:, 128 * j : 128 * j + 128]
     phase("p32_rim")
-    copies = []
     rim = sorted(enumerate(RIM), key=lambda e: far_first(e[1]))
+    spot = {i: sum(1 if d[2] else 4 for d in RIM[:i]) for i in range(len(RIM))}
     for i, (dx, dy, dz) in rim:
         there = at(-dx, -dy, -dz)
         if dz == 0:
-            copies.append(send(corr, got_corr.at[i], there))
+            send(corr, got_corr.at[spot[i] : spot[i] + 4], there, RIM_G)
         else:
-            copies.append(send(corr.at[0], got_corr.at[i, 0], there))
+            send(corr.at[0], got_corr.at[spot[i]], there, RIM_G)
 
     total = [corr[j] for j in range(4)]
-    for (i, (dx, dy, dz)), copy in reversed(list(zip(rim, copies))):
-        copy.wait_recv()
+    arrived(RIM_G, got_corr)
+    for i, (dx, dy, dz) in rim:
         turn = side * 8 * dx + side * dy
         keep = (at_x == side + 1) if dx else (at_x <= side)
         keep = keep & ((at_y == side + 1) if dy else (at_y <= side))
@@ -585,7 +640,7 @@
         if dz:
             keep = keep & (c < ngz - 1) & (at_z == 1)
         for j in range(4) if dz == 0 else (0,):
-            v = got_corr[i, j]
+            v = got_corr[spot[i] + j]
             v = pltpu.roll(v, turn, 1) if turn else v
             total[j if dz == 0 else 3] += jnp.where(keep, v, 0.0)
     rows = []
@@ -593,7 +648,10 @@
         rows += [total[j][:, 0:64], total[j][:, 64:128]]
     out_h[...] = jnp.concatenate(rows, axis=0)
     phase("p34_finish")
-    drain()
+    sent(GAP_G, gap2.at[1 : 2 * plane])
+    sent(FIRST_GAP_G, gap1.at[1 : 2 * ngz])
+    sent(DOWN_G, down_send)
+    sent(RIM_G, got_corr)
     stack.close()
 
 
@@ -661,9 +719,7 @@
     cells = side**3
     inputs = [rs, it, cf, od, li, lf, ls, lt, fi, fs, ft, si, st, ti]
     v = pltpu.VMEM
-    width = ntop // ngz
-    step = 128 if width % 128 == 0 else width
-    copies = len(HALO) + 4 + 8 + 3 * ngz - 2 + 6 * plane - 4 + 2 + (ngx - 1) + len(RIM)
+    width = 2 * (ntop // ngz)
     narrow = [x.reshape(x.shape[0], -1) if any(x is y for y in (li, lf, ls, fs, ft, st)) else x for x in inputs]
     scratch = [v(x.shape, x.dtype) for x in narrow]
     scratch += [
@@ -676,19 +732,19 @@
         v((64, 128 * groups2), F32), v((128, 128 * groups2), BF16), v((128, 128 * groups2), BF16),
         v(fi.shape, F32), v(si.shape, F32), v((ngz, 32, 128 * groups2), F32),
         v((128, 128 * groups2), BF16), v((128, 128 * groups2), BF16),
-        v((4, rhs, 128), F32), v((len(FLAT), 4, rhs, 128), F32), v((len(HALO) - len(FLAT), rhs, 128), F32),
+        v((4, rhs, 128), F32), v((len(HALO) + 3 * len(FLAT), rhs, 128), F32),
         v((groups1, rhs, 128), F32), v((ngz, rhs, 128), F32),
-        v((groups2, rhs, 128), F32), v((2, plane, rhs, 128), F32),
+        v((groups2, rhs, 128), F32), v((2 * plane, rhs, 128), F32),
         v((rhs, 128), F32), v((rhs, 128), F32),
-        v((rhs, ngz, 1, width), F32), v((plane, 1, width), F32),
+        v((rhs, ngz // 2, 1, width), F32), v((plane, 1, width), F32),
         v((1, width), F32), v((ngx, 1, width), F32),
-        v((rhs, ngz, 1, width), F32),
+        v((rhs, ngz // 2, 1, width), F32),
         v((rhs, 128), F32), v((rhs, 128), F32),
-        v((2, plane, rhs, 128), F32), v((2, ngz, rhs, 128), F32), v((rhs, 128), F32), v((rhs, 128), F32),
-        v((4, rhs, 128), F32), v((len(RIM), 4, rhs, 128), F32),
-        pltpu.SemaphoreType.DMA((len(inputs) + 4 * rhs - 2,)),
-        *[pltpu.SemaphoreType.REGULAR] * 3,
-        pltpu.SemaphoreType.DMA((copies,)), pltpu.SemaphoreType.DMA((copies,)),
+        v((2 * plane, rhs, 128), F32), v((2 * ngz, rhs, 128), F32), v((rhs, 128), F32), v((rhs, 128), F32),
+        v((4, rhs, 128), F32), v((sum(1 if d[2] else 4 for d in RIM), rhs, 128), F32),
+        pltpu.SemaphoreType.DMA((len(inputs) + rhs - 2,)),
+        *[pltpu.SemaphoreType.REGULAR] * 4,
+        pltpu.SemaphoreType.DMA((SPREAD_G + 1,)), pltpu.SemaphoreType.DMA((SPREAD_G + ngz // 2,)),
     ]
     coarse = pl.pallas_call(
         functools.partial(kernel, cfg),

time: 57.5 us -> 51.4 us (0.89)
  Pallas kernels: 57.3 us -> 51.2 us
    pallas_call x1, Pallas kernels: 55.2 us -> 49.1 us  [per_device(): pl.pallas_call(functools.partial(kernel, cfg), out_shape=jax.ShapeDtypeSt...]
where the time goes in v5:
time: 51.4 us; the launch traced here: 51.2 us
  Pallas kernels  51.2 us (100%)
    pallas_call x1, Pallas kernels, per_device(): pl.pallas_call(functools.partial(kernel, cfg), out_shape=jax.ShapeDtypeSt...  49.1 us
    pallas_call x1, Pallas kernels, per_device(): pl.pallas_call(functools.partial(prolong, cfg), out_shape=jax.ShapeDtypeS...  2.17 us

profile of v5, /device:TPU:1, one launch (start us, length us, event | category | flops | bytes accessed | tf_op | source)
XLA Modules:
  0.0 51.2 jit_solution(16062313531611861808)
XLA Ops:
  0.0 49.1 %coarse_correction.1.ct_h = f32[32,64]{1,0:T(8,128)} custom-call(f32[4,24,24,24]{3,2,1,0:T(8,128)} %refs_0_.1, f32[4,24,24,24]{3,2,1,0:T(8,128)} %refs_1_.1, f32[24,24,24]{2,1,0:T(8,128)} %refs_2_.1, s32[1,216]{1,0:T(1,128)} %bitcast.25, f32[125,1,125]{2,1,0:T(1,128)} %bitcast.17, f32[50,1,125]{2,1,0:T(1,128)} %bitcast.20, f32[60,1,125]{2,1,0:T(1,128)} %bitcast.19, ...), custom_call_target="tpu_custom_call" | custom-call | tf_op jit(solution)/shard_map/coarse_correction/pallas_call | solution.py:749
  49.1 2.2 %prolong.1 = f32[4,24,24,24]{3,2,1,0:T(8,128)} custom-call(f32[32,64]{1,0:T(8,128)} %coarse_correction.1.ct_h), custom_call_target="tpu_custom_call" | custom-call | tf_op jit(solution)/shard_map/prolong/pallas_call | solution.py:760

commit v6 on v5

--- a/solution.py
+++ b/solution.py
@@ -23,6 +23,7 @@
     HALO_G, FI_G, SI_G, ST_G, FT_G, FIRST_G, SECOND_G, UP_G, ROWS_G, ACROSS_G, CORE_G,
     TERM_G, LINE_G, GAP_G, FIRST_GAP_G, DOWN_G, RIM_G, SPREAD_G,
 ) = range(18)
+SENT = {FI_G: 1, SI_G: 2, ST_G: 3, FT_G: 4, ROWS_G: 5, ACROSS_G: 5, CORE_G: 5, TERM_G: 6, LINE_G: 7, SPREAD_G: 8}
 
 
 def split(value):
@@ -86,7 +87,7 @@
         stu, ftu, back_hi, back_lo, st_high, ft_high,
         w1, w1_h, w1_l, w2, w2_h, w2_l, fi_low, si_low, rall, r_hi, r_lo,
         flat, got_halo, send1, got1, send2, got2, up_send, up_got,
-        part, got5, s6, got6, yall, down_send, down_got, gap2, gap1, low2, low1, corr, got_corr,
+        part, got5, s6, got6, yall, down_send, down_got, gap2, gap1, low2, low1, blocks, corr, got_corr,
         local_sem, word1, word2, word3, go, send_sem, recv_sem,
     ) = refs[15:]
 
@@ -133,7 +134,7 @@
         return pltpu.make_async_remote_copy(
             src_ref=src,
             dst_ref=dst,
-            send_sem=send_sem.at[group],
+            send_sem=send_sem.at[SENT.get(group, 0)],
             recv_sem=recv_sem.at[group if into is None else into],
             device_id=device,
             device_id_type=MESH,
@@ -149,16 +150,13 @@
         copy_of(ref, ref, other, group).wait_send()
 
     phase("p00_loads")
-    first = [(cf_h, cf)]
-    for r in range(rhs):
-        first += [(it_h.at[r], it.at[r]), (rs_h.at[r], rs.at[r])]
+    first = [(it_h, it), (cf_h, cf)] + [(rs_h.at[r], rs.at[r]) for r in range(rhs)]
     pairs = [
         (od_h, od), (li_h, li), (lf_h, lf), (ls_h, ls), (lt_h, lt),
         (fi_h, fi), (si_h, si), (fs_h, fs), (ft_h, ft), (st_h, st),
     ]
     pairs = first + [(s.at[:, 0, :] if len(s.shape) > len(d.shape) else s, d) for s, d in pairs] + [(ti_h, ti)]
-    spots = [0] + [1 + i // 2 for i in range(2 * rhs)] + list(range(1 + rhs, len(pairs) - rhs))
-    loads = [pltpu.make_async_copy(s, d, local_sem.at[i]) for i, (s, d) in zip(spots, pairs)]
+    loads = [pltpu.make_async_copy(s, d, local_sem.at[i]) for i, (s, d) in enumerate(pairs)]
     for load in loads[:-1]:
         load.start()
 
@@ -202,19 +200,19 @@
     wvz = wvz.astype(BF16)
 
     phase("p03_wait_residual")
+    own = a21[64:128, :]
+    both = a21[...]
     loads[0].wait()
+    for r in range(rhs):
+        pack_it[:, fine * r : fine * r + fine] = it[r].reshape(fine * fine, fine)
+    i_h, i_l = split(pack_it[...])
+    from_it = dot(both, i_h) + dot(both, i_l)
+    loads[1].wait()
     diagonal = 6.0 + cf[...]
     for r in range(rhs):
-        pltpu.make_async_copy(it_h.at[0:2], it.at[0:2], local_sem.at[1 + r]).wait()
-        now = it[r]
-        at_r = slice(fine * r, fine * r + fine)
-        pack_it[:, at_r] = now.reshape(fine * fine, fine)
-        pack_q[:, at_r] = (rs[r] - diagonal * now).reshape(fine * fine, fine)
-    i_h, i_l = split(pack_it[...])
+        loads[2 + r].wait()
+        pack_q[:, fine * r : fine * r + fine] = (rs[r] - diagonal * it[r]).reshape(fine * fine, fine)
     q_h, q_l = split(pack_q[...])
-    own = a21[64:128, :]
-    both = a21[...]
-    from_it = dot(both, i_h) + dot(both, i_l)
     g1 = from_it[0:64] + dot(own, q_h) + dot(own, q_l)
     g_h, g_l = split(jnp.concatenate([g1, from_it[64:128]], axis=1))
     ct = dot(wvz, g_h, BACK) + dot(wvz, g_l, BACK)
@@ -241,7 +239,7 @@
 
     tell(word1)
     loads[-1].start()
-    for load in loads[1 + 2 * rhs : -1]:
+    for load in loads[2 + rhs : -1]:
         load.wait()
     send(fi, fi_low, at(0, 0, 1), FI_G)
     send(si, si_low, at(0, 1, 0), SI_G)
@@ -392,13 +390,10 @@
             return lax.div(step_along("y", b, dy, ngy) * ngz + step_along("z", c, dz, ngz), 4)
         return step_along("y", b, dy, ngy) * (ngz // 4) + quarter(dz)
 
-    for dy, dz in offsets:
-        there = at(-1, dy, dz)
-        send(send2.at[group_of(dy, dz)], got2.at[plane + dy * ngz + dz], there, SECOND_G)
-    for dy, dz in offsets:
-        there = at(0, dy, dz)
-        send(send2.at[group_of(dy, dz)], got2.at[dy * ngz + dz], there, SECOND_G)
-    send(send2.at[me // 4], got2.at[plane], at(-1, 0, 0), SECOND_G)
+    both_planes = [(0,) + d for d in offsets] + [(1,) + d for d in offsets] + [(1, 0, 0)]
+    both_planes = sorted(both_planes, key=far_first)
+    for dx, dy, dz in both_planes:
+        send(send2.at[group_of(dy, dz)], got2.at[plane * dx + dy * ngz + dz], at(-dx, dy, dz), SECOND_G)
     word(word2, 2)
     tell(word3)
     own2 = send2[me // 4]
@@ -555,11 +550,9 @@
     low2[...] = right_sides[:, 128:256]
     gap1[c] = own1 + right_sides[:, 256:384]
     low1[...] = right_sides[:, 384:512]
-    for dy, dz in offsets:
-        send(low2, gap2.at[plane + me], at(1, dy, dz), GAP_G)
-    for dy, dz in offsets:
-        send(gap2.at[me], gap2.at[me], at(0, dy, dz), GAP_G)
-    send(low2, gap2.at[plane + me], at(1, 0, 0), GAP_G)
+    for dx, dy, dz in both_planes:
+        src = low2 if dx else gap2.at[me]
+        send(src, gap2.at[plane * dx + me], at(dx, dy, dz), GAP_G)
     for k in steps + [0]:
         send(low1, gap1.at[ngz + c], at(1, 0, k), FIRST_GAP_G)
     for k in steps:
@@ -585,14 +578,9 @@
             blocks.append(own_part + jnp.where(a > 0, lower_part, 0.0))
         return jnp.concatenate(blocks, axis=1)
 
-    for group, ref in ((HALO_G, got_halo), (FI_G, fi), (SI_G, si), (ST_G, st), (FT_G, ft), (FIRST_G, got1.at[1:ngz])):
+    for group, ref in ((FI_G, fi), (SI_G, si), (ST_G, st), (FT_G, ft)):
         sent(group, ref)
-    sent(SECOND_G, got2.at[1 : 2 * plane])
-    sent(UP_G, up_send)
-    sent(ROWS_G, rall.at[0 : 3 if chips > 1 else 1])
-    if chips > 1:
-        sent(ACROSS_G, rall.at[0])
-        sent(CORE_G, rall.at[0:3])
+    sent(ROWS_G, rall.at[0 : 7 if chips > 1 else 1])
 
     @pl.when(keeper)
     def _():
@@ -648,10 +636,7 @@
         rows += [total[j][:, 0:64], total[j][:, 64:128]]
     out_h[...] = jnp.concatenate(rows, axis=0)
     phase("p34_finish")
-    sent(GAP_G, gap2.at[1 : 2 * plane])
-    sent(FIRST_GAP_G, gap1.at[1 : 2 * ngz])
-    sent(DOWN_G, down_send)
-    sent(RIM_G, got_corr)
+    sent(HALO_G, blocks)
     stack.close()
 
 
@@ -722,6 +707,7 @@
     width = 2 * (ntop // ngz)
     narrow = [x.reshape(x.shape[0], -1) if any(x is y for y in (li, lf, ls, fs, ft, st)) else x for x in inputs]
     scratch = [v(x.shape, x.dtype) for x in narrow]
+    small = len(HALO) + 3 * len(FLAT) + len(RIM) + 9 + 4 * plane + 3 * ngz - 2
     scratch += [
         v((fine * fine, rhs * fine), F32), v((fine * fine, rhs * fine), F32), v((128, fine * fine), BF16),
         v((cells, 384), F32), v((512, 384), BF16), v((512, 384), BF16),
@@ -740,11 +726,11 @@
         v((1, width), F32), v((ngx, 1, width), F32),
         v((rhs, ngz // 2, 1, width), F32),
         v((rhs, 128), F32), v((rhs, 128), F32),
-        v((2 * plane, rhs, 128), F32), v((2 * ngz, rhs, 128), F32), v((rhs, 128), F32), v((rhs, 128), F32),
+        v((2 * plane, rhs, 128), F32), v((2 * ngz, rhs, 128), F32), v((rhs, 128), F32), v((rhs, 128), F32), v((small, rhs, 128), F32),
         v((4, rhs, 128), F32), v((sum(1 if d[2] else 4 for d in RIM), rhs, 128), F32),
-        pltpu.SemaphoreType.DMA((len(inputs) + rhs - 2,)),
+        pltpu.SemaphoreType.DMA((len(inputs) + rhs - 1,)),
         *[pltpu.SemaphoreType.REGULAR] * 4,
-        pltpu.SemaphoreType.DMA((SPREAD_G + 1,)), pltpu.SemaphoreType.DMA((SPREAD_G + ngz // 2,)),
+        pltpu.SemaphoreType.DMA((9,)), pltpu.SemaphoreType.DMA((SPREAD_G + ngz // 2,)),
     ]
     coarse = pl.pallas_call(
         functools.partial(kernel, cfg),

time: 51.4 us -> 51.3 us (level)
  no operation moved by 1% of the time
where the time goes in v6:
time: 51.3 us; the launch traced here: 51.2 us
  Pallas kernels  51.1 us (100%)
    pallas_call x1, Pallas kernels, per_device(): pl.pallas_call(functools.partial(kernel, cfg), out_shape=jax.ShapeDtypeSt...  49 us
    pallas_call x1, Pallas kernels, per_device(): pl.pallas_call(functools.partial(prolong, cfg), out_shape=jax.ShapeDtypeS...  2.17 us

profile of v6, /device:TPU:1, one launch (start us, length us, event | category | flops | bytes accessed | tf_op | source)
XLA Modules:
  0.0 51.2 jit_solution(8959359065088365072)
XLA Ops:
  0.0 49.0 %coarse_correction.1.ct_h = f32[32,64]{1,0:T(8,128)} custom-call(f32[4,24,24,24]{3,2,1,0:T(8,128)} %refs_0_.1, f32[4,24,24,24]{3,2,1,0:T(8,128)} %refs_1_.1, f32[24,24,24]{2,1,0:T(8,128)} %refs_2_.1, s32[1,216]{1,0:T(1,128)} %bitcast.25, f32[125,1,125]{2,1,0:T(1,128)} %bitcast.17, f32[50,1,125]{2,1,0:T(1,128)} %bitcast.20, f32[60,1,125]{2,1,0:T(1,128)} %bitcast.19, ...), custom_call_target="tpu_custom_call" | custom-call | tf_op jit(solution)/shard_map/coarse_correction/pallas_call | solution.py:735
  49.0 2.2 %prolong.1 = f32[4,24,24,24]{3,2,1,0:T(8,128)} custom-call(f32[32,64]{1,0:T(8,128)} %coarse_correction.1.ct_h), custom_call_target="tpu_custom_call" | custom-call | tf_op jit(solution)/shard_map/prolong/pallas_call | solution.py:746
